TPU v7x, 32 devices: a 4x2x2 block of a 4x4x8 slice. The times are simulated.
32 devices in a mesh: dp: 4 (over y, z), tp: 8 (over x, core).
Axes of the slice: x: 4, y: 2, z: 2, core: 2. Of those that a mesh axis runs over, the one named last changes fastest.
The devices are a block of a 4x4x8 slice.
Arguments:
- x: bfloat16 [16384, 3072], P('dp'), parts along dimension 0
- pos: int32 [16384], P('dp'), parts along dimension 0
- g1: bfloat16 [3072], replicated
- g2: bfloat16 [3072], replicated
- wq: bfloat16 [3072, 3072], P(None, 'tp')
- wk: bfloat16 [3072, 1024], replicated
- wv: bfloat16 [3072, 1024], replicated
- wo: bfloat16 [3072, 3072], P('tp')
- wg: bfloat16 [3072, 8192], P(None, 'tp')
- wu: bfloat16 [3072, 8192], P(None, 'tp')
- wd: bfloat16 [8192, 3072], P('tp')
Outputs:
- output 1: bfloat16 [16384, 3072], P('dp'), parts along dimension 0
- output 2: bfloat16 [16384, 8, 128], P('dp', 'tp'), parts along dimension 0
- output 3: bfloat16 [16384, 8, 128], P('dp', 'tp'), parts along dimension 0
There are 4 independent parts. A program takes and returns all parts, laid end to end along the dimension named above; an argument that names none is the same for every part.
All inputs are finite; a program needn't handle non-finite values.
Results may differ from a plain program's by a relative error of at most 0.0168319.
Values are sent between devices in bfloat16 or wider.
A program may use at most 768 MiB of HBM per device.

v0:
```python
import jax
import jax.numpy as jnp
from jax import lax
from jax.sharding import PartitionSpec as P

HEAD = 128
EPS = 1e-5
ROPE_BASE = 500000.0


def _rms(x, g):
    x32 = x.astype(jnp.float32)
    inv = lax.rsqrt(jnp.mean(x32 * x32, axis=-1, keepdims=True) + EPS)
    return (x32 * inv * g.astype(jnp.float32)).astype(jnp.bfloat16)


def _cs(pos, width):
    half = width // 2
    inv = ROPE_BASE ** (-2.0 * jnp.arange(half, dtype=jnp.float32) / width)
    ang = pos.astype(jnp.float32)[..., None] * inv
    return jnp.cos(ang)[..., None, :], jnp.sin(ang)[..., None, :]


def _rope(t, c, s):
    half = t.shape[-1] // 2
    t1, t2 = t[..., :half], t[..., half:]
    return jnp.concatenate([t1 * c - t2 * s, t2 * c + t1 * s], axis=-1)


def _attend(q, k, v, pos_q, pos_k, block, tail):
    tq, tk = q.shape[0], k.shape[0]
    qb = min(tq, block)
    scale = q.shape[-1] ** -0.5
    outs = []
    for i in range(tq // qb):
        lo, hi = i * qb, (i + 1) * qb
        n = tk - tq + hi if tail else tk
        pp = pos_q[lo:hi]
        sc = jnp.einsum("qgrd,kgd->grqk", q[lo:hi], k[:n], preferred_element_type=jnp.float32) * scale
        sc = jnp.where((pos_k[:n][None, :] <= pp[:, None])[None, None], sc, -jnp.inf)
        e = jnp.exp(sc - jnp.max(sc, axis=-1, keepdims=True))
        pr = (e / jnp.sum(e, axis=-1, keepdims=True)).astype(jnp.bfloat16)
        outs.append(jnp.einsum("grqk,kgd->qgrd", pr, v[:n], preferred_element_type=jnp.float32).astype(jnp.bfloat16))
    return jnp.concatenate(outs, axis=0).reshape(tq, -1)


def solution(mesh):
    tp = mesh.shape["tp"]

    def local(x, pos, g1, g2, wq, wk, wv, wo, wg, wu, wd):
        f32, bf = jnp.float32, jnp.bfloat16
        t, d = x.shape
        hl = wq.shape[1] // HEAD
        g = wk.shape[1] // HEAD
        slots = max(g, tp)
        kvl = slots // tp
        r = lax.axis_index("tp")
        start = r * kvl * g // slots
        wk_l = lax.dynamic_slice_in_dim(wk, start * HEAD, kvl * HEAD, axis=1)
        wv_l = lax.dynamic_slice_in_dim(wv, start * HEAD, kvl * HEAD, axis=1)
        a = _rms(x, g1)
        c, s = _cs(pos, HEAD)
        q = _rope(jnp.dot(a, wq, preferred_element_type=f32).reshape(t, hl, HEAD), c, s).astype(bf)
        k = _rope(jnp.dot(a, wk_l, preferred_element_type=f32).reshape(t, kvl, HEAD), c, s).astype(bf)
        v = jnp.dot(a, wv_l, preferred_element_type=f32).astype(bf).reshape(t, kvl, HEAD)
        o = _attend(q.reshape(t, kvl, hl // kvl, HEAD), k, v, pos, pos, 256, True)
        p = jnp.dot(o, wo, preferred_element_type=f32).astype(bf)
        h = (x.astype(f32) + lax.psum(p, "tp").astype(f32)).astype(bf)
        b = _rms(h, g2)
        gt = jnp.dot(b, wg, preferred_element_type=f32)
        up = jnp.dot(b, wu, preferred_element_type=f32)
        u = (jax.nn.silu(gt) * up).astype(bf)
        rr = jnp.dot(u, wd, preferred_element_type=f32).astype(bf)
        y = (h.astype(f32) + lax.psum(rr, "tp").astype(f32)).astype(bf)
        return y, k, v

    return jax.shard_map(
        local,
        mesh=mesh,
        in_specs=(P("dp", None), P("dp"), P(), P(), P(None, "tp"), P(), P(), P("tp", None),
                  P(None, "tp"), P(None, "tp"), P("tp", None)),
        out_specs=(P("dp", None), P("dp", "tp", None), P("dp", "tp", None)),
        check_vma=False,
    )
```

profile of v0, /device:TPU:81, one launch (start us, length us, event | category | flops | bytes accessed | tf_op | source)
XLA Modules:
  0.0 1006.0 jit_solution(8375742251258627189)
XLA Ops:
  11.1 10.3 %fusion = f32[4096]{0:T(1024)S(1)} fusion(bf16[4096,3072]{1,0:T(8,128)(2,1)} %param.11), kind=kLoop, calls=%fused_computation.6 | loop fusion | flops 37744640 | bytes 25182208 | tf_op jit(solution)/shard_map/reduce_sum | solution.py:13
  21.5 2.7 broadcast_compare_fusion
  24.2 22.5 %fusion.2 = bf16[4096,3072]{1,0:T(8,128)(2,1)} fusion(bf16[4096,3072]{1,0:T(8,128)(2,1)} %param.11, f32[3072]{0:T(1024)S(1)} %convert_element_type.251, f32[4096]{0:T(1024)S(1)} %add_rsqrt_fusion.1), kind=kLoop, calls=%fused_computation.8 | loop fusion | flops 50331648 | bytes 50360320 | tf_op jit(solution)/shard_map/convert_element_type | solution.py:14
  46.8 12.6 %convolution_convert_fusion.2 = bf16[4096,128]{1,0:T(8,128)(2,1)} fusion(bf16[4096,3072]{1,0:T(8,128)(2,1)} %fusion.2, bf16[3072,1024]{1,0:T(8,128)(2,1)} %param.17, s32[]{:T(128)S(6)} %select_n.74), kind=kOutput, calls=%fused_computation.75 | convolution fusion | flops 3221749760 | bytes 27000836 | tf_op jit(solution)/shard_map/dot_general | solution.py:65
  59.4 14.3 %convolution_bitcast_fusion = f32[4096,1,128]{0,2,1:T(8,128)} fusion(bf16[4096,3072]{1,0:T(8,128)(2,1)} %fusion.2, bf16[3072,1024]{1,0:T(8,128)(2,1)} %param.16, s32[]{:T(128)S(6)} %select_n.74), kind=kOutput, calls=%fused_computation.73 | convolution fusion | flops 3221225472 | bytes 28049412 | tf_op jit(solution)/shard_map/dot_general | solution.py:64
  73.7 18.1 %fusion.407 = f32[4096,384]{0,1:T(8,128)} fusion(bf16[4096,3072]{1,0:T(8,128)(2,1)} %fusion.2, bf16[3072,384]{1,0:T(8,128)(2,1)} %param.15), kind=kOutput, calls=%fused_computation.440 | convolution fusion | flops 9663676416 | bytes 33816576 | tf_op jit(solution)/shard_map/dot_general | solution.py:63
  91.8 9.3 multiply_cosine_fusion
  101.1 4.8 fusion.203
  106.0 6.6 fusion.384
  112.6 5.7 copy.146
  118.3 5.8 copy.145
  124.3 6.8 subtract_convert_fusion
  135.5 2.4 fusion.52
  139.4 3.2 fusion.389
  143.0 3.6 fusion.40
  147.0 4.0 fusion.35
  155.3 4.8 fusion.26
  161.4 5.1 fusion.22
  168.0 4.9 fusion.391
  178.0 5.4 fusion.14
  185.1 6.0 fusion.13
  192.7 2.3 fusion.121
  205.7 3.9 fusion.34
  209.6 5.1 fusion.197
  214.7 4.2 fusion.29
  218.9 5.6 fusion.179
  227.6 4.9 fusion.21
  232.5 6.3 fusion.167
  238.8 5.3 fusion.16
  244.1 6.3 fusion.115
  250.5 5.3 fusion.12
  257.8 3.6 fusion.161
  261.4 6.6 fusion.155
  268.0 6.5 fusion.10
  274.6 7.1 fusion.149
  281.7 6.9 fusion.9
  288.6 7.4 fusion.143
  296.0 2.6 fusion.11
  298.7 2.9 fusion.8
  301.5 4.7 fusion.137
  306.2 19.4 %convolution_convert_fusion.1 = bf16[4096,3072]{1,0:T(8,128)(2,1)} fusion(bf16[4096,384]{0,1:T(8,128)(2,1)} %bitcast.630, bf16[384,3072]{1,0:T(8,128)(2,1)S(1)} %copy-done), kind=kOutput, calls=%fused_computation.15 | convolution fusion | flops 9676259328 | bytes 30670848 | tf_op jit(solution)/shard_map/dot_general | solution.py:67
  326.3 258.8 %all-reduce.3.cloned.1.call-done = bf16[4096,3072]{1,0:T(8,128)(2,1)} async-done(((bf16[4096,3072]{1,0:T(8,128)(2,1)}), bf16[4096,3072]{1,0:T(8,128)(2,1)}) %all-reduce.3.cloned.1.call-update) | async-done | bytes 25165840 | tf_op jit(solution)/shard_map/psum | solution.py:68
  585.1 25.4 %fusion.4 = (f32[4096]{0:T(1024)S(1)}, bf16[4096,3072]{1,0:T(8,128)(2,1)}) fusion(bf16[4096,3072]{1,0:T(8,128)(2,1)} %all-reduce.3.cloned.1.call-done, bf16[4096,3072]{1,0:T(8,128)(2,1)} %param.11), kind=kLoop, calls=%fused_computation.10 | loop fusion | flops 88076288 | bytes 75513856 | tf_op jit(solution)/shard_map/reduce_sum | solution.py:13
  610.6 33.4 %fusion.18 = f32[4096,1024]{1,0:T(8,128)} fusion(bf16[3072,1024]{1,0:T(8,128)(2,1)} %param.19, bf16[4096,3072]{1,0:T(8,128)(2,1)} %get-tuple-element.7, f32[3072]{0:T(1024)S(1)} %convert_element_type.323, f32[4096]{0:T(1024)S(1)} %add_rsqrt_fusion), kind=kOutput, calls=%fused_computation.47 | convolution fusion | flops 25820135424 | bytes 48263168 | tf_op jit(solution)/shard_map/dot_general | solution.py:70
  644.0 35.1 %multiply_convert_fusion = bf16[4096,1024]{1,0:T(8,128)(2,1)} fusion(f32[4096,1024]{1,0:T(8,128)} %fusion.18, bf16[3072,1024]{1,0:T(8,128)(2,1)} %param.20, bf16[4096,3072]{1,0:T(8,128)(2,1)} %get-tuple-element.7, f32[3072]{0:T(1024)S(1)} %convert_element_type.323, f32[4096]{0:T(1024)S(1)} %add_rsqrt_fusion), kind=kOutput, calls=%fused_computation.16 | convolution fusion | flops 25845301248 | bytes 56651776 | tf_op jit(solution)/shard_map/dot_general | solution.py:71
  679.1 34.4 %convolution_convert_fusion = bf16[4096,3072]{1,0:T(8,128)(2,1)} fusion(bf16[4096,1024]{1,0:T(8,128)(2,1)} %multiply_convert_fusion, bf16[1024,3072]{1,0:T(8,128)(2,1)} %param.21), kind=kOutput, calls=%fused_computation.14 | convolution fusion | flops 25782386688 | bytes 39845888 | tf_op jit(solution)/shard_map/dot_general | solution.py:73
  716.1 252.9 %all-reduce.5.cloned.1.call-done = bf16[4096,3072]{1,0:T(8,128)(2,1)} async-done(((bf16[4096,3072]{1,0:T(8,128)(2,1)}), bf16[4096,3072]{1,0:T(8,128)(2,1)}) %all-reduce.5.cloned.1.call-update) | async-done | bytes 25165840 | tf_op jit(solution)/shard_map/psum | solution.py:74
  969.0 30.0 %fusion.7 = bf16[4096,3072]{1,0:T(8,128)(2,1)} fusion(bf16[4096,3072]{1,0:T(8,128)(2,1)} %get-tuple-element.7, bf16[4096,3072]{1,0:T(8,128)(2,1)} %all-reduce.5.cloned.1.call-done), kind=kLoop, calls=%fused_computation.13 | loop fusion | flops 50331648 | bytes 75497472 | tf_op jit(solution)/shard_map/convert_element_type | solution.py:74
  (126 shorter events, 45.1 us)
Async XLA Ops:
  7.2 299.1 %copy-start = (bf16[384,3072]{1,0:T(8,128)(2,1)S(1)}, bf16[384,3072]{1,0:T(8,128)(2,1)}, u32[]{:S(2)}) copy-start(bf16[384,3072]{1,0:T(8,128)(2,1)} %param.18) | copy-start | bytes 7077892
  7.2 578.0 %all-reduce.3.cloned.1.call-start = ((), (), s32[]{:S(2)}) async-start(), calls=%async_computation | async-start | bytes 50331648 | tf_op jit(solution)/shard_map/psum | solution.py:68
  7.3 84.5 %copy-start.22 = (f32[64]{0:T(128)}, f32[64]{0:T(128)S(1)}, u32[]{:S(2)}) copy-start(f32[64]{0:T(128)S(1)} %multiply_power_fusion) | copy-start | bytes 772
  11.1 10.5 %copy-start.14 = (s32[4096]{0:T(1024)S(1)}, s32[4096]{0:T(1024)}, u32[]{:S(2)}) copy-start(s32[4096]{0:T(1024)} %param.12) | copy-start | bytes 49156
  91.8 9.3 copy-start.9
  106.0 190.1 %copy-start.2 = (bf16[4096,1,64]{0,2,1:T(8,128)(2,1)}, bf16[4096,1,64]{0,2,1:T(8,128)(2,1)S(1)}, u32[]{:S(2)}) copy-start(bf16[4096,1,64]{0,2,1:T(8,128)(2,1)S(1)} %get-tuple-element.12) | copy-start | bytes 1572868
  106.0 190.1 %copy-start.4 = (bf16[4096,1,64]{0,2,1:T(8,128)(2,1)}, bf16[4096,1,64]{0,2,1:T(8,128)(2,1)S(1)}, u32[]{:S(2)}) copy-start(bf16[4096,1,64]{0,2,1:T(8,128)(2,1)S(1)} %get-tuple-element.13) | copy-start | bytes 1572868
  118.3 5.8 slice-start.2
  118.3 5.8 copy-start.20
  132.4 0.7 slice-start.4
  132.4 0.7 copy-start.19
  133.3 2.0 slice-start.3
  133.3 2.0 copy-start.18
  135.5 2.4 copy-start.12
  135.5 2.4 slice-start.8
  135.5 2.4 copy-start.17
  138.2 0.9 slice-start.7
  139.4 3.2 slice-start.6
  143.0 3.6 copy-start.10
  143.0 3.6 slice-start.5
  147.0 4.0 slice-start.11
  152.1 1.5 slice-start.10
  155.3 4.8 slice-start.9
  161.4 5.1 copy-start.15
  174.3 2.0 copy-start.21
  191.1 3.9 copy-start.23
  192.7 3.4 copy-start.8
  196.6 2.0 copy-start.7
  196.6 2.0 copy-start.13
  201.1 2.2 slice-start
  201.6 1.9 slice-start.1
  204.2 1.6 copy-start.11
  205.7 3.9 copy-start.24
  255.7 2.1 copy-start.25
  288.6 7.5 copy-start.6
  325.6 0.7 copy-start.16
  325.7 643.3 %all-reduce.5.cloned.1.call-start = ((), (), s32[]{:S(2)}) async-start(), calls=%async_computation.1 | async-start | bytes 50331648 | tf_op jit(solution)/shard_map/psum | solution.py:74
  713.5 1.0 copy-start.3
  713.5 1.2 copy-start.5
  969.0 30.0 %copy-start.1 = (bf16[384,3072]{1,0:T(8,128)(2,1)S(1)}, bf16[384,3072]{1,0:T(8,128)(2,1)}, u32[]{:S(2)}) copy-start(bf16[384,3072]{1,0:T(8,128)(2,1)} %param.18) | copy-start | bytes 7077892
Sparse Core Ops, SparseCore 0:
  325.8 259.2 all-reduce.2
  713.7 255.2 all-reduce.4
where the time goes:
time: 1010 us
  waiting for transfers between devices  512 us (51%)
  matrix products  282 us (28%)
  other arithmetic  172 us (17%)
  local copies, waits for them, and re-layouts  24.5 us (2%)
  between operations  14.8 us (1%)
    psum x1, waiting for transfers between devices, local(): h = (x.astype(f32) + lax.psum(p, 'tp').astype(f32)).astype(bf)  259 us
    psum x1, waiting for transfers between devices, local(): y = (h.astype(f32) + lax.psum(rr, 'tp').astype(f32)).astype(bf)  253 us
    dot_general x16, matrix products, _attend(): jnp.einsum('grqk,kgd->qgrd', pr, v[:n], preferred_element_type=jnp.float32)  64.8 us
    dot_general x16, matrix products, _attend(): jnp.einsum('qgrd,kgd->grqk', q[lo:hi], k[:n], preferred_element_type=jnp....  50.3 us
    reduce_sum x16, other arithmetic, _attend(): pr = (e / jnp.sum(e, axis=-1, keepdims=True)).astype(jnp.bfloat16)  46.9 us
    reduce_sum x2, other arithmetic, _rms(): inv = lax.rsqrt(jnp.mean(x32 * x32, axis=-1, keepdims=True) + EPS)  35.7 us
    dot_general x1, matrix products, local(): up = jnp.dot(b, wu, preferred_element_type=f32)  35.1 us
    dot_general x1, matrix products, local(): rr = jnp.dot(u, wd, preferred_element_type=f32).astype(bf)  34.4 us
  transfers between devices with their start and end apart: 2, of which 2 were waited for; matrix products, arithmetic and copies ran while one was open for 0% of the time, Pallas kernels for 0%

commit v1 on v0

v1 whole, which is shorter than its diff:
```python
import functools

import jax
import jax.numpy as jnp
from jax import lax
from jax.experimental import pallas as pl
from jax.experimental.pallas import tpu as pltpu
from jax.sharding import PartitionSpec as P

HEAD = 128
EPS = 1e-5
ROPE_BASE = 500000.0
MESH = pl.DeviceIdType.MESH
BLOCK = 256
BF = jnp.bfloat16
F32 = jnp.float32


def _sincos(ang):
    n = jnp.floor(ang * 0.6366197723675814 + 0.5)
    r = ((ang - n * 1.5703125) - n * 4.837512969970703125e-4) - n * 7.54978995489188216e-8
    z = r * r
    s = ((-1.9515295891e-4 * z + 8.3321608736e-3) * z - 1.6666654611e-1) * z * r + r
    c = ((2.443315711809948e-5 * z - 1.388731625493765e-3) * z + 4.166664568298827e-2) * z * z - 0.5 * z + 1.0
    m = n.astype(jnp.int32)
    odd = (m & 1) == 1
    cs = jnp.where(odd, s, c)
    sn = jnp.where(odd, c, s)
    cs = jnp.where(((m + 1) & 2) == 2, -cs, cs)
    sn = jnp.where((m & 2) == 2, -sn, sn)
    return cs, sn


def _kernel(tp, dp, l1, l2, w2, w3,
            x_ref, posf_ref, inv_ref, g1_ref, g2_ref, wq_ref, wk_ref, wv_ref, wo_ref, wg_ref, wu_ref, wd_ref,
            y_ref, k_ref, v_ref, oall_ref,
            wqkv, wo_v, wg_v, wu_v, wd_v, x_buf, pos_buf, a_buf, q_scr, k_scr, v_scr, m_scr, l_scr, acc_scr, o_buf,
            o_blk, xh, hbuf, u_buf, r_buf, rsib, cp, rs1, rs2, sums, ych, hst,
            ld_w, ld_mlp, ld_x, ld_pos, kv_s,
            wo_a, wo_rel_s, wo_rel_r, wo_z_s, wo_z_r,
            o_s, o_rl, o_rr, o_rlr, o_rrr, o_rs, o_rel,
            ld_o, h_s, h_r, r_s, r_r, s1_s, s1_r, s2_s, s2_r, y_s, y_rl, y_rr, y_rlr, y_rrr, y_rs, y_rel):
    t, d = x_ref.shape
    qw = wq_ref.shape[1]
    f = wg_ref.shape[1]
    hl = qw // HEAD
    b = BLOCK
    nb = t // b
    dh = d // 2
    hb = b // 2
    nc = tp // 2
    ow = hb // nc
    hw = ow // 2
    kvt = min(2 * b, t)

    r = lax.axis_index("tp")
    c = r // 2
    s = r % 2
    c_r = (c + 1) % nc
    c_l = (c + nc - 1) % nc
    c_o = (c + 2) % nc
    right = {"tp": c_r * 2 + s}
    left = {"tp": c_l * 2 + s}
    sib = {"tp": c * 2 + 1 - s}
    share = dp % 2 == 0
    dpi = lax.axis_index("dp")
    par = dpi % 2
    peer = {"dp": dpi + 1 - 2 * par}

    def al(v, m):
        return pl.multiple_of(v, m)

    def send(src, dst, ss, rs, dev):
        pltpu.make_async_remote_copy(
            src_ref=src, dst_ref=dst, send_sem=ss, recv_sem=rs, device_id=dev, device_id_type=MESH).start()

    def put(src, dst, sem):
        pltpu.make_async_copy(src, dst, sem).start()

    def wait(region, sem):
        pltpu.make_async_copy(region, region, sem).wait()

    barrier = pltpu.get_barrier_semaphore()
    others = [right, left, sib] + ([peer] if share else [])
    for dev in others:
        pl.semaphore_signal(barrier, inc=1, device_id=dev, device_id_type=MESH)
    pl.semaphore_wait(barrier, len(others))

    ro = al(r * qw, 128)
    mine = al(s * dh, 128)
    other = al((1 - s) * dh, 128)
    send(wo_ref.at[:, pl.ds(other, dh)], wo_v.at[pl.ds(ro, qw)], wo_a.at[0], wo_a.at[1], sib)
    put(wo_ref.at[:, pl.ds(mine, dh)], wo_v.at[pl.ds(ro, qw)], wo_a.at[2])
    put(x_ref.at[pl.ds(0, b)], x_buf.at[0], ld_x.at[0])
    put(posf_ref.at[pl.ds(0, b)], pos_buf.at[0], ld_pos.at[0])
    rk = al(r * HEAD, 128)
    put(wq_ref, wqkv.at[:, pl.ds(0, qw)], ld_w.at[0])
    put(wk_ref.at[:, pl.ds(rk, HEAD)], wqkv.at[:, pl.ds(qw, HEAD)], ld_w.at[1])
    put(wv_ref.at[:, pl.ds(rk, HEAD)], wqkv.at[:, pl.ds(qw + HEAD, HEAD)], ld_w.at[2])
    put(wg_ref, wg_v, ld_mlp.at[0])
    put(wu_ref, wu_v, ld_mlp.at[1])
    put(wd_ref, wd_v, ld_mlp.at[2])

    wr = qw if share else 2 * qw
    woff = par * qw if share else 0

    def wrow(chip, half=None):
        base = al(chip * (2 * qw) + woff, 64)
        if half is None:
            return wo_v.at[pl.ds(base, wr)]
        return wo_v.at[pl.ds(al(base + half * (wr // 2), 64), wr // 2)]

    rs_sib = al((r + 1 - 2 * s) * qw, 128)
    wait(wo_v.at[pl.ds(rs_sib, qw)], wo_a.at[1])
    wait(wo_v.at[pl.ds(ro, qw)], wo_a.at[2])
    send(wrow(c), wrow(c), wo_a.at[3], wo_a.at[4], right)
    send(wrow(c), wrow(c), wo_a.at[5], wo_a.at[6], left)

    def wo_stage2():
        wait(wrow(c_l), wo_a.at[4])
        send(wrow(c_l, 0), wrow(c_l, 0), wo_rel_s.at[0], wo_rel_r.at[0], right)
        if share:
            send(wrow(c_l), wrow(c_l), wo_z_s, wo_z_r, peer)
        wait(wrow(c_r), wo_a.at[6])
        send(wrow(c_r, 1), wrow(c_r, 1), wo_rel_s.at[1], wo_rel_r.at[1], left)
        if share:
            send(wrow(c_r), wrow(c_r), wo_z_s, wo_z_r, peer)

    def wo_stage3():
        wait(wrow(c_o, 0), wo_rel_r.at[0])
        wait(wrow(c_o, 1), wo_rel_r.at[1])
        if share:
            send(wrow(c_o), wrow(c_o), wo_z_s, wo_z_r, peer)

    def ocol(chip, core):
        return pl.ds(al((chip * 2 + core) * qw, 128), qw)

    def orow(j):
        return pl.ds(al(j * b, b), b)

    def orow_half(j, half):
        return pl.ds(al(j * b + half * hb, hb), hb)

    def o_stage2(j):
        @pl.when((j >= 0) & (j < nb))
        def _():
            reg = oall_ref.at[orow(j), ocol(c_l, s)]
            top = oall_ref.at[orow_half(j, 0), ocol(c_l, s)]
            wait(reg, o_rl.at[j])
            send(top, top, o_rel.at[0], o_rlr.at[j], right)
            send(reg, reg, o_rel.at[2], o_rs.at[j], sib)
            reg = oall_ref.at[orow(j), ocol(c_r, s)]
            bot = oall_ref.at[orow_half(j, 1), ocol(c_r, s)]
            wait(reg, o_rr.at[j])
            send(bot, bot, o_rel.at[1], o_rrr.at[j], left)
            send(reg, reg, o_rel.at[2], o_rs.at[j], sib)

    def o_stage3(j):
        @pl.when((j >= 0) & (j < nb))
        def _():
            top = oall_ref.at[orow_half(j, 0), ocol(c_o, s)]
            bot = oall_ref.at[orow_half(j, 1), ocol(c_o, s)]
            reg = oall_ref.at[orow(j), ocol(c_o, s)]
            wait(top, o_rlr.at[j])
            wait(bot, o_rrr.at[j])
            send(reg, reg, o_rel.at[2], o_rs.at[j], sib)

    scale = HEAD ** -0.5 * 1.4426950408889634
    for h in range(t // kvt):
        v_scr[h * kvt:(h + 1) * kvt, :] = jnp.zeros((kvt, HEAD), BF)
        k_scr[h * kvt:(h + 1) * kvt, :] = jnp.zeros((kvt, HEAD), BF)
    wait(wqkv.at[:, pl.ds(0, qw)], ld_w.at[0])
    wait(wqkv.at[:, pl.ds(qw, HEAD)], ld_w.at[1])
    wait(wqkv.at[:, pl.ds(qw, HEAD)], ld_w.at[2])
    lane = lax.broadcasted_iota(jnp.int32, (b, HEAD), 1)

    def tile(i, j, masked):
        keys = pl.ds(al(j * kvt, kvt), kvt)
        kk = k_scr[keys, :]
        vv = v_scr[keys, :]
        for h in range(hl):
            sc = lax.dot_general(q_scr[h], kk, (((1,), (1,)), ((), ())), preferred_element_type=F32)
            if masked:
                rows = i * b + lax.broadcasted_iota(jnp.int32, (b, kvt), 0)
                cols = j * kvt + lax.broadcasted_iota(jnp.int32, (b, kvt), 1)
                sc = jnp.where(cols <= rows, sc, -jnp.inf)
            m_prev = m_scr[h]
            m_new = jnp.maximum(m_prev, jnp.max(sc, axis=1, keepdims=True))
            parts = [jnp.exp2((sc[:, e * HEAD:(e + 1) * HEAD] - m_new) * scale) for e in range(kvt // HEAD)]
            alpha = jnp.exp2((m_prev - m_new) * scale)
            l_scr[h] = l_scr[h] * alpha + functools.reduce(lambda p, q: p + q, parts)
            pr = jnp.concatenate([p.astype(BF) for p in parts], axis=1)
            acc_scr[h] = acc_scr[h] * alpha + jnp.dot(pr, vv, preferred_element_type=F32)
            m_scr[h] = m_new

    def phase1(i, carry):
        slot = i % 2
        wait(x_buf.at[slot], ld_x.at[slot])
        wait(pos_buf.at[slot], ld_pos.at[slot])

        @pl.when(i + 1 < nb)
        def _():
            put(x_ref.at[pl.ds(al((i + 1) * b, b), b)], x_buf.at[1 - slot], ld_x.at[1 - slot])
            put(posf_ref.at[pl.ds(al((i + 1) * b, b), b)], pos_buf.at[1 - slot], ld_pos.at[1 - slot])

        def norm(j, carry):
            rows = pl.ds(al(j * 16, 16), 16)
            v32 = x_buf[slot, rows, :].astype(F32)
            inv = lax.rsqrt(jnp.mean(v32 * v32, axis=1, keepdims=True) + EPS)
            a_buf[rows, :] = (v32 * inv * g1_ref[...].astype(F32)).astype(BF)
            return carry

        lax.fori_loop(0, b // 16, norm, 0)
        co, si = _sincos(pos_buf[slot] * inv_ref[...])
        si = jnp.where(lane < HEAD // 2, -si, si)
        qkv = jnp.dot(a_buf[...], wqkv[...], preferred_element_type=F32)

        def rope(v32):
            return (v32 * co + pltpu.roll(v32, HEAD // 2, 1) * si).astype(BF)

        rows = pl.ds(al(i * b, b), b)
        for h in range(hl):
            q_scr[h] = rope(qkv[:, h * HEAD:(h + 1) * HEAD])
        k_scr[rows, :] = rope(qkv[:, qw:qw + HEAD])
        v_scr[rows, :] = qkv[:, qw + HEAD:qw + 2 * HEAD].astype(BF)
        for h in range(hl):
            m_scr[h] = jnp.full((b, HEAD), -jnp.inf, F32)
            l_scr[h] = jnp.zeros((b, HEAD), F32)
            acc_scr[h] = jnp.zeros((b, HEAD), F32)
        last = (i * b) // kvt

        def inner(j, carry):
            tile(i, j, False)
            return carry

        lax.fori_loop(0, last, inner, 0)
        tile(i, last, True)
        for h in range(hl):
            o_buf[rows, h * HEAD:(h + 1) * HEAD] = (
                acc_scr[h] / jnp.sum(l_scr[h], axis=1, keepdims=True)).astype(BF)
        src = o_buf.at[rows]
        dst = oall_ref.at[orow(i), ocol(c, s)]
        send(src, dst, o_s.at[0], o_rl.at[i], right)
        send(src, dst, o_s.at[1], o_rr.at[i], left)
        send(src, dst, o_s.at[2], o_rs.at[i], sib)
        put(src, dst, o_s.at[3])

        @pl.when(i == w2)
        def _():
            wo_stage2()

        @pl.when(i == w3)
        def _():
            wo_stage3()

        o_stage2(i - l1)
        o_stage3(i - l2)
        return carry

    lax.fori_loop(0, nb, phase1, 0)
    put(k_scr, k_ref, kv_s.at[0])
    put(v_scr, v_ref, kv_s.at[1])
    wait(o_buf, o_s.at[3])
    wait(wg_v, ld_mlp.at[0])
    wait(wu_v, ld_mlp.at[1])
    wait(wd_v, ld_mlp.at[2])
    if share:
        wait(wo_v.at[pl.ds(0, 3 * wr)], wo_z_r)

    def load_o(j):
        wait(oall_ref.at[orow(j), pl.ds(0, 4 * qw)], o_rs.at[j])
        put(oall_ref.at[orow(j)], o_blk, ld_o.at[0])
        put(x_ref.at[orow(j), pl.ds(mine, dh)], xh, ld_o.at[1])

    nt_h = min(512, dh)
    nt_f = min(256, f)
    nt_d = min(512, d)

    def sum_start(j):
        @pl.when((j >= 0) & (j < nb))
        def _():
            two = j % 2
            q4 = j % 4
            wait(rsib.at[two], r_r.at[two])
            wait(rsib.at[two], r_s)

            def add(e, carry):
                rows = pl.ds(al(e * 16, 16), 16)
                own = r_buf[pl.ds(al(s * hb + e * 16, 16), 16), :]
                cp[q4, rows, :] = (own.astype(F32) + rsib[two, rows, :].astype(F32)).astype(BF)
                return carry

            lax.fori_loop(0, hb // 16, add, 0)

            def part(chip, half):
                return cp.at[q4, pl.ds(al(chip * ow + half * hw, hw), hw)]

            send(part(c_o, 0), rs1.at[q4, 0], s1_s.at[q4, 0], s1_r.at[q4, 0], right)
            send(part(c_o, 1), rs1.at[q4, 2], s1_s.at[q4, 2], s1_r.at[q4, 2], left)
            send(part(c_r, 1), rs1.at[q4, 1], s1_s.at[q4, 1], s1_r.at[q4, 1], right)
            send(part(c_l, 0), rs1.at[q4, 3], s1_s.at[q4, 3], s1_r.at[q4, 3], left)

    def own_h(j):
        @pl.when(j < nb)
        def _():
            two = j % 2
            wait(o_blk, ld_o.at[0])
            wait(xh, ld_o.at[1])

            def col(n, carry):
                cols = pl.ds(al(n * nt_h, nt_h), nt_h)
                v32 = jnp.dot(o_blk[...], wo_v[:, cols], preferred_element_type=F32)
                hbuf[two, :, pl.ds(al(s * dh + n * nt_h, 128), nt_h)] = (xh[:, cols].astype(F32) + v32).astype(BF)
                return carry

            lax.fori_loop(0, dh // nt_h, col, 0)
            half = hbuf.at[two, :, pl.ds(mine, dh)]
            send(half, half, h_s.at[two], h_r.at[two], sib)

        @pl.when(j + 1 < nb)
        def _():
            load_o(j + 1)

    def mlp_norm(j):
        @pl.when((j >= 0) & (j < nb))
        def _():
            two = j % 2
            wait(hbuf.at[two, :, pl.ds(other, dh)], h_r.at[two])
            wait(hbuf.at[two, :, pl.ds(mine, dh)], h_s.at[two])

            def norm(e, carry):
                rows = pl.ds(al(e * 16, 16), 16)
                v32 = hbuf[two, rows, :].astype(F32)
                inv = lax.rsqrt(jnp.mean(v32 * v32, axis=1, keepdims=True) + EPS)
                a_buf[rows, :] = (v32 * inv * g2_ref[...].astype(F32)).astype(BF)
                return carry

            lax.fori_loop(0, b // 16, norm, 0)
            hst[j % 4] = hbuf[two, pl.ds(al(s * hb + c * ow, 16), ow), :]

    def mlp_up(j):
        @pl.when((j >= 0) & (j < nb))
        def _():
            def col(n, carry):
                cols = pl.ds(al(n * nt_f, nt_f), nt_f)
                gt = jnp.dot(a_buf[...], wg_v[:, cols], preferred_element_type=F32)
                up = jnp.dot(a_buf[...], wu_v[:, cols], preferred_element_type=F32)
                u_buf[:, cols] = (gt * (1.0 / (1.0 + jnp.exp(-gt))) * up).astype(BF)
                return carry

            lax.fori_loop(0, f // nt_f, col, 0)

    def mlp_down(j):
        @pl.when((j >= 0) & (j < nb))
        def _():
            def col(n, carry):
                cols = pl.ds(al(n * nt_d, nt_d), nt_d)
                r_buf[:, cols] = jnp.dot(u_buf[...], wd_v[:, cols], preferred_element_type=F32).astype(BF)
                return carry

            lax.fori_loop(0, d // nt_d, col, 0)
            send(r_buf.at[pl.ds(al((1 - s) * hb, hb), hb)], rsib.at[j % 2], r_s, r_r.at[j % 2], sib)

    def sum_relay(j):
        @pl.when((j >= 0) & (j < nb))
        def _():
            q4 = j % 4

            @pl.when(j >= 4)
            def _():
                wait(sums.at[q4, 0], s2_s.at[q4, 0])
                wait(sums.at[q4, 1], s2_s.at[q4, 1])

            wait(rs1.at[q4, 0], s1_r.at[q4, 0])
            sums[q4, 0] = (rs1[q4, 0].astype(F32) + cp[q4, pl.ds(al(c_r * ow, 16), hw), :].astype(F32)).astype(BF)
            send(sums.at[q4, 0], rs2.at[q4, 0], s2_s.at[q4, 0], s2_r.at[q4, 0], right)
            wait(rs1.at[q4, 2], s1_r.at[q4, 2])
            sums[q4, 1] = (rs1[q4, 2].astype(F32) + cp[q4, pl.ds(al(c_l * ow + hw, 16), hw), :].astype(F32)).astype(BF)
            send(sums.at[q4, 1], rs2.at[q4, 1], s2_s.at[q4, 1], s2_r.at[q4, 1], left)

    def yrow(j, core, chip):
        return y_ref.at[pl.ds(al(j * b + core * hb + chip * ow, ow), ow)]

    def yrow_half(j, core, chip, half):
        return y_ref.at[pl.ds(al(j * b + core * hb + chip * ow + half * hw, hw), hw)]

    def sum_end(j):
        @pl.when((j >= 0) & (j < nb))
        def _():
            q4 = j % 4

            @pl.when(j >= 4)
            def _():
                for e in range(4):
                    wait(ych.at[q4], y_s.at[q4, e])

            for e in range(4):
                wait(rs1.at[q4, e], s1_s.at[q4, e])
            wait(rs1.at[q4, 1], s1_r.at[q4, 1])
            wait(rs1.at[q4, 3], s1_r.at[q4, 3])
            wait(rs2.at[q4, 0], s2_r.at[q4, 0])
            wait(rs2.at[q4, 1], s2_r.at[q4, 1])
            for half, (near, far) in enumerate(((3, 0), (1, 1))):
                own = cp[q4, pl.ds(al(c * ow + half * hw, 16), hw), :].astype(F32)
                tot = own + rs1[q4, near].astype(F32) + rs2[q4, far].astype(F32)
                hh = hst[q4, half * hw:(half + 1) * hw, :].astype(F32)
                ych[q4, half * hw:(half + 1) * hw, :] = (hh + tot).astype(BF)
            dst = yrow(j, s, c)
            send(ych.at[q4], dst, y_s.at[q4, 0], y_rl.at[j], right)
            send(ych.at[q4], dst, y_s.at[q4, 1], y_rr.at[j], left)
            send(ych.at[q4], dst, y_s.at[q4, 2], y_rs.at[j], sib)
            put(ych.at[q4], dst, y_s.at[q4, 3])

    def y_stage2(j):
        @pl.when((j >= 0) & (j < nb))
        def _():
            reg = yrow(j, s, c_l)
            top = yrow_half(j, s, c_l, 0)
            wait(reg, y_rl.at[j])
            send(top, top, y_rel.at[0], y_rlr.at[j], right)
            send(reg, reg, y_rel.at[2], y_rs.at[j], sib)
            reg = yrow(j, s, c_r)
            bot = yrow_half(j, s, c_r, 1)
            wait(reg, y_rr.at[j])
            send(bot, bot, y_rel.at[1], y_rrr.at[j], left)
            send(reg, reg, y_rel.at[2], y_rs.at[j], sib)

    def y_stage3(j):
        @pl.when((j >= 0) & (j < nb))
        def _():
            wait(yrow_half(j, s, c_o, 0), y_rlr.at[j])
            wait(yrow_half(j, s, c_o, 1), y_rrr.at[j])
            reg = yrow(j, s, c_o)
            send(reg, reg, y_rel.at[2], y_rs.at[j], sib)

    load_o(0)

    def phase2(i, carry):
        sum_start(i - 2)
        own_h(i)
        mlp_norm(i - 1)
        sum_relay(i - 3)
        mlp_up(i - 1)
        sum_end(i - 4)
        mlp_down(i - 1)
        y_stage2(i - 5)
        y_stage3(i - 6)
        o_stage2(nb + i - l1)
        o_stage3(nb + i - l2)
        return carry

    lax.fori_loop(0, nb + 6, phase2, 0)

    def drain(j, carry):
        wait(y_ref.at[pl.ds(0, hb)], y_rs.at[j])
        return carry

    lax.fori_loop(0, nb, drain, 0)
    for q4 in range(4):
        for e in range(4):
            wait(ych.at[q4], y_s.at[q4, e])
        for e in range(2):
            wait(sums.at[q4, e], s2_s.at[q4, e])
    wait(y_ref.at[pl.ds(0, nb * hw)], y_rel.at[0])
    wait(y_ref.at[pl.ds(0, nb * hw)], y_rel.at[1])
    wait(y_ref.at[pl.ds(0, nb * ow * 3)], y_rel.at[2])
    for e in range(3):
        wait(o_buf, o_s.at[e])
    wait(oall_ref.at[pl.ds(0, t // 2), pl.ds(0, qw)], o_rel.at[0])
    wait(oall_ref.at[pl.ds(0, t // 2), pl.ds(0, qw)], o_rel.at[1])
    wait(oall_ref.at[:, pl.ds(0, 3 * qw)], o_rel.at[2])
    wait(wo_v.at[pl.ds(0, qw)], wo_a.at[0])
    wait(wo_v.at[pl.ds(0, wr)], wo_a.at[3])
    wait(wo_v.at[pl.ds(0, wr)], wo_a.at[5])
    for e in range(2):
        wait(wo_v.at[pl.ds(0, wr // 2)], wo_rel_s.at[e])
    if share:
        wait(wo_v.at[pl.ds(0, 3 * wr)], wo_z_s)
    wait(k_scr, kv_s.at[0])
    wait(v_scr, kv_s.at[1])


def _layer(tp, dp, x, posf, inv, g1, g2, wq, wk, wv, wo, wg, wu, wd):
    t, d = x.shape
    qw = wq.shape[1]
    f = wg.shape[1]
    hl = qw // HEAD
    b = BLOCK
    nb = t // b
    hb = b // 2
    nc = tp // 2
    ow = hb // nc
    hw = ow // 2
    assert nc == 4 and t % b == 0 and wk.shape[1] == tp * HEAD
    l1 = max(1, nb * 3 // 8)
    l2 = l1 + max(1, nb // 8)
    w2 = nb * 5 // 16
    w3 = nb * 9 // 16
    dma = pltpu.SemaphoreType.DMA
    hbm = pl.BlockSpec(memory_space=pl.ANY)
    vm = pl.BlockSpec(memory_space=pltpu.VMEM)
    scratch = [
        pltpu.VMEM((d, qw + 2 * HEAD), BF),
        pltpu.VMEM((tp * qw, d // 2), BF),
        pltpu.VMEM((d, f), BF),
        pltpu.VMEM((d, f), BF),
        pltpu.VMEM((f, d), BF),
        pltpu.VMEM((2, b, d), BF),
        pltpu.VMEM((2, b, HEAD), F32),
        pltpu.VMEM((b, d), BF),
        pltpu.VMEM((hl, b, HEAD), BF),
        pltpu.VMEM((t, HEAD), BF),
        pltpu.VMEM((t, HEAD), BF),
        pltpu.VMEM((hl, b, HEAD), F32),
        pltpu.VMEM((hl, b, HEAD), F32),
        pltpu.VMEM((hl, b, HEAD), F32),
        pltpu.VMEM((t, qw), BF),
        pltpu.VMEM((b, tp * qw), BF),
        pltpu.VMEM((b, d // 2), BF),
        pltpu.VMEM((2, b, d), BF),
        pltpu.VMEM((b, f), BF),
        pltpu.VMEM((b, d), BF),
        pltpu.VMEM((2, hb, d), BF),
        pltpu.VMEM((4, hb, d), BF),
        pltpu.VMEM((4, 4, hw, d), BF),
        pltpu.VMEM((4, 2, hw, d), BF),
        pltpu.VMEM((4, 2, hw, d), BF),
        pltpu.VMEM((4, ow, d), BF),
        pltpu.VMEM((4, ow, d), BF),
        dma((3,)), dma((3,)), dma((2,)), dma((2,)), dma((2,)),
        dma((7,)), dma((2,)), dma((2,)), dma(()), dma(()),
        dma((4,)), dma((nb,)), dma((nb,)), dma((nb,)), dma((nb,)), dma((nb,)), dma((3,)),
        dma((2,)), dma((2,)), dma((2,)), dma(()), dma((2,)), dma((4, 4)), dma((4, 4)), dma((4, 2)), dma((4, 2)),
        dma((4, 4)), dma((nb,)), dma((nb,)), dma((nb,)), dma((nb,)), dma((nb,)), dma((3,)),
    ]
    flops = 2 * t * (d * (qw + 2 * HEAD) + qw * t + tp * qw * d // 2 + 3 * d * f)
    return pl.pallas_call(
        functools.partial(_kernel, tp, dp, l1, l2, w2, w3),
        name="layer",
        out_shape=(
            jax.ShapeDtypeStruct((t, d), BF),
            jax.ShapeDtypeStruct((t, HEAD), BF),
            jax.ShapeDtypeStruct((t, HEAD), BF),
            jax.ShapeDtypeStruct((t, tp * qw), BF),
        ),
        in_specs=[hbm, hbm, vm, vm, vm] + [hbm] * 7,
        out_specs=(hbm, hbm, hbm, hbm),
        scratch_shapes=scratch,
        compiler_params=pltpu.CompilerParams(
            collective_id=0, has_side_effects=True, vmem_limit_bytes=66 * 1000 * 1000),
        cost_estimate=pl.CostEstimate(flops=flops, bytes_accessed=8 * t * d, transcendentals=t * t * hl),
    )(x, posf, inv, g1, g2, wq, wk, wv, wo, wg, wu, wd)


def solution(mesh):
    tp = mesh.shape["tp"]
    dp = mesh.shape["dp"]

    def local(x, pos, g1, g2, wq, wk, wv, wo, wg, wu, wd):
        t, d = x.shape
        half = HEAD // 2
        inv = ROPE_BASE ** (-2.0 * jnp.arange(half, dtype=F32) / HEAD)
        inv = jnp.concatenate([inv, inv])[None, :]
        posf = jnp.broadcast_to(pos.astype(F32)[:, None], (t, HEAD))
        y, k, v, _ = _layer(tp, dp, x, posf, inv, g1[None, :], g2[None, :], wq, wk, wv, wo, wg, wu, wd)
        return y, k.reshape(t, 1, HEAD), v.reshape(t, 1, HEAD)

    return jax.shard_map(
        local,
        mesh=mesh,
        in_specs=(P("dp", None), P("dp"), P(), P(), P(None, "tp"), P(), P(), P("tp", None),
                  P(None, "tp"), P(None, "tp"), P("tp", None)),
        out_specs=(P("dp", None), P("dp", "tp", None), P("dp", "tp", None)),
        check_vma=False,
    )
```

time: 1010 us -> 465 us (0.46)
  waiting for transfers between devices: 512 us -> 0 us
  Pallas kernels: 0 us -> 435 us
  matrix products: 282 us -> 0 us
  other arithmetic: 172 us -> 1.32 us
  between operations: 14.8 us -> 0.66 us
    psum x2 -> x0, waiting for transfers between devices: 512 us -> none  [the longest x1 259 us: local(): h = (x.astype(f32) + lax.psum(p, 'tp').astype(f32)).astype(bf)]
    pallas_call x0 -> x1, Pallas kernels: none -> 435 us  [_layer(): pl.pallas_call(functools.partial(_kernel, tp, dp, l1, l2, w2, w3), name='...]
    dot_general x39 -> x0, matrix products: 282 us -> none  [the longest x16 64.8 us: _attend(): jnp.einsum('grqk,kgd->qgrd', pr, v[:n], preferred_element_type=jnp.float32)]
    reduce_sum x18 -> x0, other arithmetic: 82.6 us -> none  [the longest x16 46.9 us: _attend(): pr = (e / jnp.sum(e, axis=-1, keepdims=True)).astype(jnp.bfloat16)]
    convert_element_type x5 -> x1, other arithmetic: 53.9 us -> 0.72 us  [local(): posf = jnp.broadcast_to(pos.astype(F32)[:, None], (t, HEAD))]
    le x16 -> x0, other arithmetic: 14.7 us -> none  [_attend(): pos_k[:n][None, :] <= pp[:, None]]
    another operation x2 -> x0, other arithmetic: 11.7 us -> none
    unnamed x59 -> x7, local copies, waits for them, and re-layouts: 15.4 us -> 22.8 us
  transfers between devices with their start and end apart: 2 -> 0, of which waited for: 2 -> 0; matrix products, arithmetic and copies ran while one was open for 0% -> 0% of each run, Pallas kernels for 0% -> 0%
where the time goes in v1:
time: 465 us; the launch traced here: 464 us
  Pallas kernels  435 us (94%)
  local copies, waits for them, and re-layouts  27.3 us (6%)
    pallas_call x1, Pallas kernels, _layer(): pl.pallas_call(functools.partial(_kernel, tp, dp, l1, l2, w2, w3), name='...  435 us
    unnamed x7, local copies, waits for them, and re-layouts  22.8 us

profile of v1, /device:TPU:81, one launch (start us, length us, event | category | flops | bytes accessed | tf_op | source)
XLA Modules:
  0.0 464.1 jit_solution(1957027266048985441)
XLA Ops:
  0.6 0.6 maximum_bitcast_fusion.inv_ref
  1.2 1.3 broadcast_in_dim.17.g1_ref
  2.5 1.3 broadcast_in_dim.18.g2_ref
  3.8 0.7 convert_element_type.3
  4.6 1.9 broadcast_in_dim.15.posf_ref
  6.5 434.8 %layer.1 = (bf16[4096,3072]{1,0:T(8,128)(2,1)}, bf16[4096,128]{1,0:T(8,128)(2,1)}, bf16[4096,128]{1,0:T(8,128)(2,1)}, bf16[4096,3072]{1,0:T(8,128)(2,1)}) custom-call(bf16[4096,3072]{1,0:T(8,128)(2,1)} %x_ref.1, f32[4096,128]{1,0:T(8,128)} %broadcast_in_dim.15.posf_ref, f32[1,128]{1,0:T(1,128)} %maximum_bitcast_fusion.inv_ref, ...), custom_call_target="tpu_custom_call" | custom-call | flops 144955146240 | bytes 100663296 | tf_op jit(solution)/shard_map/layer/pallas_call | solution.py:537
  441.3 0.0 copy-start.1
  441.3 0.0 copy-start
  441.3 20.8 %copy.17 = bf16[4096,3072]{1,0:T(8,128)(2,1)} copy(bf16[4096,3072]{1,0:T(8,128)(2,1)} %get-tuple-element.12) | data formatting | bytes 50331648
  462.1 0.0 copy-done.1
  462.1 1.0 copy.18
  463.1 0.0 copy-done
  463.1 1.0 copy.19
  (1 shorter events, 0.0 us)
Async XLA Ops:
  441.3 20.8 %copy-start.1 = (bf16[4096,128]{1,0:T(8,128)(2,1)S(1)}, bf16[4096,128]{1,0:T(8,128)(2,1)}, u32[]{:S(2)}) copy-start(bf16[4096,128]{1,0:T(8,128)(2,1)} %get-tuple-element.7) | copy-start | bytes 3145732
  441.3 21.8 %copy-start = (bf16[4096,128]{1,0:T(8,128)(2,1)S(1)}, bf16[4096,128]{1,0:T(8,128)(2,1)}, u32[]{:S(2)}) copy-start(bf16[4096,128]{1,0:T(8,128)(2,1)} %get-tuple-element.8) | copy-start | bytes 3145732

commit v2 on v1

--- a/solution.py
+++ b/solution.py
@@ -2,6 +2,7 @@
 
 import jax
 import jax.numpy as jnp
+import numpy as np
 from jax import lax
 from jax.experimental import pallas as pl
 from jax.experimental.pallas import tpu as pltpu
@@ -12,6 +13,7 @@
 ROPE_BASE = 500000.0
 MESH = pl.DeviceIdType.MESH
 BLOCK = 256
+NR = 64
 BF = jnp.bfloat16
 F32 = jnp.float32
 
@@ -32,11 +34,11 @@
 
 
 def _kernel(tp, dp, l1, l2, w2, w3,
-            x_ref, posf_ref, inv_ref, g1_ref, g2_ref, wq_ref, wk_ref, wv_ref, wo_ref, wg_ref, wu_ref, wd_ref,
+            x_ref, pos_ref, inv_ref, g1_ref, g2_ref, wq_ref, wk_ref, wv_ref, wo_ref, wg_ref, wu_ref, wd_ref,
             y_ref, k_ref, v_ref, oall_ref,
-            wqkv, wo_v, wg_v, wu_v, wd_v, x_buf, pos_buf, a_buf, q_scr, k_scr, v_scr, m_scr, l_scr, acc_scr, o_buf,
+            wqkv, wo_v, wg_v, wu_v, wd_v, x_buf, g_scr, a_buf, q_scr, k_scr, v_scr, m_scr, l_scr, acc_scr, o_buf,
             o_blk, xh, hbuf, u_buf, r_buf, rsib, cp, rs1, rs2, sums, ych, hst,
-            ld_w, ld_mlp, ld_x, ld_pos, kv_s,
+            ld_w, ld_mlp, ld_x, kv_s,
             wo_a, wo_rel_s, wo_rel_r, wo_z_s, wo_z_r,
             o_s, o_rl, o_rr, o_rlr, o_rrr, o_rs, o_rel,
             ld_o, h_s, h_r, r_s, r_r, s1_s, s1_r, s2_s, s2_r, y_s, y_rl, y_rr, y_rlr, y_rrr, y_rs, y_rel):
@@ -77,8 +79,12 @@
     def put(src, dst, sem):
         pltpu.make_async_copy(src, dst, sem).start()
 
-    def wait(region, sem):
-        pltpu.make_async_copy(region, region, sem).wait()
+    def wait(region, sem, tag=None):
+        if tag is None:
+            pltpu.make_async_copy(region, region, sem).wait()
+        else:
+            with jax.named_scope("w_" + tag):
+                pltpu.make_async_copy(region, region, sem).wait()
 
     barrier = pltpu.get_barrier_semaphore()
     others = [right, left, sib] + ([peer] if share else [])
@@ -92,15 +98,10 @@
     send(wo_ref.at[:, pl.ds(other, dh)], wo_v.at[pl.ds(ro, qw)], wo_a.at[0], wo_a.at[1], sib)
     put(wo_ref.at[:, pl.ds(mine, dh)], wo_v.at[pl.ds(ro, qw)], wo_a.at[2])
     put(x_ref.at[pl.ds(0, b)], x_buf.at[0], ld_x.at[0])
-    put(posf_ref.at[pl.ds(0, b)], pos_buf.at[0], ld_pos.at[0])
     rk = al(r * HEAD, 128)
     put(wq_ref, wqkv.at[:, pl.ds(0, qw)], ld_w.at[0])
     put(wk_ref.at[:, pl.ds(rk, HEAD)], wqkv.at[:, pl.ds(qw, HEAD)], ld_w.at[1])
     put(wv_ref.at[:, pl.ds(rk, HEAD)], wqkv.at[:, pl.ds(qw + HEAD, HEAD)], ld_w.at[2])
-    put(wg_ref, wg_v, ld_mlp.at[0])
-    put(wu_ref, wu_v, ld_mlp.at[1])
-    put(wd_ref, wd_v, ld_mlp.at[2])
-
     wr = qw if share else 2 * qw
     woff = par * qw if share else 0
 
@@ -111,24 +112,24 @@
         return wo_v.at[pl.ds(al(base + half * (wr // 2), 64), wr // 2)]
 
     rs_sib = al((r + 1 - 2 * s) * qw, 128)
-    wait(wo_v.at[pl.ds(rs_sib, qw)], wo_a.at[1])
+    wait(wo_v.at[pl.ds(rs_sib, qw)], wo_a.at[1], "wo")
     wait(wo_v.at[pl.ds(ro, qw)], wo_a.at[2])
     send(wrow(c), wrow(c), wo_a.at[3], wo_a.at[4], right)
     send(wrow(c), wrow(c), wo_a.at[5], wo_a.at[6], left)
 
     def wo_stage2():
-        wait(wrow(c_l), wo_a.at[4])
+        wait(wrow(c_l), wo_a.at[4], "wo2")
         send(wrow(c_l, 0), wrow(c_l, 0), wo_rel_s.at[0], wo_rel_r.at[0], right)
         if share:
             send(wrow(c_l), wrow(c_l), wo_z_s, wo_z_r, peer)
-        wait(wrow(c_r), wo_a.at[6])
+        wait(wrow(c_r), wo_a.at[6], "wo2")
         send(wrow(c_r, 1), wrow(c_r, 1), wo_rel_s.at[1], wo_rel_r.at[1], left)
         if share:
             send(wrow(c_r), wrow(c_r), wo_z_s, wo_z_r, peer)
 
     def wo_stage3():
-        wait(wrow(c_o, 0), wo_rel_r.at[0])
-        wait(wrow(c_o, 1), wo_rel_r.at[1])
+        wait(wrow(c_o, 0), wo_rel_r.at[0], "wo3")
+        wait(wrow(c_o, 1), wo_rel_r.at[1], "wo3")
         if share:
             send(wrow(c_o), wrow(c_o), wo_z_s, wo_z_r, peer)
 
@@ -146,12 +147,12 @@
         def _():
             reg = oall_ref.at[orow(j), ocol(c_l, s)]
             top = oall_ref.at[orow_half(j, 0), ocol(c_l, s)]
-            wait(reg, o_rl.at[j])
+            wait(reg, o_rl.at[j], "o2")
             send(top, top, o_rel.at[0], o_rlr.at[j], right)
             send(reg, reg, o_rel.at[2], o_rs.at[j], sib)
             reg = oall_ref.at[orow(j), ocol(c_r, s)]
             bot = oall_ref.at[orow_half(j, 1), ocol(c_r, s)]
-            wait(reg, o_rr.at[j])
+            wait(reg, o_rr.at[j], "o2")
             send(bot, bot, o_rel.at[1], o_rrr.at[j], left)
             send(reg, reg, o_rel.at[2], o_rs.at[j], sib)
 
@@ -161,9 +162,27 @@
             top = oall_ref.at[orow_half(j, 0), ocol(c_o, s)]
             bot = oall_ref.at[orow_half(j, 1), ocol(c_o, s)]
             reg = oall_ref.at[orow(j), ocol(c_o, s)]
-            wait(top, o_rlr.at[j])
-            wait(bot, o_rrr.at[j])
+            wait(top, o_rlr.at[j], "o3")
+            wait(bot, o_rrr.at[j], "o3")
             send(reg, reg, o_rel.at[2], o_rs.at[j], sib)
+
+    def unrolled(n, body):
+        for e in range(n):
+            body(e, 0)
+
+    def norm_rows(src, which):
+        def step(e, carry):
+            for q in range(NR // 16):
+                rows = pl.ds(al(e * NR + q * 16, 16), 16)
+                v32 = src[rows, :].astype(F32)
+                inv = lax.rsqrt(jnp.mean(v32 * v32, axis=1, keepdims=True) + EPS)
+                a_buf[rows, :] = (v32 * inv * g_scr[which]).astype(BF)
+            return carry
+
+        lax.fori_loop(0, b // NR, step, 0)
+
+    g_scr[0] = g1_ref[...].astype(F32).reshape(1, d)
+    g_scr[1] = g2_ref[...].astype(F32).reshape(1, d)
 
     scale = HEAD ** -0.5 * 1.4426950408889634
     for h in range(t // kvt):
@@ -178,72 +197,79 @@
         keys = pl.ds(al(j * kvt, kvt), kvt)
         kk = k_scr[keys, :]
         vv = v_scr[keys, :]
-        for h in range(hl):
-            sc = lax.dot_general(q_scr[h], kk, (((1,), (1,)), ((), ())), preferred_element_type=F32)
-            if masked:
-                rows = i * b + lax.broadcasted_iota(jnp.int32, (b, kvt), 0)
-                cols = j * kvt + lax.broadcasted_iota(jnp.int32, (b, kvt), 1)
-                sc = jnp.where(cols <= rows, sc, -jnp.inf)
-            m_prev = m_scr[h]
-            m_new = jnp.maximum(m_prev, jnp.max(sc, axis=1, keepdims=True))
-            parts = [jnp.exp2((sc[:, e * HEAD:(e + 1) * HEAD] - m_new) * scale) for e in range(kvt // HEAD)]
-            alpha = jnp.exp2((m_prev - m_new) * scale)
-            l_scr[h] = l_scr[h] * alpha + functools.reduce(lambda p, q: p + q, parts)
-            pr = jnp.concatenate([p.astype(BF) for p in parts], axis=1)
-            acc_scr[h] = acc_scr[h] * alpha + jnp.dot(pr, vv, preferred_element_type=F32)
-            m_scr[h] = m_new
+        sc = lax.dot_general(q_scr[...], kk, (((1,), (1,)), ((), ())), preferred_element_type=F32)
+        if masked:
+            rows = i * b + lax.broadcasted_iota(jnp.int32, (b, kvt), 0)
+            cols = j * kvt + lax.broadcasted_iota(jnp.int32, (b, kvt), 1)
+            keep = cols <= rows
+            sc = jnp.concatenate([jnp.where(keep, sc[h * b:(h + 1) * b], -jnp.inf) for h in range(hl)], axis=0)
+        m_prev = m_scr[...]
+        m_new = jnp.maximum(m_prev, jnp.max(sc, axis=1, keepdims=True))
+        parts = [jnp.exp2((sc[:, e * HEAD:(e + 1) * HEAD] - m_new) * scale) for e in range(kvt // HEAD)]
+        alpha = jnp.exp2((m_prev - m_new) * scale)
+        l_scr[...] = l_scr[...] * alpha + functools.reduce(lambda p, q: p + q, parts)
+        pr = jnp.concatenate([p.astype(BF) for p in parts], axis=1)
+        acc_scr[...] = acc_scr[...] * alpha + jnp.dot(pr, vv, preferred_element_type=F32)
+        m_scr[...] = m_new
 
     def phase1(i, carry):
+        with jax.named_scope("slot1"):
+            return phase1_slot(i, carry)
+
+    def phase1_slot(i, carry):
         slot = i % 2
-        wait(x_buf.at[slot], ld_x.at[slot])
-        wait(pos_buf.at[slot], ld_pos.at[slot])
+        wait(x_buf.at[slot], ld_x.at[slot], "x")
 
         @pl.when(i + 1 < nb)
         def _():
             put(x_ref.at[pl.ds(al((i + 1) * b, b), b)], x_buf.at[1 - slot], ld_x.at[1 - slot])
-            put(posf_ref.at[pl.ds(al((i + 1) * b, b), b)], pos_buf.at[1 - slot], ld_pos.at[1 - slot])
-
-        def norm(j, carry):
-            rows = pl.ds(al(j * 16, 16), 16)
-            v32 = x_buf[slot, rows, :].astype(F32)
-            inv = lax.rsqrt(jnp.mean(v32 * v32, axis=1, keepdims=True) + EPS)
-            a_buf[rows, :] = (v32 * inv * g1_ref[...].astype(F32)).astype(BF)
-            return carry
-
-        lax.fori_loop(0, b // 16, norm, 0)
-        co, si = _sincos(pos_buf[slot] * inv_ref[...])
+
+        with jax.named_scope("norm1"):
+            norm_rows(x_buf.at[slot], 0)
+        pcol = []
+        for e in range(b // 128):
+            prow = pos_ref[pl.ds(i * (b // 128) + e, 1), :].astype(F32)
+            pcol.append(jnp.transpose(jnp.broadcast_to(prow, (128, 128))))
+        co, si = _sincos(jnp.concatenate(pcol, axis=0) * inv_ref[...])
         si = jnp.where(lane < HEAD // 2, -si, si)
-        qkv = jnp.dot(a_buf[...], wqkv[...], preferred_element_type=F32)
+        q32 = jnp.dot(a_buf[...], wqkv[:, 0:qw + HEAD], preferred_element_type=F32)
+        v32 = jnp.dot(a_buf[...], wqkv[:, qw + HEAD:qw + 2 * HEAD], preferred_element_type=F32)
 
         def rope(v32):
             return (v32 * co + pltpu.roll(v32, HEAD // 2, 1) * si).astype(BF)
 
         rows = pl.ds(al(i * b, b), b)
         for h in range(hl):
-            q_scr[h] = rope(qkv[:, h * HEAD:(h + 1) * HEAD])
-        k_scr[rows, :] = rope(qkv[:, qw:qw + HEAD])
-        v_scr[rows, :] = qkv[:, qw + HEAD:qw + 2 * HEAD].astype(BF)
-        for h in range(hl):
-            m_scr[h] = jnp.full((b, HEAD), -jnp.inf, F32)
-            l_scr[h] = jnp.zeros((b, HEAD), F32)
-            acc_scr[h] = jnp.zeros((b, HEAD), F32)
+            q_scr[h * b:(h + 1) * b, :] = rope(q32[:, h * HEAD:(h + 1) * HEAD])
+        k_scr[rows, :] = rope(q32[:, qw:qw + HEAD])
+        v_scr[rows, :] = v32.astype(BF)
+        m_scr[...] = jnp.full((hl * b, HEAD), -jnp.inf, F32)
+        l_scr[...] = jnp.zeros((hl * b, HEAD), F32)
+        acc_scr[...] = jnp.zeros((hl * b, HEAD), F32)
         last = (i * b) // kvt
 
         def inner(j, carry):
             tile(i, j, False)
             return carry
 
-        lax.fori_loop(0, last, inner, 0)
+        with jax.named_scope("tiles"):
+            lax.fori_loop(0, last, inner, 0)
         tile(i, last, True)
         for h in range(hl):
             o_buf[rows, h * HEAD:(h + 1) * HEAD] = (
-                acc_scr[h] / jnp.sum(l_scr[h], axis=1, keepdims=True)).astype(BF)
+                acc_scr[h * b:(h + 1) * b, :] / jnp.sum(l_scr[h * b:(h + 1) * b, :], axis=1, keepdims=True)).astype(BF)
         src = o_buf.at[rows]
         dst = oall_ref.at[orow(i), ocol(c, s)]
         send(src, dst, o_s.at[0], o_rl.at[i], right)
         send(src, dst, o_s.at[1], o_rr.at[i], left)
         send(src, dst, o_s.at[2], o_rs.at[i], sib)
         put(src, dst, o_s.at[3])
+
+        @pl.when(i == 1)
+        def _():
+            put(wg_ref, wg_v, ld_mlp.at[0])
+            put(wu_ref, wu_v, ld_mlp.at[1])
+            put(wd_ref, wd_v, ld_mlp.at[2])
 
         @pl.when(i == w2)
         def _():
@@ -265,15 +291,15 @@
     wait(wu_v, ld_mlp.at[1])
     wait(wd_v, ld_mlp.at[2])
     if share:
-        wait(wo_v.at[pl.ds(0, 3 * wr)], wo_z_r)
+        wait(wo_v.at[pl.ds(0, 3 * wr)], wo_z_r, "woz")
 
     def load_o(j):
-        wait(oall_ref.at[orow(j), pl.ds(0, 4 * qw)], o_rs.at[j])
+        wait(oall_ref.at[orow(j), pl.ds(0, 4 * qw)], o_rs.at[j], "os")
         put(oall_ref.at[orow(j)], o_blk, ld_o.at[0])
         put(x_ref.at[orow(j), pl.ds(mine, dh)], xh, ld_o.at[1])
 
     nt_h = min(512, dh)
-    nt_f = min(256, f)
+    nt_f = min(512, f)
     nt_d = min(512, d)
 
     def sum_start(j):
@@ -281,8 +307,8 @@
         def _():
             two = j % 2
             q4 = j % 4
-            wait(rsib.at[two], r_r.at[two])
-            wait(rsib.at[two], r_s)
+            wait(rsib.at[two], r_r.at[two], "r")
+            wait(rsib.at[two], r_s, "rs")
 
             def add(e, carry):
                 rows = pl.ds(al(e * 16, 16), 16)
@@ -290,7 +316,8 @@
                 cp[q4, rows, :] = (own.astype(F32) + rsib[two, rows, :].astype(F32)).astype(BF)
                 return carry
 
-            lax.fori_loop(0, hb // 16, add, 0)
+            with jax.named_scope("add"):
+                lax.fori_loop(0, hb // 16, add, 0)
 
             def part(chip, half):
                 return cp.at[q4, pl.ds(al(chip * ow + half * hw, hw), hw)]
@@ -304,16 +331,22 @@
         @pl.when(j < nb)
         def _():
             two = j % 2
-            wait(o_blk, ld_o.at[0])
-            wait(xh, ld_o.at[1])
+            wait(o_blk, ld_o.at[0], "ldo")
+            wait(xh, ld_o.at[1], "ldo")
 
             def col(n, carry):
-                cols = pl.ds(al(n * nt_h, nt_h), nt_h)
+                cols = pl.ds(n * nt_h, nt_h)
                 v32 = jnp.dot(o_blk[...], wo_v[:, cols], preferred_element_type=F32)
                 hbuf[two, :, pl.ds(al(s * dh + n * nt_h, 128), nt_h)] = (xh[:, cols].astype(F32) + v32).astype(BF)
                 return carry
 
-            lax.fori_loop(0, dh // nt_h, col, 0)
+            with jax.named_scope("own_h"):
+                unrolled(dh // nt_h, col)
+
+    def swap_h(j):
+        @pl.when(j < nb)
+        def _():
+            two = j % 2
             half = hbuf.at[two, :, pl.ds(mine, dh)]
             send(half, half, h_s.at[two], h_r.at[two], sib)
 
@@ -325,40 +358,36 @@
         @pl.when((j >= 0) & (j < nb))
         def _():
             two = j % 2
-            wait(hbuf.at[two, :, pl.ds(other, dh)], h_r.at[two])
-            wait(hbuf.at[two, :, pl.ds(mine, dh)], h_s.at[two])
-
-            def norm(e, carry):
-                rows = pl.ds(al(e * 16, 16), 16)
-                v32 = hbuf[two, rows, :].astype(F32)
-                inv = lax.rsqrt(jnp.mean(v32 * v32, axis=1, keepdims=True) + EPS)
-                a_buf[rows, :] = (v32 * inv * g2_ref[...].astype(F32)).astype(BF)
-                return carry
-
-            lax.fori_loop(0, b // 16, norm, 0)
+            wait(hbuf.at[two, :, pl.ds(other, dh)], h_r.at[two], "h")
+            wait(hbuf.at[two, :, pl.ds(mine, dh)], h_s.at[two], "hs")
+
+            with jax.named_scope("norm2"):
+                norm_rows(hbuf.at[two], 1)
             hst[j % 4] = hbuf[two, pl.ds(al(s * hb + c * ow, 16), ow), :]
 
     def mlp_up(j):
         @pl.when((j >= 0) & (j < nb))
         def _():
             def col(n, carry):
-                cols = pl.ds(al(n * nt_f, nt_f), nt_f)
+                cols = pl.ds(n * nt_f, nt_f)
                 gt = jnp.dot(a_buf[...], wg_v[:, cols], preferred_element_type=F32)
                 up = jnp.dot(a_buf[...], wu_v[:, cols], preferred_element_type=F32)
                 u_buf[:, cols] = (gt * (1.0 / (1.0 + jnp.exp(-gt))) * up).astype(BF)
                 return carry
 
-            lax.fori_loop(0, f // nt_f, col, 0)
+            with jax.named_scope("up"):
+                unrolled(f // nt_f, col)
 
     def mlp_down(j):
         @pl.when((j >= 0) & (j < nb))
         def _():
             def col(n, carry):
-                cols = pl.ds(al(n * nt_d, nt_d), nt_d)
+                cols = pl.ds(n * nt_d, nt_d)
                 r_buf[:, cols] = jnp.dot(u_buf[...], wd_v[:, cols], preferred_element_type=F32).astype(BF)
                 return carry
 
-            lax.fori_loop(0, d // nt_d, col, 0)
+            with jax.named_scope("down"):
+                unrolled(d // nt_d, col)
             send(r_buf.at[pl.ds(al((1 - s) * hb, hb), hb)], rsib.at[j % 2], r_s, r_r.at[j % 2], sib)
 
     def sum_relay(j):
@@ -371,10 +400,10 @@
                 wait(sums.at[q4, 0], s2_s.at[q4, 0])
                 wait(sums.at[q4, 1], s2_s.at[q4, 1])
 
-            wait(rs1.at[q4, 0], s1_r.at[q4, 0])
+            wait(rs1.at[q4, 0], s1_r.at[q4, 0], "s1")
             sums[q4, 0] = (rs1[q4, 0].astype(F32) + cp[q4, pl.ds(al(c_r * ow, 16), hw), :].astype(F32)).astype(BF)
             send(sums.at[q4, 0], rs2.at[q4, 0], s2_s.at[q4, 0], s2_r.at[q4, 0], right)
-            wait(rs1.at[q4, 2], s1_r.at[q4, 2])
+            wait(rs1.at[q4, 2], s1_r.at[q4, 2], "s1")
             sums[q4, 1] = (rs1[q4, 2].astype(F32) + cp[q4, pl.ds(al(c_l * ow + hw, 16), hw), :].astype(F32)).astype(BF)
             send(sums.at[q4, 1], rs2.at[q4, 1], s2_s.at[q4, 1], s2_r.at[q4, 1], left)
 
@@ -395,11 +424,11 @@
                     wait(ych.at[q4], y_s.at[q4, e])
 
             for e in range(4):
-                wait(rs1.at[q4, e], s1_s.at[q4, e])
-            wait(rs1.at[q4, 1], s1_r.at[q4, 1])
-            wait(rs1.at[q4, 3], s1_r.at[q4, 3])
-            wait(rs2.at[q4, 0], s2_r.at[q4, 0])
-            wait(rs2.at[q4, 1], s2_r.at[q4, 1])
+                wait(rs1.at[q4, e], s1_s.at[q4, e], "s1s")
+            wait(rs1.at[q4, 1], s1_r.at[q4, 1], "s2")
+            wait(rs1.at[q4, 3], s1_r.at[q4, 3], "s2")
+            wait(rs2.at[q4, 0], s2_r.at[q4, 0], "s2")
+            wait(rs2.at[q4, 1], s2_r.at[q4, 1], "s2")
             for half, (near, far) in enumerate(((3, 0), (1, 1))):
                 own = cp[q4, pl.ds(al(c * ow + half * hw, 16), hw), :].astype(F32)
                 tot = own + rs1[q4, near].astype(F32) + rs2[q4, far].astype(F32)
@@ -416,28 +445,33 @@
         def _():
             reg = yrow(j, s, c_l)
             top = yrow_half(j, s, c_l, 0)
-            wait(reg, y_rl.at[j])
+            wait(reg, y_rl.at[j], "y2")
             send(top, top, y_rel.at[0], y_rlr.at[j], right)
             send(reg, reg, y_rel.at[2], y_rs.at[j], sib)
             reg = yrow(j, s, c_r)
             bot = yrow_half(j, s, c_r, 1)
-            wait(reg, y_rr.at[j])
+            wait(reg, y_rr.at[j], "y2")
             send(bot, bot, y_rel.at[1], y_rrr.at[j], left)
             send(reg, reg, y_rel.at[2], y_rs.at[j], sib)
 
     def y_stage3(j):
         @pl.when((j >= 0) & (j < nb))
         def _():
-            wait(yrow_half(j, s, c_o, 0), y_rlr.at[j])
-            wait(yrow_half(j, s, c_o, 1), y_rrr.at[j])
+            wait(yrow_half(j, s, c_o, 0), y_rlr.at[j], "y3")
+            wait(yrow_half(j, s, c_o, 1), y_rrr.at[j], "y3")
             reg = yrow(j, s, c_o)
             send(reg, reg, y_rel.at[2], y_rs.at[j], sib)
 
     load_o(0)
 
     def phase2(i, carry):
+        with jax.named_scope("slot2"):
+            return phase2_slot(i, carry)
+
+    def phase2_slot(i, carry):
+        own_h(i)
         sum_start(i - 2)
-        own_h(i)
+        swap_h(i)
         mlp_norm(i - 1)
         sum_relay(i - 3)
         mlp_up(i - 1)
@@ -452,7 +486,7 @@
     lax.fori_loop(0, nb + 6, phase2, 0)
 
     def drain(j, carry):
-        wait(y_ref.at[pl.ds(0, hb)], y_rs.at[j])
+        wait(y_ref.at[pl.ds(0, hb)], y_rs.at[j], "ys")
         return carry
 
     lax.fori_loop(0, nb, drain, 0)
@@ -480,7 +514,7 @@
     wait(v_scr, kv_s.at[1])
 
 
-def _layer(tp, dp, x, posf, inv, g1, g2, wq, wk, wv, wo, wg, wu, wd):
+def _layer(tp, dp, x, pos, inv, g1, g2, wq, wk, wv, wo, wg, wu, wd):
     t, d = x.shape
     qw = wq.shape[1]
     f = wg.shape[1]
@@ -492,8 +526,8 @@
     ow = hb // nc
     hw = ow // 2
     assert nc == 4 and t % b == 0 and wk.shape[1] == tp * HEAD
-    l1 = max(1, nb * 3 // 8)
-    l2 = l1 + max(1, nb // 8)
+    l1 = min(nb * 3 // 8, nb - 3)
+    l2 = min(nb * 3 // 4, nb - 2)
     w2 = nb * 5 // 16
     w3 = nb * 9 // 16
     dma = pltpu.SemaphoreType.DMA
@@ -506,14 +540,14 @@
         pltpu.VMEM((d, f), BF),
         pltpu.VMEM((f, d), BF),
         pltpu.VMEM((2, b, d), BF),
-        pltpu.VMEM((2, b, HEAD), F32),
+        pltpu.VMEM((2, 1, d), F32),
         pltpu.VMEM((b, d), BF),
-        pltpu.VMEM((hl, b, HEAD), BF),
+        pltpu.VMEM((hl * b, HEAD), BF),
         pltpu.VMEM((t, HEAD), BF),
         pltpu.VMEM((t, HEAD), BF),
-        pltpu.VMEM((hl, b, HEAD), F32),
-        pltpu.VMEM((hl, b, HEAD), F32),
-        pltpu.VMEM((hl, b, HEAD), F32),
+        pltpu.VMEM((hl * b, HEAD), F32),
+        pltpu.VMEM((hl * b, HEAD), F32),
+        pltpu.VMEM((hl * b, HEAD), F32),
         pltpu.VMEM((t, qw), BF),
         pltpu.VMEM((b, tp * qw), BF),
         pltpu.VMEM((b, d // 2), BF),
@@ -527,7 +561,7 @@
         pltpu.VMEM((4, 2, hw, d), BF),
         pltpu.VMEM((4, ow, d), BF),
         pltpu.VMEM((4, ow, d), BF),
-        dma((3,)), dma((3,)), dma((2,)), dma((2,)), dma((2,)),
+        dma((3,)), dma((3,)), dma((2,)), dma((2,)),
         dma((7,)), dma((2,)), dma((2,)), dma(()), dma(()),
         dma((4,)), dma((nb,)), dma((nb,)), dma((nb,)), dma((nb,)), dma((nb,)), dma((3,)),
         dma((2,)), dma((2,)), dma((2,)), dma(()), dma((2,)), dma((4, 4)), dma((4, 4)), dma((4, 2)), dma((4, 2)),
@@ -543,13 +577,63 @@
             jax.ShapeDtypeStruct((t, HEAD), BF),
             jax.ShapeDtypeStruct((t, tp * qw), BF),
         ),
-        in_specs=[hbm, hbm, vm, vm, vm] + [hbm] * 7,
+        in_specs=[hbm, vm, vm, vm, vm] + [hbm] * 7,
         out_specs=(hbm, hbm, hbm, hbm),
         scratch_shapes=scratch,
         compiler_params=pltpu.CompilerParams(
             collective_id=0, has_side_effects=True, vmem_limit_bytes=66 * 1000 * 1000),
         cost_estimate=pl.CostEstimate(flops=flops, bytes_accessed=8 * t * d, transcendentals=t * t * hl),
-    )(x, posf, inv, g1, g2, wq, wk, wv, wo, wg, wu, wd)
+    )(x, pos, inv, g1, g2, wq, wk, wv, wo, wg, wu, wd)
+
+
+def _copy_kernel(src, k_src, v_src, dst, k_dst, v_dst, buf, kv, rd, wr, kv_sem):
+    n, rows = buf.shape[0], buf.shape[1]
+    steps = src.shape[0] // rows
+
+    def read(i):
+        return pltpu.make_async_copy(src.at[pl.ds(i * rows, rows)], buf.at[i % n], rd.at[i % n])
+
+    def write(i):
+        return pltpu.make_async_copy(buf.at[i % n], dst.at[pl.ds(i * rows, rows)], wr.at[i % n])
+
+    small = [(k_src, k_dst), (v_src, v_dst)]
+    kv_in = [pltpu.make_async_copy(a, kv.at[e], kv_sem.at[e]) for e, (a, _) in enumerate(small)]
+    kv_out = [pltpu.make_async_copy(kv.at[e], z, kv_sem.at[e]) for e, (_, z) in enumerate(small)]
+    for i in range(min(n, steps)):
+        read(i).start()
+    for e in range(2):
+        kv_in[e].start()
+    for i in range(steps):
+        read(i).wait()
+        write(i).start()
+        if i >= 1 and i - 1 + n < steps:
+            write(i - 1).wait()
+            read(i - 1 + n).start()
+    for e in range(2):
+        kv_in[e].wait()
+        kv_out[e].start()
+    for i in range(max(0, steps - n), steps):
+        write(i).wait()
+    for e in range(2):
+        kv_out[e].wait()
+
+
+def _copy(y, k, v):
+    t, d = y.shape
+    rows, n = min(256, t), min(16, t // 256)
+    hbm = pl.BlockSpec(memory_space=pl.ANY)
+    dma = pltpu.SemaphoreType.DMA
+    return pl.pallas_call(
+        _copy_kernel,
+        name="copy_out",
+        out_shape=tuple(jax.ShapeDtypeStruct(a.shape, a.dtype) for a in (y, k, v)),
+        in_specs=[hbm] * 3,
+        out_specs=(hbm,) * 3,
+        scratch_shapes=[pltpu.VMEM((n, rows, d), y.dtype), pltpu.VMEM((2,) + k.shape, k.dtype),
+                        dma((n,)), dma((n,)), dma((2,))],
+        compiler_params=pltpu.CompilerParams(vmem_limit_bytes=66 * 1000 * 1000),
+        cost_estimate=pl.CostEstimate(flops=0, bytes_accessed=4 * t * d, transcendentals=0),
+    )(y, k, v)
 
 
 def solution(mesh):
@@ -558,11 +642,10 @@
 
     def local(x, pos, g1, g2, wq, wk, wv, wo, wg, wu, wd):
         t, d = x.shape
-        half = HEAD // 2
-        inv = ROPE_BASE ** (-2.0 * jnp.arange(half, dtype=F32) / HEAD)
-        inv = jnp.concatenate([inv, inv])[None, :]
-        posf = jnp.broadcast_to(pos.astype(F32)[:, None], (t, HEAD))
-        y, k, v, _ = _layer(tp, dp, x, posf, inv, g1[None, :], g2[None, :], wq, wk, wv, wo, wg, wu, wd)
+        half = ROPE_BASE ** (-2.0 * np.arange(HEAD // 2) / HEAD)
+        inv = jnp.asarray(np.concatenate([half, half])[None, :].astype(np.float32))
+        y, k, v, _ = _layer(tp, dp, x, pos.reshape(t // 128, 128), inv, g1, g2, wq, wk, wv, wo, wg, wu, wd)
+        y, k, v = _copy(y, k, v)
         return y, k.reshape(t, 1, HEAD), v.reshape(t, 1, HEAD)
 
     return jax.shard_map(

time: 465 us -> 378 us (0.81)
  Pallas kernels: 435 us -> 377 us
  local copies, waits for them, and re-layouts: 27.3 us -> 0 us
    pallas_call x1, Pallas kernels: 435 us -> 359 us  [_layer(): pl.pallas_call(functools.partial(_kernel, tp, dp, l1, l2, w2, w3), name='...]
    unnamed x7 -> x0, local copies, waits for them, and re-layouts: 22.8 us -> none
    pallas_call x0 -> x1, Pallas kernels: none -> 18.8 us  [_copy(): pl.pallas_call(_copy_kernel, name='copy_out', out_shape=tuple((jax.ShapeD...]
where the time goes in v2:
time: 378 us
  Pallas kernels  377 us (100%)
    pallas_call x1, Pallas kernels, _layer(): pl.pallas_call(functools.partial(_kernel, tp, dp, l1, l2, w2, w3), name='...  359 us
    pallas_call x1, Pallas kernels, _copy(): pl.pallas_call(_copy_kernel, name='copy_out', out_shape=tuple((jax.ShapeD...  18.8 us

profile of v2, /device:TPU:81, one launch (start us, length us, event | category | flops | bytes accessed | tf_op | source)
XLA Modules:
  0.0 378.0 jit_solution(4464571695750856734)
XLA Ops:
  0.6 358.5 %layer.1 = (bf16[4096,3072]{1,0:T(8,128)(2,1)}, bf16[4096,128]{1,0:T(8,128)(2,1)}, bf16[4096,128]{1,0:T(8,128)(2,1)}, bf16[4096,3072]{1,0:T(8,128)(2,1)}) custom-call(bf16[4096,3072]{1,0:T(8,128)(2,1)} %x_ref.1, s32[32,128]{1,0:T(8,128)} %bitcast.5, f32[1,128]{1,0:T(1,128)} %constant.2.clone.inv_ref, bf16[3072]{0:T(1024)(128)(2,1)} %g1_ref.1, ...), custom_call_target="tpu_custom_call" | custom-call | flops 144955146240 | bytes 100663296 | tf_op jit(solution)/shard_map/layer/pallas_call | solution.py:571
  359.2 18.8 %copy_out.1 = (bf16[4096,3072]{1,0:T(8,128)(2,1)}, bf16[4096,128]{1,0:T(8,128)(2,1)}, bf16[4096,128]{1,0:T(8,128)(2,1)}) custom-call(bf16[4096,3072]{1,0:T(8,128)(2,1)} %get-tuple-element.9.src, bf16[4096,128]{1,0:T(8,128)(2,1)} %get-tuple-element.10.k_src, bf16[4096,128]{1,0:T(8,128)(2,1)} %get-tuple-element.11.v_src), custom_call_target="tpu_custom_call" | custom-call | bytes 50331648 | tf_op jit(solution)/shard_map/copy_out/pallas_call | solution.py:626

commit v3 on v0

v3 whole, which is shorter than its diff:
```python
import functools

import jax
import jax.numpy as jnp
import numpy as np
from jax import lax
from jax.experimental import pallas as pl
from jax.experimental.pallas import tpu as pltpu
from jax.sharding import PartitionSpec as P

HEAD = 128
LANES = 128
SUB = 16
EPS = 1e-5
ROPE_BASE = 500000.0
MESH = pl.DeviceIdType.MESH
BLOCK = 256
NR = 64
SLOTS = 4
SIDES = (0, 1)
BF = jnp.bfloat16
F32 = jnp.float32
VMEM_BYTES = 66000000
TWO_OVER_PI = 0.6366197723675814
PI_2 = (1.5703125, 4.837512969970703125e-4, 7.54978995489188216e-8)
SIN = (-1.9515295891e-4, 8.3321608736e-3, -1.6666654611e-1)
COS = (2.443315711809948e-5, -1.388731625493765e-3, 4.166664568298827e-2)
LOG2E = 1.4426950408889634


def _sincos(ang):
    n = jnp.floor(ang * TWO_OVER_PI + 0.5)
    r = ang
    for p in PI_2:
        r = r - n * p
    z = r * r
    s = functools.reduce(lambda a, p: a * z + p, SIN[1:], SIN[0]) * z * r + r
    c = functools.reduce(lambda a, p: a * z + p, COS[1:], COS[0]) * z * z - 0.5 * z + 1.0
    m = n.astype(jnp.int32)
    odd = (m & 1) == 1
    cs = jnp.where(odd, s, c)
    sn = jnp.where(odd, c, s)
    return jnp.where(((m + 1) & 2) == 2, -cs, cs), jnp.where((m & 2) == 2, -sn, sn)


def _al(v, m):
    return pl.multiple_of(v, m)


def _first(ref, n):
    return ref.at[pl.ds(0, n)]


def _kernel(tp, dp, zn, l1, l2, w2, w3, w4,
            x_ref, pos_ref, inv_ref, g1_ref, g2_ref, wq_ref, wk_ref, wv_ref, wo_ref, wg_ref, wu_ref, wd_ref,
            y_ref, k_ref, v_ref, oall_ref,
            pos_v, inv_v, g1_v, g2_v, wqkv, wo_v, wg_v, wu_v, wd_v, x_buf, g_scr, a_buf, q_scr, k_scr, v_scr, m_scr, l_scr, acc_scr, o_buf,
            o_blk, xh, hbuf, u_buf, r_buf, rsib, cp, rs_far, rs_near, rs_sum, sums, ych, hst,
            ld_s, ld_w, ld_mlp, ld_x, kv_s,
            wo_d, wo_s, wo_r, wo_fs, wo_fr, wo_ps, wo_pr,
            o_s, o_sx, o_r, o_f, o_rs, o_rel, o_fwd,
            ld_o, h_s, h_r, r_s, r_r, far_s, far_r, near_s, near_r, sum_s, sum_r,
            y_s, y_sx, y_r, y_f, y_rs, y_rel, y_fwd):
    t, d = x_ref.shape
    qw = wq_ref.shape[1]
    f = wg_ref.shape[1]
    hl = qw // HEAD
    b = BLOCK
    nb = t // b
    dh = d // 2
    hb = b // 2
    nc = tp // 2
    ow = hb // nc
    hw = ow // 2
    kvt = 2 * b

    r = lax.axis_index("tp")
    c = r // 2
    s = r % 2
    c_r = (c + 1) % nc
    c_l = (c + nc - 1) % nc
    c_o = (c + 2) % nc
    dest = ({"tp": c_r * 2 + s}, {"tp": c_l * 2 + s})
    origin = (c_l, c_r)
    target = (c_r, c_l)
    sib = {"tp": c * 2 + 1 - s}
    dpi = lax.axis_index("dp")
    par = dpi % 2
    peers = [{"dp": dpi + 1 - 2 * par}] if dp % 2 == 0 else []
    if zn:
        par_y = (dpi // zn) % 2
        peers.append({"dp": dpi + zn * (1 - 2 * par_y)})

    def send(src, dst, ss, rs, dev):
        pltpu.make_async_remote_copy(
            src_ref=src, dst_ref=dst, send_sem=ss, recv_sem=rs, device_id=dev, device_id_type=MESH).start()

    def put(src, dst, sem):
        pltpu.make_async_copy(src, dst, sem).start()

    def wait(region, sem, tag=None):
        with jax.named_scope("w_" + (tag or "end")):
            pltpu.make_async_copy(region, region, sem).wait()

    def when_block(j, body):
        @pl.when((j >= 0) & (j < nb))
        def _():
            body()

    barrier = pltpu.get_barrier_semaphore()
    cross = [{"tp": target[e] * 2 + 1 - s} for e in SIDES]
    others = [*dest, *cross, sib, *peers]
    for dev in others:
        pl.semaphore_signal(barrier, inc=1, device_id=dev, device_id_type=MESH)

    rk = _al(r * HEAD, HEAD)
    wq_dst = wqkv.at[:, pl.ds(0, qw)]
    kv_dst = [wqkv.at[:, pl.ds(qw + e * HEAD, HEAD)] for e in SIDES]
    small = ((pos_ref, pos_v), (inv_ref, inv_v), (g1_ref, g1_v), (g2_ref, g2_v))
    put(_first(x_ref, b), x_buf.at[0], ld_x.at[0])
    for e, (src, dst) in enumerate(small):
        put(src, dst, ld_s.at[e])
    put(wq_ref, wq_dst, ld_w.at[2])
    for e, ref in enumerate((wk_ref, wv_ref)):
        put(ref.at[:, pl.ds(rk, HEAD)], kv_dst[e], ld_w.at[e])
    with jax.named_scope("barrier"):
        pl.semaphore_wait(barrier, len(others))

    mine = _al(s * dh, LANES)
    other = _al((1 - s) * dh, LANES)
    parts = 4 if zn else len(peers) + 1
    wr = qw // parts
    part = (2 * par_y + par) if zn else (par if peers else 0)

    def shard(dev):
        return wo_v.at[pl.ds(_al(dev * qw, LANES), qw)]

    def piece(chip, core, q=None):
        return wo_v.at[pl.ds(_al((chip * 2 + core) * qw + (part if q is None else q) * wr, 32), wr)]

    rows = pl.ds(_al(part * wr, 32), wr)
    for e in SIDES:
        for k, (cols, dev) in enumerate(((mine, dest[e]), (other, cross[e]))):
            send(wo_ref.at[rows, pl.ds(cols, dh)], piece(c, s), wo_s.at[e, k], wo_r.at[e, s], dev)
    send(wo_ref.at[:, pl.ds(other, dh)], shard(r), wo_d.at[0], wo_d.at[1], sib)
    put(wo_ref.at[:, pl.ds(mine, dh)], shard(r), wo_d.at[2])

    def wo_swap(chip):
        for e, dev in enumerate(peers):
            for core in SIDES:
                send(piece(chip, core), piece(chip, core), wo_ps.at[0, e], wo_pr.at[0, e], dev)

    def wo_stage2():
        for e in SIDES:
            for core in SIDES:
                wait(piece(origin[e], core), wo_r.at[e, core], "wo2")
            reg = piece(origin[e], e)
            send(reg, reg, wo_fs.at[e], wo_fr.at[e], dest[e])
            wo_swap(origin[e])

    def wo_stage3():
        for e in SIDES:
            wait(piece(c_o, e), wo_fr.at[e], "wo3")
        wo_swap(c_o)

    def wo_stage4():
        for e in range(len(peers)):
            wait(_first(wo_v, 6 * wr), wo_pr.at[0, e], "wo4")
        if zn:
            for chip in (*origin, c_o):
                for e, q in enumerate((2 * (1 - par_y) + par, 2 * par_y + 1 - par)):
                    reg = piece(chip, e, q)
                    send(reg, reg, wo_ps.at[1, e], wo_pr.at[1, e], peers[e])

    def wo_end(which):
        for e in SIDES if zn else ():
            wait(_first(wo_v, 3 * wr), which.at[1, e], "wo5")

    def ocol(chip, core):
        return pl.ds(_al((chip * 2 + core) * qw, LANES), qw)

    def oreg(j, chip):
        return oall_ref.at[pl.ds(_al(j * b, b), b), ocol(chip, s)]

    def ohalf(j, chip, half):
        return oall_ref.at[pl.ds(_al(j * b + half * hb, hb), hb), ocol(chip, s)]

    def orow(j):
        return pl.ds(_al(j * b, b), b)

    def o_stage2(j):
        def body():
            for e in SIDES:
                reg = oreg(j, origin[e])
                wait(reg, o_r.at[e, j], "o2")
                half = ohalf(j, origin[e], e)
                send(half, half, o_rel.at[e], o_f.at[e, j], dest[e])
                send(reg, reg, o_fwd, o_rs.at[j], sib)

        when_block(j, body)

    def o_stage3(j):
        def body():
            for e in SIDES:
                wait(ohalf(j, c_o, e), o_f.at[e, j], "o3")
            send(oreg(j, c_o), oreg(j, c_o), o_fwd, o_rs.at[j], sib)

        when_block(j, body)

    def unrolled(n, body):
        for e in range(n):
            body(e)

    def norm_rows(src, which):
        def step(e, carry):
            for q in range(NR // SUB):
                rows = pl.ds(_al(e * NR + q * SUB, SUB), SUB)
                v32 = src[rows, :].astype(F32)
                inv = lax.rsqrt(jnp.mean(v32 * v32, axis=1, keepdims=True) + EPS)
                a_buf[rows, :] = (v32 * inv * g_scr[which]).astype(BF)
            return carry

        with jax.named_scope("norm"):
            lax.fori_loop(0, b // NR, step, 0)

    for e, (src, dst) in enumerate(small):
        wait(dst, ld_s.at[e], "small")
    for e, ref in enumerate((g1_v, g2_v)):
        g_scr[e] = ref[...].astype(F32).reshape(1, d)

    scale = HEAD ** -0.5 * LOG2E
    lane = lax.broadcasted_iota(jnp.int32, (b, HEAD), 1)

    def heads(ref, h):
        return ref.at[pl.ds(h * b, b)]

    def tile(first, n, masked=False):
        keys = pl.ds(_al(first, n), n)
        kk = k_scr[keys, :]
        vv = v_scr[keys, :]
        sc = lax.dot_general(q_scr[...], kk, (((1,), (1,)), ((), ())), preferred_element_type=F32)
        if masked:
            keep = lax.broadcasted_iota(jnp.int32, (b, n), 1) <= lax.broadcasted_iota(jnp.int32, (b, n), 0)
            sc = jnp.concatenate([jnp.where(keep, sc[h * b:(h + 1) * b], -jnp.inf) for h in range(hl)], axis=0)
        m_prev = m_scr[...]
        m_new = jnp.maximum(m_prev, jnp.max(sc, axis=1, keepdims=True))
        ps = [jnp.exp2((sc[:, e * HEAD:(e + 1) * HEAD] - m_new) * scale) for e in range(n // HEAD)]
        alpha = jnp.exp2((m_prev - m_new) * scale)
        l_scr[...] = l_scr[...] * alpha + functools.reduce(lambda p, q: p + q, ps)
        pr = jnp.concatenate([p.astype(BF) for p in ps], axis=1)
        acc_scr[...] = acc_scr[...] * alpha + jnp.dot(pr, vv, preferred_element_type=F32)
        m_scr[...] = m_new

    def phase1(i, carry):
        with jax.named_scope("slot1"):
            phase1_slot(i)
        return carry

    def phase1_slot(i):
        slot = i % 2
        wait(x_buf.at[slot], ld_x.at[slot], "x")

        @pl.when(i + 1 < nb)
        def _():
            put(x_ref.at[pl.ds(_al((i + 1) * b, b), b)], x_buf.at[1 - slot], ld_x.at[1 - slot])

        norm_rows(x_buf.at[slot], 0)

        @pl.when(i == 0)
        def _():
            wait(wq_dst, ld_w.at[2], "w")
            for e in SIDES:
                wait(kv_dst[e], ld_w.at[e], "w")

        for e, (src, dst) in enumerate(((wg_ref, wg_v), (wu_ref, wu_v), (wd_ref, wd_v))):
            @pl.when(i == w2 + e)
            def _(src=src, dst=dst, e=e):
                put(src, dst, ld_mlp.at[e])

        pcol = []
        for e in range(b // LANES):
            prow = pos_v[pl.ds(i * (b // LANES) + e, 1), :].astype(F32)
            pcol.append(jnp.transpose(jnp.broadcast_to(prow, (LANES, LANES))))
        co, si = _sincos(jnp.concatenate(pcol, axis=0) * inv_v[...])
        si = jnp.where(lane < HEAD // 2, -si, si)
        qk32 = jnp.dot(a_buf[...], wqkv[:, :qw + HEAD], preferred_element_type=F32)
        v32 = jnp.dot(a_buf[...], wqkv[:, qw + HEAD:], preferred_element_type=F32)
        rows = pl.ds(_al(i * b, b), b)
        for h in range(hl + 1):
            head = qk32[:, h * HEAD:(h + 1) * HEAD]
            head = (head * co + pltpu.roll(head, HEAD // 2, 1) * si).astype(BF)
            if h < hl:
                heads(q_scr, h)[...] = head
            else:
                k_scr[rows, :] = head
        v_scr[rows, :] = v32.astype(BF)
        m_scr[...] = jnp.full(m_scr.shape, -jnp.inf, F32)
        l_scr[...] = jnp.zeros(l_scr.shape, F32)
        acc_scr[...] = jnp.zeros(acc_scr.shape, F32)
        full = i // 2

        def inner(j, carry):
            for e in SIDES:
                tile((2 * j + e) * kvt, kvt)
            return carry

        with jax.named_scope("tiles"):
            lax.fori_loop(0, full // 2, inner, 0)

        @pl.when(full % 2 == 1)
        def _():
            tile((full - 1) * kvt, kvt)

        @pl.when(i % 2 == 1)
        def _():
            tile((i - 1) * b, b)

        tile(i * b, b, masked=True)
        for h in range(hl):
            o_buf[rows, h * HEAD:(h + 1) * HEAD] = (
                heads(acc_scr, h)[...] / jnp.sum(heads(l_scr, h)[...], axis=1, keepdims=True)).astype(BF)
        src = o_buf.at[rows]
        dst = oreg(i, c)
        for e in SIDES:
            send(src, dst, o_s.at[e], o_r.at[e, i], dest[e])
        send(src, dst, o_sx.at[0], o_rs.at[i], sib)
        put(src, dst, o_sx.at[1])
        for when, stage in ((w2, wo_stage2), (w3, wo_stage3), (w4, wo_stage4)):
            pl.when(i == when)(stage)
        o_stage2(i - l1)
        o_stage3(i - l2)

    lax.fori_loop(0, nb, phase1, 0)
    for e, (src, dst) in enumerate(((k_scr, k_ref), (v_scr, v_ref))):
        put(src, dst, kv_s.at[e])
    wait(o_buf, o_sx.at[1])
    for e, dst in enumerate((wg_v, wu_v, wd_v)):
        wait(dst, ld_mlp.at[e])
    wait(shard(r + 1 - 2 * s), wo_d.at[1])
    wait(shard(r), wo_d.at[2])
    wo_end(wo_pr)

    def load_o(j):
        wait(oall_ref.at[orow(j), pl.ds(0, 4 * qw)], o_rs.at[j], "os")
        put(oall_ref.at[orow(j)], o_blk, ld_o.at[0])
        put(x_ref.at[orow(j), pl.ds(mine, dh)], xh, ld_o.at[1])

    nt_h = min(512, dh)
    nt_f = min(512, f)
    nt_d = min(512, d)

    def cpart(q4, chip, half):
        return cp.at[q4, pl.ds(_al(chip * ow + half * hw, hw), hw)]

    def sum_start(j):
        def body():
            two = j % 2
            q4 = j % SLOTS
            wait(rsib.at[two], r_r.at[two], "r")
            wait(rsib.at[two], r_s, "rs")

            def add(e, carry):
                rows = pl.ds(_al(e * SUB, SUB), SUB)
                own = r_buf[pl.ds(_al(s * hb + e * SUB, SUB), SUB), :]
                cp[q4, rows, :] = (own.astype(F32) + rsib[two, rows, :].astype(F32)).astype(BF)
                return carry

            with jax.named_scope("add"):
                lax.fori_loop(0, hb // SUB, add, 0)
            for e in SIDES:
                send(cpart(q4, c_o, e), rs_far.at[q4, e], far_s.at[q4, e], far_r.at[q4, e], dest[e])
            for e in SIDES:
                send(cpart(q4, target[e], 1 - e), rs_near.at[q4, e], near_s.at[q4, e], near_r.at[q4, e], dest[e])

        when_block(j, body)

    def own_h(j):
        @pl.when(j < nb)
        def _():
            wait(o_blk, ld_o.at[0], "ldo")
            wait(xh, ld_o.at[1], "ldo")

            def col(n):
                cols = pl.ds(n * nt_h, nt_h)
                v32 = jnp.dot(o_blk[...], wo_v[:, cols], preferred_element_type=F32)
                hbuf[j % 2, :, pl.ds(_al(s * dh + n * nt_h, LANES), nt_h)] = (xh[:, cols].astype(F32) + v32).astype(BF)

            with jax.named_scope("own_h"):
                unrolled(dh // nt_h, col)

    def swap_h(j):
        @pl.when(j < nb)
        def _():
            half = hbuf.at[j % 2, :, pl.ds(mine, dh)]
            send(half, half, h_s.at[j % 2], h_r.at[j % 2], sib)

        @pl.when(j + 1 < nb)
        def _():
            load_o(j + 1)

    def mlp_norm(j):
        def body():
            two = j % 2
            wait(hbuf.at[two, :, pl.ds(other, dh)], h_r.at[two], "h")
            wait(hbuf.at[two, :, pl.ds(mine, dh)], h_s.at[two], "hs")
            norm_rows(hbuf.at[two], 1)
            hst[j % SLOTS] = hbuf[two, pl.ds(_al(s * hb + c * ow, SUB), ow), :]

        when_block(j, body)

    def mlp_up(j):
        def body():
            def col(n):
                cols = pl.ds(n * nt_f, nt_f)
                gt = jnp.dot(a_buf[...], wg_v[:, cols], preferred_element_type=F32)
                up = jnp.dot(a_buf[...], wu_v[:, cols], preferred_element_type=F32)
                u_buf[:, cols] = (gt * (1.0 / (1.0 + jnp.exp(-gt))) * up).astype(BF)

            with jax.named_scope("up"):
                unrolled(f // nt_f, col)

        when_block(j, body)

    def mlp_down(j):
        def body():
            def col(n):
                cols = pl.ds(n * nt_d, nt_d)
                r_buf[:, cols] = jnp.dot(u_buf[...], wd_v[:, cols], preferred_element_type=F32).astype(BF)

            with jax.named_scope("down"):
                unrolled(d // nt_d, col)
            send(r_buf.at[pl.ds(_al((1 - s) * hb, hb), hb)], rsib.at[j % 2], r_s, r_r.at[j % 2], sib)

        when_block(j, body)

    def sum_relay(j):
        def body():
            q4 = j % SLOTS
            for e in SIDES:
                @pl.when(j >= SLOTS)
                def _():
                    wait(sums.at[q4, e], sum_s.at[q4, e], "sums")

                wait(rs_far.at[q4, e], far_r.at[q4, e], "s1")
                sums[q4, e] = (rs_far[q4, e].astype(F32) + cpart(q4, target[e], e)[...].astype(F32)).astype(BF)
                send(sums.at[q4, e], rs_sum.at[q4, e], sum_s.at[q4, e], sum_r.at[q4, e], dest[e])

        when_block(j, body)

    def yrow(j, chip):
        return y_ref.at[pl.ds(_al(j * b + s * hb + chip * ow, ow), ow)]

    def yhalf(j, chip, half):
        return y_ref.at[pl.ds(_al(j * b + s * hb + chip * ow + half * hw, hw), hw)]

    def y_sent(q4):
        for e in SIDES:
            wait(ych.at[q4], y_s.at[q4, e], "ysent")
            wait(ych.at[q4], y_sx.at[q4, e], "ysent")

    def sum_end(j):
        def body():
            q4 = j % SLOTS

            @pl.when(j >= SLOTS)
            def _():
                y_sent(q4)

            for e in SIDES:
                wait(rs_far.at[q4, e], far_s.at[q4, e], "s1s")
                wait(rs_near.at[q4, e], near_s.at[q4, e], "s1s")
                wait(rs_near.at[q4, e], near_r.at[q4, e], "s2")
                wait(rs_sum.at[q4, e], sum_r.at[q4, e], "s2")
            for e in SIDES:
                rows = pl.ds(e * hw, hw)
                tot = cpart(q4, c, e)[...].astype(F32) + rs_near[q4, 1 - e].astype(F32) + rs_sum[q4, e].astype(F32)
                ych[q4, rows, :] = (hst[q4, rows, :].astype(F32) + tot).astype(BF)
            for e in SIDES:
                send(ych.at[q4], yrow(j, c), y_s.at[q4, e], y_r.at[e, j], dest[e])
            send(ych.at[q4], yrow(j, c), y_sx.at[q4, 0], y_rs.at[j], sib)
            put(ych.at[q4], yrow(j, c), y_sx.at[q4, 1])

        when_block(j, body)

    def y_stage2(j):
        def body():
            for e in SIDES:
                reg = yrow(j, origin[e])
                wait(reg, y_r.at[e, j], "y2")
                half = yhalf(j, origin[e], e)
                send(half, half, y_rel.at[e], y_f.at[e, j], dest[e])
                send(reg, reg, y_fwd, y_rs.at[j], sib)

        when_block(j, body)

    def y_stage3(j):
        def body():
            for e in SIDES:
                wait(yhalf(j, c_o, e), y_f.at[e, j], "y3")
            send(yrow(j, c_o), yrow(j, c_o), y_fwd, y_rs.at[j], sib)

        when_block(j, body)

    load_o(0)

    def phase2(i, carry):
        with jax.named_scope("slot2"):
            own_h(i)
            sum_start(i - 2)
            swap_h(i)
            mlp_norm(i - 1)
            sum_relay(i - 3)
            mlp_up(i - 1)
            sum_end(i - 4)
            mlp_down(i - 1)
            y_stage2(i - 5)
            y_stage3(i - 6)
            o_stage2(nb + i - l1)
            o_stage3(nb + i - l2)
        return carry

    lax.fori_loop(0, nb + 6, phase2, 0)

    def drain(j, carry):
        wait(_first(y_ref, hb), y_rs.at[j])
        return carry

    lax.fori_loop(0, nb, drain, 0)
    for q4 in range(SLOTS):
        y_sent(q4)
        for e in SIDES:
            wait(sums.at[q4, e], sum_s.at[q4, e])
    for e in SIDES:
        wait(_first(y_ref, nb * hw), y_rel.at[e])
        wait(o_buf, o_s.at[e])
        wait(oall_ref.at[pl.ds(0, t // 2), pl.ds(0, qw)], o_rel.at[e])
        wait(_first(wo_v, wr), wo_fs.at[e])
        for k in SIDES:
            wait(_first(wo_v, wr), wo_s.at[e, k])
    wait(_first(y_ref, nb * ow * 3), y_fwd)
    wait(o_buf, o_sx.at[0])
    wait(oall_ref.at[:, pl.ds(0, 3 * qw)], o_fwd)
    wait(_first(wo_v, qw), wo_d.at[0])
    for e in range(len(peers)):
        wait(_first(wo_v, 6 * wr), wo_ps.at[0, e])
    wo_end(wo_ps)
    for e, src in enumerate((k_scr, v_scr)):
        wait(src, kv_s.at[e])


def _layer(tp, dp, zn, x, pos, inv, g1, g2, wq, wk, wv, wo, wg, wu, wd):
    t, d = x.shape
    qw = wq.shape[1]
    f = wg.shape[1]
    hl = qw // HEAD
    b = BLOCK
    nb = t // b
    hb = b // 2
    nc = tp // 2
    ow = hb // nc
    hw = ow // 2
    dh = d // 2
    assert nc == SLOTS and t % b == 0 and wk.shape[1] == tp * HEAD
    l1 = max(nb // 4, 1)
    l2 = min(nb * 3 // 4, nb - 2)
    hbm = pl.BlockSpec(memory_space=pl.ANY)
    bufs = [
        (d, qw + 2 * HEAD), (tp * qw, dh), (d, f), (d, f), (f, d), (2, b, d), None, (b, d),
        (hl * b, HEAD), (t, HEAD), (t, HEAD), None, None, None, (t, qw),
        (b, tp * qw), (b, dh), (2, b, d), (b, f), (b, d), (2, hb, d), (SLOTS, hb, d),
        (SLOTS, 2, hw, d), (SLOTS, 2, hw, d), (SLOTS, 2, hw, d), (SLOTS, 2, hw, d), (SLOTS, ow, d), (SLOTS, ow, d),
    ]
    wide = iter([(2, 1, d)] + [(hl * b, HEAD)] * 3)
    scratch = [pltpu.VMEM(a.shape, a.dtype) for a in (pos, inv, g1, g2)]
    scratch += [pltpu.VMEM(next(wide), F32) if shape is None else pltpu.VMEM(shape, BF) for shape in bufs]
    two, four, ring, per = (2,), (SLOTS, 2), (2, nb), (nb,)
    sems = [(4,), (3,), (3,), two, two,
            (3,), (2, 2), (2, 2), two, two, (2, 2), (2, 2),
            two, two, ring, ring, per, two, (),
            two, two, two, (), two, four, four, four, four, four, four,
            four, four, ring, ring, per, two, ()]
    scratch += [pltpu.SemaphoreType.DMA(shape) for shape in sems]
    flops = 2 * t * (d * (qw + 2 * HEAD) + qw * t + tp * qw * dh + 3 * d * f)
    outs = [(t, d), (t, HEAD), (t, HEAD), (t, tp * qw)]
    return pl.pallas_call(
        functools.partial(_kernel, tp, dp, zn, l1, l2, nb // 4, nb // 2, nb * 3 // 4),
        name="layer",
        out_shape=tuple(jax.ShapeDtypeStruct(shape, BF) for shape in outs),
        in_specs=[hbm] * 12,
        out_specs=(hbm,) * len(outs),
        scratch_shapes=scratch,
        compiler_params=pltpu.CompilerParams(collective_id=0, has_side_effects=True, vmem_limit_bytes=VMEM_BYTES),
        cost_estimate=pl.CostEstimate(flops=flops, bytes_accessed=8 * t * d, transcendentals=t * t * hl),
    )(x, pos, inv, g1, g2, wq, wk, wv, wo, wg, wu, wd)


def _copy_kernel(src, k_src, v_src, dst, k_dst, v_dst, buf, kv, rd, wr, kv_sem):
    n, rows = buf.shape[0], buf.shape[1]
    steps = src.shape[0] // rows

    def read(i):
        return pltpu.make_async_copy(src.at[pl.ds(i * rows, rows)], buf.at[i % n], rd.at[i % n])

    def write(i):
        return pltpu.make_async_copy(buf.at[i % n], dst.at[pl.ds(i * rows, rows)], wr.at[i % n])

    small = ((k_src, k_dst), (v_src, v_dst))
    kv_in = [pltpu.make_async_copy(a, kv.at[e], kv_sem.at[e]) for e, (a, _) in enumerate(small)]
    kv_out = [pltpu.make_async_copy(kv.at[e], z, kv_sem.at[e]) for e, (_, z) in enumerate(small)]
    for i in range(min(n, steps)):
        read(i).start()
    for copy in kv_in:
        copy.start()
    for i in range(steps):
        read(i).wait()
        write(i).start()
        if i >= 1 and i - 1 + n < steps:
            write(i - 1).wait()
            read(i - 1 + n).start()
    for e in SIDES:
        kv_in[e].wait()
        kv_out[e].start()
    for i in range(max(0, steps - n), steps):
        write(i).wait()
    for copy in kv_out:
        copy.wait()


def _copy(y, k, v):
    t, d = y.shape
    rows, n = 128, 32
    hbm = pl.BlockSpec(memory_space=pl.ANY)
    dma = pltpu.SemaphoreType.DMA
    n = min(n, t // rows)
    return pl.pallas_call(
        _copy_kernel,
        name="copy_out",
        out_shape=tuple(jax.ShapeDtypeStruct(a.shape, a.dtype) for a in (y, k, v)),
        in_specs=[hbm] * 3,
        out_specs=(hbm,) * 3,
        scratch_shapes=[pltpu.VMEM((n, rows, d), y.dtype), pltpu.VMEM((2,) + k.shape, k.dtype),
                        dma((n,)), dma((n,)), dma((2,))],
        compiler_params=pltpu.CompilerParams(vmem_limit_bytes=VMEM_BYTES),
        cost_estimate=pl.CostEstimate(flops=0, bytes_accessed=4 * t * d, transcendentals=0),
    )(y, k, v)


def _row_length(mesh):
    at = [getattr(dev, "coords", None) for dev in mesh.devices.reshape(mesh.shape["dp"], -1)[:, 0]]
    if any(p is None for p in at):
        return None
    n = len(at)

    def apart(i, j):
        return sum(abs(p - q) for p, q in zip(at[i], at[j]))

    length = next((i for i in range(1, n) if at[i][-1] == at[0][-1]), n)
    if length % 2 or n % (2 * length):
        return None
    rows = all(apart(i, i + 1) == 1 for i in range(0, n, 2))
    across = all(apart(i, i + length) == 1 for i in range(n) if (i // length) % 2 == 0)
    return length if rows and across else None


def solution(mesh):
    tp = mesh.shape["tp"]
    dp = mesh.shape["dp"]
    zn = _row_length(mesh)

    def local(x, pos, g1, g2, wq, wk, wv, wo, wg, wu, wd):
        t = x.shape[0]
        half = ROPE_BASE ** (-2.0 * np.arange(HEAD // 2) / HEAD)
        inv = jnp.asarray(np.concatenate([half, half])[None, :].astype(np.float32))
        y, k, v, _ = _layer(tp, dp, zn, x, pos.reshape(t // LANES, LANES), inv, g1, g2, wq, wk, wv, wo, wg, wu, wd)
        y, k, v = _copy(y, k, v)
        return y, k.reshape(t, 1, HEAD), v.reshape(t, 1, HEAD)

    return jax.shard_map(
        local,
        mesh=mesh,
        in_specs=(P("dp", None), P("dp"), P(), P(), P(None, "tp"), P(), P(), P("tp", None),
                  P(None, "tp"), P(None, "tp"), P("tp", None)),
        out_specs=(P("dp", None), P("dp", "tp", None), P("dp", "tp", None)),
        check_vma=False,
    )
```

time: 1010 us -> 354 us (0.35)
  waiting for transfers between devices: 512 us -> 0 us
  Pallas kernels: 0 us -> 353 us
  matrix products: 282 us -> 0 us
  other arithmetic: 172 us -> 0 us
  local copies, waits for them, and re-layouts: 24.5 us -> 0 us
  between operations: 14.8 us -> 0.64 us
    psum x2 -> x0, waiting for transfers between devices: 512 us -> none  [the longest x1 259 us: local(): h = (x.astype(f32) + lax.psum(p, 'tp').astype(f32)).astype(bf)]
    pallas_call x0 -> x2, Pallas kernels: none -> 353 us  [the longest x1 334 us: _layer(): pl.pallas_call(functools.partial(_kernel, tp, dp, zn, l1, l2, nb // 4, nb...]
    dot_general x39 -> x0, matrix products: 282 us -> none  [the longest x16 64.8 us: _attend(): jnp.einsum('grqk,kgd->qgrd', pr, v[:n], preferred_element_type=jnp.float32)]
    reduce_sum x18 -> x0, other arithmetic: 82.6 us -> none  [the longest x16 46.9 us: _attend(): pr = (e / jnp.sum(e, axis=-1, keepdims=True)).astype(jnp.bfloat16)]
    convert_element_type x5 -> x0, other arithmetic: 53.9 us -> none  [the longest x1 30 us: local(): y = (h.astype(f32) + lax.psum(rr, 'tp').astype(f32)).astype(bf)]
    unnamed x59 -> x0, local copies, waits for them, and re-layouts: 15.4 us -> none
    le x16 -> x0, other arithmetic: 14.7 us -> none  [_attend(): pos_k[:n][None, :] <= pp[:, None]]
    another operation x2 -> x0, other arithmetic: 11.7 us -> none
  transfers between devices with their start and end apart: 2 -> 0, of which waited for: 2 -> 0; matrix products, arithmetic and copies ran while one was open for 0% -> 0% of each run, Pallas kernels for 0% -> 0%
where the time goes in v3:
time: 354 us; the launch traced here: 353 us
  Pallas kernels  353 us (100%)
    pallas_call x1, Pallas kernels, _layer(): pl.pallas_call(functools.partial(_kernel, tp, dp, zn, l1, l2, nb // 4, nb...  334 us
    pallas_call x1, Pallas kernels, _copy(): pl.pallas_call(_copy_kernel, name='copy_out', out_shape=tuple((jax.ShapeD...  18.9 us

profile of v3, /device:TPU:81, one launch (start us, length us, event | category | flops | bytes accessed | tf_op | source)
XLA Modules:
  0.0 353.5 jit_solution(13726607699122589971)
XLA Ops:
  0.6 333.9 %layer.1 = (bf16[4096,3072]{1,0:T(8,128)(2,1)}, bf16[4096,128]{1,0:T(8,128)(2,1)}, bf16[4096,128]{1,0:T(8,128)(2,1)}, bf16[4096,3072]{1,0:T(8,128)(2,1)}) custom-call(bf16[4096,3072]{1,0:T(8,128)(2,1)} %x_ref.1, s32[32,128]{1,0:T(8,128)} %bitcast.5, f32[1,128]{1,0:T(1,128)} %constant.2.clone.inv_ref, bf16[3072]{0:T(1024)(128)(2,1)} %g1_ref.1, ...), custom_call_target="tpu_custom_call" | custom-call | flops 144955146240 | bytes 100663296 | tf_op jit(solution)/shard_map/layer/pallas_call | solution.py:585
  334.6 18.9 %copy_out.1 = (bf16[4096,3072]{1,0:T(8,128)(2,1)}, bf16[4096,128]{1,0:T(8,128)(2,1)}, bf16[4096,128]{1,0:T(8,128)(2,1)}) custom-call(bf16[4096,3072]{1,0:T(8,128)(2,1)} %get-tuple-element.9.src, bf16[4096,128]{1,0:T(8,128)(2,1)} %get-tuple-element.10.k_src, bf16[4096,128]{1,0:T(8,128)(2,1)} %get-tuple-element.11.v_src), custom_call_target="tpu_custom_call" | custom-call | bytes 50331648 | tf_op jit(solution)/shard_map/copy_out/pallas_call | solution.py:635

commit v4 on v0

v4 whole, which is shorter than its diff:
```python
import functools

import jax
import jax.numpy as jnp
import numpy as np
from jax import lax
from jax.experimental import pallas as pl
from jax.experimental.pallas import tpu as pltpu
from jax.sharding import PartitionSpec as P

HEAD = 128
LANES = 128
SUB = 16
EPS = 1e-5
ROPE_BASE = 500000.0
MESH = pl.DeviceIdType.MESH
BLOCK = 256
NR = 64
SLOTS = 4
LATE = 8
SIDES = (0, 1)
BF = jnp.bfloat16
F32 = jnp.float32
VMEM_BYTES = 67000000
Y_VMEM = 8
TWO_OVER_PI = 0.6366197723675814
PI_2 = (1.5703125, 4.837512969970703125e-4, 7.54978995489188216e-8)
SIN = (-1.9515295891e-4, 8.3321608736e-3, -1.6666654611e-1)
COS = (2.443315711809948e-5, -1.388731625493765e-3, 4.166664568298827e-2)
LOG2E = 1.4426950408889634


def _sincos(ang):
    n = jnp.floor(ang * TWO_OVER_PI + 0.5)
    r = ang
    for p in PI_2:
        r = r - n * p
    z = r * r
    s = functools.reduce(lambda a, p: a * z + p, SIN[1:], SIN[0]) * z * r + r
    c = functools.reduce(lambda a, p: a * z + p, COS[1:], COS[0]) * z * z - 0.5 * z + 1.0
    m = n.astype(jnp.int32)
    odd = (m & 1) == 1
    cs = jnp.where(odd, s, c)
    sn = jnp.where(odd, c, s)
    return jnp.where(((m + 1) & 2) == 2, -cs, cs), jnp.where((m & 2) == 2, -sn, sn)


def _al(v, m):
    return pl.multiple_of(v, m)


def _first(ref, n):
    return ref.at[pl.ds(0, n)]


def _kernel(tp, dp, zn, split, l1, l2, w2, w3, w4,
            x_ref, pos_ref, inv_ref, g1_ref, g2_ref, wq_ref, wk_ref, wv_ref, wo_ref, wg_ref, wu_ref, wd_ref,
            y_ref, y_vm, k_ref, v_ref, oall_ref,
            pos_v, inv_v, g1_v, g2_v, wo_v, wg_v, wu_v, wd_v, g_scr, a_buf, o_buf,
            hbuf, rsib, rs_far, rs_near, rs_sum,
            ld_s, ld_w, ld_mlp, ld_x, kv_s,
            wo_d, wo_s, wo_r, wo_fs, wo_fr, wo_ps, wo_pr,
            o_s, o_sx, o_r, o_f, o_rs, o_rel, o_fwd,
            ld_o, h_s, h_r, r_s, r_r, part_s, far_r, near_r, sum_s, sum_r,
            y_s, y_r, y_f, y_rs, y_rel, y_fwd):
    t, d = x_ref.shape
    qw = wq_ref.shape[1]
    f = wg_ref.shape[1]
    hl = qw // HEAD
    b = BLOCK
    nb = t // b
    dh = d // 2
    hb = b // 2
    nc = tp // 2
    ow = hb // nc
    hw = ow // 2
    kvt = 2 * b

    r = lax.axis_index("tp")
    c = r // 2
    s = r % 2
    c_r = (c + 1) % nc
    c_l = (c + nc - 1) % nc
    c_o = (c + 2) % nc
    dest = ({"tp": c_r * 2 + s}, {"tp": c_l * 2 + s})
    origin = (c_l, c_r)
    target = (c_r, c_l)
    sib = {"tp": c * 2 + 1 - s}
    dpi = lax.axis_index("dp")
    par = dpi % 2
    peers = [{"dp": dpi + 1 - 2 * par}] if dp % 2 == 0 else []
    if zn:
        par_y = (dpi // zn) % 2
        peers.append({"dp": dpi + zn * (1 - 2 * par_y)})

    def send(src, dst, ss, rs, dev):
        pltpu.make_async_remote_copy(
            src_ref=src, dst_ref=dst, send_sem=ss, recv_sem=rs, device_id=dev, device_id_type=MESH).start()

    def put(src, dst, sem):
        pltpu.make_async_copy(src, dst, sem).start()

    def wait(region, sem, tag=None):
        with jax.named_scope("w_" + (tag or "end")):
            pltpu.make_async_copy(region, region, sem).wait()

    def when_block(j, body):
        @pl.when((j >= 0) & (j < nb))
        def _():
            body()

    barrier = pltpu.get_barrier_semaphore()
    cross = [{"tp": target[e] * 2 + 1 - s} for e in SIDES]
    others = [*dest, *cross, sib, *peers]
    for dev in others:
        pl.semaphore_signal(barrier, inc=1, device_id=dev, device_id_type=MESH)

    small = ((pos_ref, pos_v), (inv_ref, inv_v), (g1_ref, g1_v), (g2_ref, g2_v))
    for e, (src, dst) in enumerate(small):
        put(src, dst, ld_s.at[e])
    with jax.named_scope("barrier"):
        pl.semaphore_wait(barrier, len(others))

    mine = _al(s * dh, LANES)
    other = _al((1 - s) * dh, LANES)
    parts = 4 if zn else len(peers) + 1
    wr = qw // parts
    part = (2 * par_y + par) if zn else (par if peers else 0)

    def shard(dev):
        return wo_v.at[pl.ds(_al(dev * qw, LANES), qw)]

    def piece(chip, core, q=None):
        return wo_v.at[pl.ds(_al((chip * 2 + core) * qw + (part if q is None else q) * wr, 32), wr)]

    rows = pl.ds(_al(part * wr, 32), wr)
    for e in SIDES:
        for k, (cols, dev) in enumerate(((mine, dest[e]), (other, cross[e]))):
            send(wo_ref.at[rows, pl.ds(cols, dh)], piece(c, s), wo_s.at[e, k], wo_r.at[e, s], dev)
    send(wo_ref.at[:, pl.ds(other, dh)], shard(r), wo_d.at[0], wo_d.at[1], sib)
    put(wo_ref.at[:, pl.ds(mine, dh)], shard(r), wo_d.at[2])

    def wo_swap(chip):
        for e, dev in enumerate(peers):
            for core in SIDES:
                send(piece(chip, core), piece(chip, core), wo_ps.at[0, e], wo_pr.at[0, e], dev)

    def wo_stage2():
        for e in SIDES:
            for core in SIDES:
                wait(piece(origin[e], core), wo_r.at[e, core], "wo2")
            reg = piece(origin[e], e)
            send(reg, reg, wo_fs.at[e], wo_fr.at[e], dest[e])
            wo_swap(origin[e])

    def wo_stage3():
        for e in SIDES:
            wait(piece(c_o, e), wo_fr.at[e], "wo3")
        wo_swap(c_o)

    def wo_stage4():
        for e in range(len(peers)):
            wait(_first(wo_v, 6 * wr), wo_pr.at[0, e], "wo4")
        if zn:
            for chip in (*origin, c_o):
                for e, q in enumerate((2 * (1 - par_y) + par, 2 * par_y + 1 - par)):
                    reg = piece(chip, e, q)
                    send(reg, reg, wo_ps.at[1, e], wo_pr.at[1, e], peers[e])

    def wo_end(which):
        for e in SIDES if zn else ():
            wait(_first(wo_v, 3 * wr), which.at[1, e], "wo5")

    def ocol(chip, core):
        return pl.ds(_al((chip * 2 + core) * qw, LANES), qw)

    def oreg(j, chip):
        return oall_ref.at[pl.ds(_al(j * b, b), b), ocol(chip, s)]

    def ohalf(j, chip, half):
        return oall_ref.at[pl.ds(_al(j * b + half * hb, hb), hb), ocol(chip, s)]

    def orow(j):
        return pl.ds(_al(j * b, b), b)

    def o_stage2(j):
        def body():
            for e in SIDES:
                reg = oreg(j, origin[e])
                wait(reg, o_r.at[e, j], "o2")
                half = ohalf(j, origin[e], e)
                send(half, half, o_rel.at[e], o_f.at[e, j], dest[e])
                send(reg, reg, o_fwd, o_rs.at[j], sib)

        when_block(j, body)

    def o_stage3(j):
        def body():
            for e in SIDES:
                wait(ohalf(j, c_o, e), o_f.at[e, j], "o3")
            send(oreg(j, c_o), oreg(j, c_o), o_fwd, o_rs.at[j], sib)

        when_block(j, body)

    def unrolled(n, body):
        for e in range(n):
            body(e)

    def norm_rows(src, which):
        def step(e, carry):
            for q in range(NR // SUB):
                rows = pl.ds(_al(e * NR + q * SUB, SUB), SUB)
                v32 = src[rows, :].astype(F32)
                inv = lax.rsqrt(jnp.mean(v32 * v32, axis=1, keepdims=True) + EPS)
                a_buf[rows, :] = (v32 * inv * g_scr[which]).astype(BF)
            return carry

        with jax.named_scope("norm"):
            lax.fori_loop(0, b // NR, step, 0)

    for e, (src, dst) in enumerate(small):
        wait(dst, ld_s.at[e], "small")
    for e, ref in enumerate((g1_v, g2_v)):
        g_scr[e] = ref[...].astype(F32).reshape(1, d)

    def attention(wqkv, x_buf, q_scr, k_scr, v_scr, m_scr, l_scr, acc_scr):
        rk = _al(r * HEAD, HEAD)
        wq_dst = wqkv.at[:, pl.ds(0, qw)]
        kv_dst = [wqkv.at[:, pl.ds(qw + e * HEAD, HEAD)] for e in SIDES]
        put(_first(x_ref, b), x_buf.at[0], ld_x.at[0])
        put(wq_ref, wq_dst, ld_w.at[2])
        for e, ref in enumerate((wk_ref, wv_ref)):
            put(ref.at[:, pl.ds(rk, HEAD)], kv_dst[e], ld_w.at[e])
        caches = ((k_scr, k_ref), (v_scr, v_ref))
        scale = HEAD ** -0.5 * LOG2E
        lane = lax.broadcasted_iota(jnp.int32, (b, HEAD), 1)

        def heads(ref, h):
            return ref.at[pl.ds(h * b, b)]

        def tile(first, n, masked=False):
            keys = pl.ds(_al(first, n), n)
            kk = k_scr[keys, :]
            vv = v_scr[keys, :]
            sc = lax.dot_general(q_scr[...], kk, (((1,), (1,)), ((), ())), preferred_element_type=F32)
            if masked:
                keep = lax.broadcasted_iota(jnp.int32, (b, n), 1) <= lax.broadcasted_iota(jnp.int32, (b, n), 0)
                sc = jnp.concatenate([jnp.where(keep, sc[h * b:(h + 1) * b], -jnp.inf) for h in range(hl)], axis=0)
            m_prev = m_scr[...]
            m_new = jnp.maximum(m_prev, jnp.max(sc, axis=1, keepdims=True))
            ps = [jnp.exp2((sc[:, e * HEAD:(e + 1) * HEAD] - m_new) * scale) for e in range(n // HEAD)]
            alpha = jnp.exp2((m_prev - m_new) * scale)
            l_scr[...] = l_scr[...] * alpha + functools.reduce(lambda p, q: p + q, ps)
            pr = jnp.concatenate([p.astype(BF) for p in ps], axis=1)
            acc_scr[...] = acc_scr[...] * alpha + jnp.dot(pr, vv, preferred_element_type=F32)
            m_scr[...] = m_new

        def phase1(i, carry):
            with jax.named_scope("slot1"):
                phase1_slot(i)
            return carry

        def phase1_slot(i):
            slot = i % 2
            wait(x_buf.at[slot], ld_x.at[slot], "x")

            @pl.when(i + 1 < nb)
            def _():
                put(x_ref.at[pl.ds(_al((i + 1) * b, b), b)], x_buf.at[1 - slot], ld_x.at[1 - slot])

            norm_rows(x_buf.at[slot], 0)

            @pl.when(i == 0)
            def _():
                wait(wq_dst, ld_w.at[2], "w")
                for e in SIDES:
                    wait(kv_dst[e], ld_w.at[e], "w")

            for e, (src, dst) in enumerate(((wg_ref, wg_v), (wu_ref, wu_v), (wd_ref, wd_v))):
                @pl.when(i == w2 + e)
                def _(src=src, dst=dst, e=e):
                    put(src, dst, ld_mlp.at[e])

            pcol = []
            for e in range(b // LANES):
                prow = pos_v[pl.ds(i * (b // LANES) + e, 1), :].astype(F32)
                pcol.append(jnp.transpose(jnp.broadcast_to(prow, (LANES, LANES))))
            co, si = _sincos(jnp.concatenate(pcol, axis=0) * inv_v[...])
            si = jnp.where(lane < HEAD // 2, -si, si)
            qk32 = jnp.dot(a_buf[...], wqkv[:, :qw + HEAD], preferred_element_type=F32)
            v32 = jnp.dot(a_buf[...], wqkv[:, qw + HEAD:], preferred_element_type=F32)
            rows = pl.ds(_al(i * b, b), b)
            for h in range(hl + 1):
                head = qk32[:, h * HEAD:(h + 1) * HEAD]
                head = (head * co + pltpu.roll(head, HEAD // 2, 1) * si).astype(BF)
                if h < hl:
                    heads(q_scr, h)[...] = head
                else:
                    k_scr[rows, :] = head
            v_scr[rows, :] = v32.astype(BF)
            for e, (src, dst) in enumerate(caches):
                @pl.when(i > 0)
                def _(src=src, e=e):
                    wait(_first(src, b), kv_s.at[e])

                put(src.at[rows], dst.at[rows], kv_s.at[e])
            m_scr[...] = jnp.full(m_scr.shape, -jnp.inf, F32)
            l_scr[...] = jnp.zeros(l_scr.shape, F32)
            acc_scr[...] = jnp.zeros(acc_scr.shape, F32)
            full = i // 2

            def inner(j, carry):
                for e in SIDES:
                    tile((2 * j + e) * kvt, kvt)
                return carry

            with jax.named_scope("tiles"):
                lax.fori_loop(0, full // 2, inner, 0)

            @pl.when(full % 2 == 1)
            def _():
                tile((full - 1) * kvt, kvt)

            @pl.when(i % 2 == 1)
            def _():
                tile((i - 1) * b, b)

            tile(i * b, b, masked=True)
            for h in range(hl):
                o_buf[rows, h * HEAD:(h + 1) * HEAD] = (
                    heads(acc_scr, h)[...] / jnp.sum(heads(l_scr, h)[...], axis=1, keepdims=True)).astype(BF)
            src = o_buf.at[rows]
            dst = oreg(i, c)
            for e in SIDES:
                send(src, dst, o_s.at[e], o_r.at[e, i], dest[e])
            send(src, dst, o_sx.at[0], o_rs.at[i], sib)
            put(src, dst, o_sx.at[1])
            for when, stage in ((w2, wo_stage2), (w3, wo_stage3), (w4, wo_stage4)):
                pl.when(i == when)(stage)
            o_stage2(i - l1)
            o_stage3(i - l2)

        lax.fori_loop(0, nb, phase1, 0)
        for e, (src, _) in enumerate(caches):
            wait(_first(src, b), kv_s.at[e])

    loc = pltpu.VMEM
    pl.run_scoped(
        attention, loc((d, qw + 2 * HEAD), BF), loc((2, b, d), BF), loc((hl * b, HEAD), BF), loc((t, HEAD), BF),
        loc((t, HEAD), BF), *[loc((hl * b, HEAD), F32)] * 3)
    wait(o_buf, o_sx.at[1])
    for e, dst in enumerate((wg_v, wu_v, wd_v)):
        wait(dst, ld_mlp.at[e])
    wait(shard(r + 1 - 2 * s), wo_d.at[1])
    wait(shard(r), wo_d.at[2])
    wo_end(wo_pr)

    def rest(o_blk, xh, u_buf, r_buf, cp, sums, ych, hst):
        def load_o(j):
            wait(oall_ref.at[orow(j), pl.ds(0, 4 * qw)], o_rs.at[j], "os")
            put(oall_ref.at[orow(j)], o_blk, ld_o.at[0])
            put(x_ref.at[orow(j), pl.ds(mine, dh)], xh, ld_o.at[1])

        nt_h = min(512, dh)
        nt_f = min(512, f)
        nt_d = min(512, d)

        def cpart(q4, chip, half):
            return cp.at[q4, pl.ds(_al(chip * ow + half * hw, hw), hw)]

        def sum_start(j):
            def body():
                two = j % 2
                q4 = j % SLOTS
                wait(rsib.at[two], r_r.at[two], "r")
                wait(rsib.at[two], r_s, "rs")

                def add(e, carry):
                    rows = pl.ds(_al(e * SUB, SUB), SUB)
                    own = r_buf[pl.ds(_al(s * hb + e * SUB, SUB), SUB), :]
                    cp[q4, rows, :] = (own.astype(F32) + rsib[two, rows, :].astype(F32)).astype(BF)
                    return carry

                with jax.named_scope("add"):
                    lax.fori_loop(0, hb // SUB, add, 0)
                for e in SIDES:
                    send(cpart(q4, c_o, e), rs_far.at[q4, e], part_s.at[q4], far_r.at[q4, e], dest[e])
                for e in SIDES:
                    send(cpart(q4, target[e], 1 - e), rs_near.at[q4, e], part_s.at[q4], near_r.at[q4, e], dest[e])

            when_block(j, body)

        def own_h(j):
            @pl.when(j < nb)
            def _():
                wait(o_blk, ld_o.at[0], "ldo")
                wait(xh, ld_o.at[1], "ldo")

                def col(n):
                    cols = pl.ds(n * nt_h, nt_h)
                    v32 = jnp.dot(o_blk[...], wo_v[:, cols], preferred_element_type=F32)
                    hbuf[j % 2, :, pl.ds(_al(s * dh + n * nt_h, LANES), nt_h)] = (xh[:, cols].astype(F32) + v32).astype(BF)

                with jax.named_scope("own_h"):
                    unrolled(dh // nt_h, col)

        def swap_h(j):
            @pl.when(j < nb)
            def _():
                half = hbuf.at[j % 2, :, pl.ds(mine, dh)]
                send(half, half, h_s.at[j % 2], h_r.at[j % 2], sib)

            @pl.when(j + 1 < nb)
            def _():
                load_o(j + 1)

        def mlp_norm(j):
            def body():
                two = j % 2
                wait(hbuf.at[two, :, pl.ds(other, dh)], h_r.at[two], "h")
                wait(hbuf.at[two, :, pl.ds(mine, dh)], h_s.at[two], "hs")
                norm_rows(hbuf.at[two], 1)
                hst[j % SLOTS] = hbuf[two, pl.ds(_al(s * hb + c * ow, SUB), ow), :]

            when_block(j, body)

        def mlp_up(j):
            def body():
                def col(n):
                    cols = pl.ds(n * nt_f, nt_f)
                    gt = jnp.dot(a_buf[...], wg_v[:, cols], preferred_element_type=F32)
                    up = jnp.dot(a_buf[...], wu_v[:, cols], preferred_element_type=F32)
                    u_buf[:, cols] = (gt * (1.0 / (1.0 + jnp.exp(-gt))) * up).astype(BF)

                with jax.named_scope("up"):
                    unrolled(f // nt_f, col)

            when_block(j, body)

        def mlp_down(j):
            def body():
                def col(n):
                    cols = pl.ds(n * nt_d, nt_d)
                    r_buf[:, cols] = jnp.dot(u_buf[...], wd_v[:, cols], preferred_element_type=F32).astype(BF)

                with jax.named_scope("down"):
                    unrolled(d // nt_d, col)
                send(r_buf.at[pl.ds(_al((1 - s) * hb, hb), hb)], rsib.at[j % 2], r_s, r_r.at[j % 2], sib)

            when_block(j, body)

        def sum_relay(j):
            def body():
                q4 = j % SLOTS
                @pl.when(j >= SLOTS)
                def _():
                    wait(sums.at[q4], sum_s.at[q4], "sums")

                for e in SIDES:
                    wait(rs_far.at[q4, e], far_r.at[q4, e], "s1")
                    sums[q4, e] = (rs_far[q4, e].astype(F32) + cpart(q4, target[e], e)[...].astype(F32)).astype(BF)
                    send(sums.at[q4, e], rs_sum.at[q4, e], sum_s.at[q4], sum_r.at[q4, e], dest[e])

            when_block(j, body)

        def on_y(j, body):
            @pl.when((j >= 0) & (j < split))
            def _():
                body(y_ref, j * b, False)

            @pl.when((j >= split) & (j < nb))
            def _():
                body(y_vm, (j - split) * b, True)

        def yrow(ref, row, chip):
            return ref.at[pl.ds(_al(row + s * hb + chip * ow, ow), ow)]

        def yhalf(ref, row, chip, half):
            return ref.at[pl.ds(_al(row + s * hb + chip * ow + half * hw, hw), hw)]

        def y_sent(j, vmem):
            wait(cp.at[j % SLOTS, pl.ds(0, (3 if vmem else 4) * ow)], y_s.at[j % SLOTS], "ysent")

        def sum_end(j):
            on_y(j - SLOTS, lambda ref, row, vmem: pl.when(j < nb)(lambda: y_sent(j - SLOTS, vmem)))

            def body(ref, row, vmem):
                q4 = j % SLOTS
                wait(cp.at[q4, pl.ds(0, 4 * hw)], part_s.at[q4], "s1s")
                for e in SIDES:
                    wait(rs_near.at[q4, e], near_r.at[q4, e], "s2")
                    wait(rs_sum.at[q4, e], sum_r.at[q4, e], "s2")
                own = yrow(ref, row, c)
                src = own if vmem else ych.at[q4]
                for e in SIDES:
                    rows = pl.ds(e * hw, hw)
                    tot = cpart(q4, c, e)[...].astype(F32) + rs_near[q4, 1 - e].astype(F32) + rs_sum[q4, e].astype(F32)
                    dst = yhalf(ref, row, c, e) if vmem else ych.at[q4, rows]
                    dst[...] = (hst[q4, rows, :].astype(F32) + tot).astype(BF)
                for e in SIDES:
                    send(src, own, y_s.at[q4], y_r.at[e, q4], dest[e])
                send(src, own, y_s.at[q4], y_rs.at[j % LATE], sib)
                if not vmem:
                    put(src, own, y_s.at[q4])

            on_y(j, body)

        def y_stage2(j):
            def body(ref, row, vmem):
                for e in SIDES:
                    reg = yrow(ref, row, origin[e])
                    wait(reg, y_r.at[e, j % SLOTS], "y2")
                    half = yhalf(ref, row, origin[e], e)
                    send(half, half, y_rel.at[e], y_f.at[e, j % SLOTS], dest[e])
                    send(reg, reg, y_fwd, y_rs.at[j % LATE], sib)

            on_y(j, body)

        def y_stage3(j):
            def body(ref, row, vmem):
                for e in SIDES:
                    wait(yhalf(ref, row, c_o, e), y_f.at[e, j % SLOTS], "y3")
                reg = yrow(ref, row, c_o)
                send(reg, reg, y_fwd, y_rs.at[j % LATE], sib)

            on_y(j, body)

        def y_seen(j):
            when_block(j, lambda: wait(cp.at[0], y_rs.at[j % LATE], "ys"))

        load_o(0)

        def phase2(i, carry):
            with jax.named_scope("slot2"):
                own_h(i)
                sum_start(i - 2)
                swap_h(i)
                mlp_norm(i - 1)
                sum_relay(i - 3)
                mlp_up(i - 1)
                sum_end(i - 4)
                mlp_down(i - 1)
                y_stage2(i - 5)
                y_stage3(i - 6)
                y_seen(i - LATE)
                o_stage2(nb + i - l1)
                o_stage3(nb + i - l2)
            return carry

        lax.fori_loop(0, nb + 6, phase2, 0)

        for j in range(nb + 6 - LATE, nb):
            wait(cp.at[0], y_rs.at[j % LATE])
        for j in range(nb - SLOTS, nb):
            y_sent(j, j >= split)
            wait(sums.at[j % SLOTS], sum_s.at[j % SLOTS])
        for e in SIDES:
            wait(_first(y_ref, nb * hw), y_rel.at[e])
            wait(o_buf, o_s.at[e])
            wait(oall_ref.at[pl.ds(0, t // 2), pl.ds(0, qw)], o_rel.at[e])
            wait(_first(wo_v, wr), wo_fs.at[e])
            for k in SIDES:
                wait(_first(wo_v, wr), wo_s.at[e, k])
        wait(_first(y_ref, nb * ow * 3), y_fwd)
        wait(o_buf, o_sx.at[0])
        wait(oall_ref.at[:, pl.ds(0, 3 * qw)], o_fwd)
        wait(_first(wo_v, qw), wo_d.at[0])
        for e in range(len(peers)):
            wait(_first(wo_v, 6 * wr), wo_ps.at[0, e])
        wo_end(wo_ps)

    pl.run_scoped(
        rest, loc((b, tp * qw), BF), loc((b, dh), BF), loc((b, f), BF), loc((b, d), BF), loc((SLOTS, hb, d), BF),
        loc((SLOTS, 2, hw, d), BF), *[loc((SLOTS, ow, d), BF)] * 2)


def _held(rows, d):
    return pltpu.VMEM((rows, d), BF)


def _keep(a, space):
    return pltpu.with_memory_space_constraint(a, space)


def _layer(tp, dp, zn, x, pos, inv, g1, g2, wq, wk, wv, wo, wg, wu, wd):
    t, d = x.shape
    qw = wq.shape[1]
    f = wg.shape[1]
    hl = qw // HEAD
    b = BLOCK
    nb = t // b
    hb = b // 2
    nc = tp // 2
    ow = hb // nc
    hw = ow // 2
    dh = d // 2
    assert nc == SLOTS and t % b == 0 and wk.shape[1] == tp * HEAD
    l1 = max(nb // 4, 1)
    l2 = min(nb * 3 // 4, nb - 2)
    hbm = pl.BlockSpec(memory_space=pl.ANY)
    bufs = [
        (tp * qw, dh), (d, f), (d, f), (f, d), None, (b, d), (t, qw),
        (2, b, d), (2, hb, d), *[(SLOTS, 2, hw, d)] * 3,
    ]
    scratch = [pltpu.VMEM(a.shape, a.dtype) for a in (pos, inv, g1, g2)]
    scratch += [pltpu.VMEM((2, 1, d), F32) if shape is None else pltpu.VMEM(shape, BF) for shape in bufs]
    two, four, ring, per = (2,), (SLOTS, 2), (2, nb), (nb,)
    sems = [(4,), (3,), (3,), two, two,
            (3,), (2, 2), (2, 2), two, two, (2, 2), (2, 2),
            two, two, ring, ring, per, two, (),
            two, two, two, (), two, (SLOTS,), four, four, (SLOTS,), four,
            (SLOTS,), (2, SLOTS), (2, SLOTS), (LATE,), two, ()]
    scratch += [pltpu.SemaphoreType.DMA(shape) for shape in sems]
    flops = 2 * t * (d * (qw + 2 * HEAD) + qw * t + tp * qw * dh + 3 * d * f)
    split = nb - Y_VMEM * nb // 16
    outs = [(split * b, d), None, (t, HEAD), (t, HEAD), (t, tp * qw)]
    vm = _held((nb - split) * b, d)
    return pl.pallas_call(
        functools.partial(_kernel, tp, dp, zn, split, l1, l2, nb // 4, nb // 2, nb * 3 // 4),
        name="layer",
        out_shape=tuple(jax.ShapeDtypeStruct(shape, BF) if shape else vm for shape in outs),
        in_specs=[hbm] * 12,
        out_specs=tuple(hbm if shape else pl.BlockSpec(memory_space=pltpu.VMEM) for shape in outs),
        scratch_shapes=scratch,
        compiler_params=pltpu.CompilerParams(collective_id=0, has_side_effects=True,
                                             vmem_limit_bytes=VMEM_BYTES - 2 * (nb - split) * b * d),
        cost_estimate=pl.CostEstimate(flops=flops, bytes_accessed=8 * t * d, transcendentals=t * t * hl),
    )(x, pos, inv, g1, g2, wq, wk, wv, wo, wg, wu, wd)


def _copy_kernel(src, held, k_src, v_src, dst, k_dst, v_dst, buf, kv, rd, wr, kv_sem):
    rows = buf.shape[1]
    steps = src.shape[0] // rows
    small = ((k_src, k_dst), (v_src, v_dst))
    reads, writes, late = [], [], []
    for i in range(steps):
        part = pl.ds(i * rows, rows)
        reads.append(pltpu.make_async_copy(src.at[part], buf.at[i], rd.at[i]))
        writes.append(pltpu.make_async_copy(buf.at[i], dst.at[part], rd.at[i]))
    for e, (a, z) in enumerate(small):
        reads.append(pltpu.make_async_copy(a, kv.at[e], kv_sem.at[e]))
        writes.append(pltpu.make_async_copy(kv.at[e], z, kv_sem.at[e]))
    for i in range(held.shape[0] // rows):
        to = pl.ds(src.shape[0] + i * rows, rows)
        late.append(pltpu.make_async_copy(held.at[pl.ds(i * rows, rows)], dst.at[to], wr.at[i]))
    for copy in reads:
        copy.start()
    for copy in late:
        copy.start()
    for read, write in zip(reads, writes):
        read.wait()
        write.start()
    for copy in (*late, *writes):
        copy.wait()


def _copy(y, held, k, v):
    d = y.shape[1]
    t = y.shape[0] + held.shape[0]
    rows = 256
    hbm = pl.BlockSpec(memory_space=pltpu.HBM)
    dma = pltpu.SemaphoreType.DMA
    n = y.shape[0] // rows
    shapes = ((t, d), k.shape, v.shape)
    return pl.pallas_call(
        _copy_kernel,
        name="copy_out",
        out_shape=tuple(jax.ShapeDtypeStruct(shape, BF) for shape in shapes),
        in_specs=[hbm, pl.BlockSpec(memory_space=pltpu.VMEM), hbm, hbm],
        out_specs=(hbm,) * 3,
        scratch_shapes=[pltpu.VMEM((n, rows, d), BF), pltpu.VMEM((2,) + k.shape, BF),
                        dma((n,)), dma((held.shape[0] // rows,)), dma((2,))],
        compiler_params=pltpu.CompilerParams(vmem_limit_bytes=VMEM_BYTES - 3 * held.size),
        cost_estimate=pl.CostEstimate(flops=0, bytes_accessed=4 * t * d, transcendentals=0),
    )(y, held, k, v)


def _row_length(mesh):
    at = [getattr(dev, "coords", None) for dev in mesh.devices.reshape(mesh.shape["dp"], -1)[:, 0]]
    if any(p is None for p in at):
        return None
    n = len(at)

    def apart(i, j):
        return sum(abs(p - q) for p, q in zip(at[i], at[j]))

    length = next((i for i in range(1, n) if at[i][-1] == at[0][-1]), n)
    if length % 2 or n % (2 * length):
        return None
    rows = all(apart(i, i + 1) == 1 for i in range(0, n, 2))
    across = all(apart(i, i + length) == 1 for i in range(n) if (i // length) % 2 == 0)
    return length if rows and across else None


def solution(mesh):
    tp = mesh.shape["tp"]
    dp = mesh.shape["dp"]
    zn = _row_length(mesh)

    def local(x, pos, g1, g2, wq, wk, wv, wo, wg, wu, wd):
        t = x.shape[0]
        half = ROPE_BASE ** (-2.0 * np.arange(HEAD // 2) / HEAD)
        inv = jnp.asarray(np.concatenate([half, half])[None, :].astype(np.float32))
        y, held, k, v, _ = _layer(tp, dp, zn, x, pos.reshape(t // LANES, LANES), inv, g1, g2, wq, wk, wv, wo, wg, wu, wd)
        y, k, v = (_keep(a, pltpu.HBM) for a in (y, k, v))
        y, k, v = _copy(y, _keep(held, pltpu.VMEM), k, v)
        return y, k.reshape(t, 1, HEAD), v.reshape(t, 1, HEAD)

    return jax.shard_map(
        local,
        mesh=mesh,
        in_specs=(P("dp", None), P("dp"), P(), P(), P(None, "tp"), P(), P(), P("tp", None),
                  P(None, "tp"), P(None, "tp"), P("tp", None)),
        out_specs=(P("dp", None), P("dp", "tp", None), P("dp", "tp", None)),
        check_vma=False,
    )
```

time: 1010 us -> 349 us (0.35)
  waiting for transfers between devices: 512 us -> 0 us
  Pallas kernels: 0 us -> 348 us
  matrix products: 282 us -> 0 us
  other arithmetic: 172 us -> 0 us
  local copies, waits for them, and re-layouts: 24.5 us -> 0 us
  between operations: 14.8 us -> 0.64 us
    psum x2 -> x0, waiting for transfers between devices: 512 us -> none  [the longest x1 259 us: local(): h = (x.astype(f32) + lax.psum(p, 'tp').astype(f32)).astype(bf)]
    pallas_call x0 -> x2, Pallas kernels: none -> 348 us  [the longest x1 333 us: _layer(): pl.pallas_call(functools.partial(_kernel, tp, dp, zn, split, l1, l2, nb /...]
    dot_general x39 -> x0, matrix products: 282 us -> none  [the longest x16 64.8 us: _attend(): jnp.einsum('grqk,kgd->qgrd', pr, v[:n], preferred_element_type=jnp.float32)]
    reduce_sum x18 -> x0, other arithmetic: 82.6 us -> none  [the longest x16 46.9 us: _attend(): pr = (e / jnp.sum(e, axis=-1, keepdims=True)).astype(jnp.bfloat16)]
    convert_element_type x5 -> x0, other arithmetic: 53.9 us -> none  [the longest x1 30 us: local(): y = (h.astype(f32) + lax.psum(rr, 'tp').astype(f32)).astype(bf)]
    unnamed x59 -> x0, local copies, waits for them, and re-layouts: 15.4 us -> none
    le x16 -> x0, other arithmetic: 14.7 us -> none  [_attend(): pos_k[:n][None, :] <= pp[:, None]]
    another operation x2 -> x0, other arithmetic: 11.7 us -> none
  transfers between devices with their start and end apart: 2 -> 0, of which waited for: 2 -> 0; matrix products, arithmetic and copies ran while one was open for 0% -> 0% of each run, Pallas kernels for 0% -> 0%
where the time goes in v4:
time: 349 us
  Pallas kernels  348 us (100%)
    pallas_call x1, Pallas kernels, _layer(): pl.pallas_call(functools.partial(_kernel, tp, dp, zn, split, l1, l2, nb /...  333 us
    pallas_call x1, Pallas kernels, _copy(): pl.pallas_call(_copy_kernel, name='copy_out', out_shape=tuple((jax.ShapeD...  15 us

profile of v4, /device:TPU:81, one launch (start us, length us, event | category | flops | bytes accessed | tf_op | source)
XLA Modules:
  0.0 348.8 jit_solution(15349780512646286036)
XLA Ops:
  0.6 333.2 %layer.1 = (bf16[2048,3072]{1,0:T(8,128)(2,1)}, bf16[2048,3072]{1,0:T(8,128)(2,1)S(1)}, bf16[4096,128]{1,0:T(8,128)(2,1)}, bf16[4096,128]{1,0:T(8,128)(2,1)}, bf16[4096,3072]{1,0:T(8,128)(2,1)}) custom-call(bf16[4096,3072]{1,0:T(8,128)(2,1)} %x_ref.1, s32[32,128]{1,0:T(8,128)} %bitcast.5, f32[1,128]{1,0:T(1,128)} %constant.2.clone.inv_ref, ...), custom_call_target="tpu_custom_call" | custom-call | flops 144955146240 | bytes 100663296 | tf_op jit(solution)/shard_map/layer/pallas_call | solution.py:618
  333.8 15.0 %copy_out.1 = (bf16[4096,3072]{1,0:T(8,128)(2,1)}, bf16[4096,128]{1,0:T(8,128)(2,1)}, bf16[4096,128]{1,0:T(8,128)(2,1)}) custom-call(bf16[2048,3072]{1,0:T(8,128)(2,1)} %get-tuple-element.10.src, bf16[2048,3072]{1,0:T(8,128)(2,1)S(1)} %get-tuple-element.11.held, bf16[4096,128]{1,0:T(8,128)(2,1)} %get-tuple-element.12.k_src, ...), custom_call_target="tpu_custom_call" | custom-call | bytes 50331648 | tf_op jit(solution)/shard_map/copy_out/pallas_call | solution.py:665

commit v5 on v4

--- a/solution.py
+++ b/solution.py
@@ -18,11 +18,12 @@
 NR = 64
 SLOTS = 4
 LATE = 8
+CHIP = 3
 SIDES = (0, 1)
 BF = jnp.bfloat16
 F32 = jnp.float32
-VMEM_BYTES = 67000000
-Y_VMEM = 8
+VMEM_BYTES = 67040000
+Y_VMEM = 11
 TWO_OVER_PI = 0.6366197723675814
 PI_2 = (1.5703125, 4.837512969970703125e-4, 7.54978995489188216e-8)
 SIN = (-1.9515295891e-4, 8.3321608736e-3, -1.6666654611e-1)
@@ -71,10 +72,13 @@
     nb = t // b
     dh = d // 2
     hb = b // 2
+    fh = f // 2
     nc = tp // 2
     ow = hb // nc
     hw = ow // 2
     kvt = 2 * b
+
+    wd_late = y_vm.at[pl.ds((nb - split) * b - fh, fh)]
 
     r = lax.axis_index("tp")
     c = r // 2
@@ -212,7 +216,7 @@
                 rows = pl.ds(_al(e * NR + q * SUB, SUB), SUB)
                 v32 = src[rows, :].astype(F32)
                 inv = lax.rsqrt(jnp.mean(v32 * v32, axis=1, keepdims=True) + EPS)
-                a_buf[rows, :] = (v32 * inv * g_scr[which]).astype(BF)
+                a_buf[rows, :] = (v32 * inv * g_scr[which:which + 1, :]).astype(BF)
             return carry
 
         with jax.named_scope("norm"):
@@ -221,17 +225,18 @@
     for e, (src, dst) in enumerate(small):
         wait(dst, ld_s.at[e], "small")
     for e, ref in enumerate((g1_v, g2_v)):
-        g_scr[e] = ref[...].astype(F32).reshape(1, d)
+        g_scr[e:e + 1, :] = ref[...].astype(F32).reshape(1, d)
 
     def attention(wqkv, x_buf, q_scr, k_scr, v_scr, m_scr, l_scr, acc_scr):
         rk = _al(r * HEAD, HEAD)
         wq_dst = wqkv.at[:, pl.ds(0, qw)]
         kv_dst = [wqkv.at[:, pl.ds(qw + e * HEAD, HEAD)] for e in SIDES]
-        put(_first(x_ref, b), x_buf.at[0], ld_x.at[0])
+        put(_first(x_ref, b), x_buf, ld_x)
         put(wq_ref, wq_dst, ld_w.at[2])
         for e, ref in enumerate((wk_ref, wv_ref)):
             put(ref.at[:, pl.ds(rk, HEAD)], kv_dst[e], ld_w.at[e])
         caches = ((k_scr, k_ref), (v_scr, v_ref))
+        mlp = ((wg_ref, wg_v), (wu_ref, wu_v), (_first(wd_ref, fh), wd_v), (wd_ref.at[pl.ds(fh, fh)], wd_late))
         scale = HEAD ** -0.5 * LOG2E
         lane = lax.broadcasted_iota(jnp.int32, (b, HEAD), 1)
 
@@ -261,14 +266,12 @@
             return carry
 
         def phase1_slot(i):
-            slot = i % 2
-            wait(x_buf.at[slot], ld_x.at[slot], "x")
+            wait(x_buf, ld_x, "x")
+            norm_rows(x_buf, 0)
 
             @pl.when(i + 1 < nb)
             def _():
-                put(x_ref.at[pl.ds(_al((i + 1) * b, b), b)], x_buf.at[1 - slot], ld_x.at[1 - slot])
-
-            norm_rows(x_buf.at[slot], 0)
+                put(x_ref.at[pl.ds(_al((i + 1) * b, b), b)], x_buf, ld_x)
 
             @pl.when(i == 0)
             def _():
@@ -276,8 +279,8 @@
                 for e in SIDES:
                     wait(kv_dst[e], ld_w.at[e], "w")
 
-            for e, (src, dst) in enumerate(((wg_ref, wg_v), (wu_ref, wu_v), (wd_ref, wd_v))):
-                @pl.when(i == w2 + e)
+            for e, (src, dst) in enumerate(mlp):
+                @pl.when(i == min(w2 + e, nb - 1))
                 def _(src=src, dst=dst, e=e):
                     put(src, dst, ld_mlp.at[e])
 
@@ -346,10 +349,10 @@
 
     loc = pltpu.VMEM
     pl.run_scoped(
-        attention, loc((d, qw + 2 * HEAD), BF), loc((2, b, d), BF), loc((hl * b, HEAD), BF), loc((t, HEAD), BF),
+        attention, loc((d, qw + 2 * HEAD), BF), loc((b, d), BF), loc((hl * b, HEAD), BF), loc((t, HEAD), BF),
         loc((t, HEAD), BF), *[loc((hl * b, HEAD), F32)] * 3)
     wait(o_buf, o_sx.at[1])
-    for e, dst in enumerate((wg_v, wu_v, wd_v)):
+    for e, dst in enumerate((wg_v, wu_v, wd_v, wd_late)):
         wait(dst, ld_mlp.at[e])
     wait(shard(r + 1 - 2 * s), wo_d.at[1])
     wait(shard(r), wo_d.at[2])
@@ -365,8 +368,8 @@
         nt_f = min(512, f)
         nt_d = min(512, d)
 
-        def cpart(q4, chip, half):
-            return cp.at[q4, pl.ds(_al(chip * ow + half * hw, hw), hw)]
+        def cpart(j, chip, half):
+            return cp.at[j % CHIP, pl.ds(_al(chip * ow + half * hw, hw), hw)]
 
         def sum_start(j):
             def body():
@@ -378,15 +381,15 @@
                 def add(e, carry):
                     rows = pl.ds(_al(e * SUB, SUB), SUB)
                     own = r_buf[pl.ds(_al(s * hb + e * SUB, SUB), SUB), :]
-                    cp[q4, rows, :] = (own.astype(F32) + rsib[two, rows, :].astype(F32)).astype(BF)
+                    cp[j % CHIP, rows, :] = (own.astype(F32) + rsib[two, rows, :].astype(F32)).astype(BF)
                     return carry
 
                 with jax.named_scope("add"):
                     lax.fori_loop(0, hb // SUB, add, 0)
                 for e in SIDES:
-                    send(cpart(q4, c_o, e), rs_far.at[q4, e], part_s.at[q4], far_r.at[q4, e], dest[e])
-                for e in SIDES:
-                    send(cpart(q4, target[e], 1 - e), rs_near.at[q4, e], part_s.at[q4], near_r.at[q4, e], dest[e])
+                    send(cpart(j, c_o, e), rs_far.at[q4, e], part_s.at[q4], far_r.at[q4, e], dest[e])
+                for e in SIDES:
+                    send(cpart(j, target[e], 1 - e), rs_near.at[q4, e], part_s.at[q4], near_r.at[q4, e], dest[e])
 
             when_block(j, body)
 
@@ -441,7 +444,9 @@
             def body():
                 def col(n):
                     cols = pl.ds(n * nt_d, nt_d)
-                    r_buf[:, cols] = jnp.dot(u_buf[...], wd_v[:, cols], preferred_element_type=F32).astype(BF)
+                    r32 = jnp.dot(u_buf[:, :fh], wd_v[:, cols], preferred_element_type=F32)
+                    r32 = r32 + jnp.dot(u_buf[:, fh:], wd_late[:, cols], preferred_element_type=F32)
+                    r_buf[:, cols] = r32.astype(BF)
 
                 with jax.named_scope("down"):
                     unrolled(d // nt_d, col)
@@ -452,14 +457,16 @@
         def sum_relay(j):
             def body():
                 q4 = j % SLOTS
-                @pl.when(j >= SLOTS)
+                two = j % 2
+
+                @pl.when(j >= 2)
                 def _():
-                    wait(sums.at[q4], sum_s.at[q4], "sums")
+                    wait(sums.at[two], sum_s.at[two], "sums")
 
                 for e in SIDES:
                     wait(rs_far.at[q4, e], far_r.at[q4, e], "s1")
-                    sums[q4, e] = (rs_far[q4, e].astype(F32) + cpart(q4, target[e], e)[...].astype(F32)).astype(BF)
-                    send(sums.at[q4, e], rs_sum.at[q4, e], sum_s.at[q4], sum_r.at[q4, e], dest[e])
+                    sums[two, e] = (rs_far[q4, e].astype(F32) + cpart(j, target[e], e)[...].astype(F32)).astype(BF)
+                    send(sums.at[two, e], rs_sum.at[q4, e], sum_s.at[two], sum_r.at[q4, e], dest[e])
 
             when_block(j, body)
 
@@ -479,23 +486,29 @@
             return ref.at[pl.ds(_al(row + s * hb + chip * ow + half * hw, hw), hw)]
 
         def y_sent(j, vmem):
-            wait(cp.at[j % SLOTS, pl.ds(0, (3 if vmem else 4) * ow)], y_s.at[j % SLOTS], "ysent")
+            wait(cp.at[0, pl.ds(0, (3 if vmem else 4) * ow)], y_s.at[j % SLOTS], "ysent")
 
         def sum_end(j):
-            on_y(j - SLOTS, lambda ref, row, vmem: pl.when(j < nb)(lambda: y_sent(j - SLOTS, vmem)))
+            @pl.when((j >= 2) & (j < split + 2))
+            def _():
+                y_sent(j - 2, False)
+
+            @pl.when((j >= split + SLOTS) & (j < nb))
+            def _():
+                y_sent(j - SLOTS, True)
 
             def body(ref, row, vmem):
                 q4 = j % SLOTS
-                wait(cp.at[q4, pl.ds(0, 4 * hw)], part_s.at[q4], "s1s")
+                wait(cp.at[0, pl.ds(0, 4 * hw)], part_s.at[q4], "s1s")
                 for e in SIDES:
                     wait(rs_near.at[q4, e], near_r.at[q4, e], "s2")
                     wait(rs_sum.at[q4, e], sum_r.at[q4, e], "s2")
                 own = yrow(ref, row, c)
-                src = own if vmem else ych.at[q4]
+                src = own if vmem else ych.at[j % 2]
                 for e in SIDES:
                     rows = pl.ds(e * hw, hw)
-                    tot = cpart(q4, c, e)[...].astype(F32) + rs_near[q4, 1 - e].astype(F32) + rs_sum[q4, e].astype(F32)
-                    dst = yhalf(ref, row, c, e) if vmem else ych.at[q4, rows]
+                    tot = cpart(j, c, e)[...].astype(F32) + rs_near[q4, 1 - e].astype(F32) + rs_sum[q4, e].astype(F32)
+                    dst = yhalf(ref, row, c, e) if vmem else src.at[rows]
                     dst[...] = (hst[q4, rows, :].astype(F32) + tot).astype(BF)
                 for e in SIDES:
                     send(src, own, y_s.at[q4], y_r.at[e, q4], dest[e])
@@ -551,17 +564,18 @@
 
         for j in range(nb + 6 - LATE, nb):
             wait(cp.at[0], y_rs.at[j % LATE])
-        for j in range(nb - SLOTS, nb):
-            y_sent(j, j >= split)
-            wait(sums.at[j % SLOTS], sum_s.at[j % SLOTS])
+        for j in range(max(nb - SLOTS, split), nb):
+            y_sent(j, True)
         for e in SIDES:
-            wait(_first(y_ref, nb * hw), y_rel.at[e])
+            wait(sums.at[e], sum_s.at[e])
+        for e in SIDES:
+            wait(_first(y_vm, nb * hw), y_rel.at[e])
             wait(o_buf, o_s.at[e])
             wait(oall_ref.at[pl.ds(0, t // 2), pl.ds(0, qw)], o_rel.at[e])
             wait(_first(wo_v, wr), wo_fs.at[e])
             for k in SIDES:
                 wait(_first(wo_v, wr), wo_s.at[e, k])
-        wait(_first(y_ref, nb * ow * 3), y_fwd)
+        wait(_first(y_vm, nb * ow * 3), y_fwd)
         wait(o_buf, o_sx.at[0])
         wait(oall_ref.at[:, pl.ds(0, 3 * qw)], o_fwd)
         wait(_first(wo_v, qw), wo_d.at[0])
@@ -570,8 +584,8 @@
         wo_end(wo_ps)
 
     pl.run_scoped(
-        rest, loc((b, tp * qw), BF), loc((b, dh), BF), loc((b, f), BF), loc((b, d), BF), loc((SLOTS, hb, d), BF),
-        loc((SLOTS, 2, hw, d), BF), *[loc((SLOTS, ow, d), BF)] * 2)
+        rest, loc((b, tp * qw), BF), loc((b, dh), BF), loc((b, f), BF), loc((b, d), BF), loc((CHIP, hb, d), BF),
+        loc((2, 2, hw, d), BF), loc((2, ow, d), BF), loc((SLOTS, ow, d), BF))
 
 
 def _held(rows, d):
@@ -594,21 +608,21 @@
     ow = hb // nc
     hw = ow // 2
     dh = d // 2
-    assert nc == SLOTS and t % b == 0 and wk.shape[1] == tp * HEAD
+    assert nc == SLOTS and f <= 4 * b and t % b == 0 and wk.shape[1] == tp * HEAD
     l1 = max(nb // 4, 1)
     l2 = min(nb * 3 // 4, nb - 2)
     hbm = pl.BlockSpec(memory_space=pl.ANY)
     bufs = [
-        (tp * qw, dh), (d, f), (d, f), (f, d), None, (b, d), (t, qw),
+        (tp * qw, dh), (d, f), (d, f), (f // 2, d), None, (b, d), (t, qw),
         (2, b, d), (2, hb, d), *[(SLOTS, 2, hw, d)] * 3,
     ]
     scratch = [pltpu.VMEM(a.shape, a.dtype) for a in (pos, inv, g1, g2)]
-    scratch += [pltpu.VMEM((2, 1, d), F32) if shape is None else pltpu.VMEM(shape, BF) for shape in bufs]
+    scratch += [pltpu.VMEM((2, d), F32) if shape is None else pltpu.VMEM(shape, BF) for shape in bufs]
     two, four, ring, per = (2,), (SLOTS, 2), (2, nb), (nb,)
-    sems = [(4,), (3,), (3,), two, two,
+    sems = [(4,), (3,), (4,), (), two,
             (3,), (2, 2), (2, 2), two, two, (2, 2), (2, 2),
             two, two, ring, ring, per, two, (),
-            two, two, two, (), two, (SLOTS,), four, four, (SLOTS,), four,
+            two, two, two, (), two, (SLOTS,), four, four, two, four,
             (SLOTS,), (2, SLOTS), (2, SLOTS), (LATE,), two, ()]
     scratch += [pltpu.SemaphoreType.DMA(shape) for shape in sems]
     flops = 2 * t * (d * (qw + 2 * HEAD) + qw * t + tp * qw * dh + 3 * d * f)

time: 349 us -> 346 us (level)
  no operation moved by 1% of the time
where the time goes in v5:
time: 346 us
  Pallas kernels  345 us (100%)
    pallas_call x1, Pallas kernels, _layer(): pl.pallas_call(functools.partial(_kernel, tp, dp, zn, split, l1, l2, nb /...  333 us
    pallas_call x1, Pallas kernels, _copy(): pl.pallas_call(_copy_kernel, name='copy_out', out_shape=tuple((jax.ShapeD...  12.1 us

profile of v5, /device:TPU:81, one launch (start us, length us, event | category | flops | bytes accessed | tf_op | source)
XLA Modules:
  0.0 345.9 jit_solution(13418818274323248743)
XLA Ops:
  0.6 333.2 %layer.1 = (bf16[1280,3072]{1,0:T(8,128)(2,1)}, bf16[2816,3072]{1,0:T(8,128)(2,1)S(1)}, bf16[4096,128]{1,0:T(8,128)(2,1)}, bf16[4096,128]{1,0:T(8,128)(2,1)}, bf16[4096,3072]{1,0:T(8,128)(2,1)}) custom-call(bf16[4096,3072]{1,0:T(8,128)(2,1)} %x_ref.1, s32[32,128]{1,0:T(8,128)} %bitcast.5, f32[1,128]{1,0:T(1,128)} %constant.2.clone.inv_ref, ...), custom_call_target="tpu_custom_call" | custom-call | flops 144955146240 | bytes 100663296 | tf_op jit(solution)/shard_map/layer/pallas_call | solution.py:632
  333.8 12.1 %copy_out.1 = (bf16[4096,3072]{1,0:T(8,128)(2,1)}, bf16[4096,128]{1,0:T(8,128)(2,1)}, bf16[4096,128]{1,0:T(8,128)(2,1)}) custom-call(bf16[1280,3072]{1,0:T(8,128)(2,1)} %get-tuple-element.10.src, bf16[2816,3072]{1,0:T(8,128)(2,1)S(1)} %get-tuple-element.11.held, bf16[4096,128]{1,0:T(8,128)(2,1)} %get-tuple-element.12.k_src, ...), custom_call_target="tpu_custom_call" | custom-call | bytes 50331648 | tf_op jit(solution)/shard_map/copy_out/pallas_call | solution.py:679

commit v6 on v5

--- a/solution.py
+++ b/solution.py
@@ -19,11 +19,12 @@
 SLOTS = 4
 LATE = 8
 CHIP = 3
+O_SLOTS = 6
 SIDES = (0, 1)
 BF = jnp.bfloat16
 F32 = jnp.float32
 VMEM_BYTES = 67040000
-Y_VMEM = 11
+Y_VMEM = 15
 TWO_OVER_PI = 0.6366197723675814
 PI_2 = (1.5703125, 4.837512969970703125e-4, 7.54978995489188216e-8)
 SIN = (-1.9515295891e-4, 8.3321608736e-3, -1.6666654611e-1)
@@ -61,7 +62,7 @@
             hbuf, rsib, rs_far, rs_near, rs_sum,
             ld_s, ld_w, ld_mlp, ld_x, kv_s,
             wo_d, wo_s, wo_r, wo_fs, wo_fr, wo_ps, wo_pr,
-            o_s, o_sx, o_r, o_f, o_rs, o_rel, o_fwd,
+            o_s, o_loc, o_r, o_f, o_rs, o_rel, o_fwd,
             ld_o, h_s, h_r, r_s, r_r, part_s, far_r, near_r, sum_s, sum_r,
             y_s, y_r, y_f, y_rs, y_rel, y_fwd):
     t, d = x_ref.shape
@@ -78,7 +79,11 @@
     hw = ow // 2
     kvt = 2 * b
 
-    wd_late = y_vm.at[pl.ds((nb - split) * b - fh, fh)]
+    last_y = (nb - split) * b
+    wd_late = y_vm.at[pl.ds(last_y - fh, fh)]
+    x_buf = o_blk = y_vm.at[pl.ds(last_y - 4 * b, b)]
+    xh = y_vm.at[pl.ds(last_y - 3 * b, b), pl.ds(0, dh)]
+    wqkv = wg_v.at[:, pl.ds(0, qw + 2 * HEAD)]
 
     r = lax.axis_index("tp")
     c = r // 2
@@ -227,7 +232,7 @@
     for e, ref in enumerate((g1_v, g2_v)):
         g_scr[e:e + 1, :] = ref[...].astype(F32).reshape(1, d)
 
-    def attention(wqkv, x_buf, q_scr, k_scr, v_scr, m_scr, l_scr, acc_scr):
+    def attention(q_scr, k_scr, v_scr, m_scr, l_scr, acc_scr):
         rk = _al(r * HEAD, HEAD)
         wq_dst = wqkv.at[:, pl.ds(0, qw)]
         kv_dst = [wqkv.at[:, pl.ds(qw + e * HEAD, HEAD)] for e in SIDES]
@@ -236,12 +241,15 @@
         for e, ref in enumerate((wk_ref, wv_ref)):
             put(ref.at[:, pl.ds(rk, HEAD)], kv_dst[e], ld_w.at[e])
         caches = ((k_scr, k_ref), (v_scr, v_ref))
-        mlp = ((wg_ref, wg_v), (wu_ref, wu_v), (_first(wd_ref, fh), wd_v), (wd_ref.at[pl.ds(fh, fh)], wd_late))
+        mlp = ((wu_ref, wu_v), (_first(wd_ref, fh), wd_v), (wd_ref.at[pl.ds(fh, fh)], wd_late))
         scale = HEAD ** -0.5 * LOG2E
         lane = lax.broadcasted_iota(jnp.int32, (b, HEAD), 1)
 
         def heads(ref, h):
             return ref.at[pl.ds(h * b, b)]
+
+        def o_sent(slot):
+            wait(oall_ref.at[pl.ds(0, 3 * b), pl.ds(0, qw)], o_s.at[slot], "osent")
 
         def tile(first, n, masked=False):
             keys = pl.ds(_al(first, n), n)
@@ -290,8 +298,8 @@
                 pcol.append(jnp.transpose(jnp.broadcast_to(prow, (LANES, LANES))))
             co, si = _sincos(jnp.concatenate(pcol, axis=0) * inv_v[...])
             si = jnp.where(lane < HEAD // 2, -si, si)
-            qk32 = jnp.dot(a_buf[...], wqkv[:, :qw + HEAD], preferred_element_type=F32)
-            v32 = jnp.dot(a_buf[...], wqkv[:, qw + HEAD:], preferred_element_type=F32)
+            qk32 = jnp.dot(a_buf[...], wg_v[:, :qw + HEAD], preferred_element_type=F32)
+            v32 = jnp.dot(a_buf[...], wg_v[:, qw + HEAD:qw + 2 * HEAD], preferred_element_type=F32)
             rows = pl.ds(_al(i * b, b), b)
             for h in range(hl + 1):
                 head = qk32[:, h * HEAD:(h + 1) * HEAD]
@@ -329,36 +337,45 @@
                 tile((i - 1) * b, b)
 
             tile(i * b, b, masked=True)
+            slot = i % O_SLOTS
+
+            @pl.when(i >= O_SLOTS)
+            def _():
+                o_sent(slot)
+
+            @pl.when(i > 0)
+            def _():
+                wait(o_buf.at[0], o_loc, "oloc")
+
             for h in range(hl):
-                o_buf[rows, h * HEAD:(h + 1) * HEAD] = (
+                o_buf[slot, :, h * HEAD:(h + 1) * HEAD] = (
                     heads(acc_scr, h)[...] / jnp.sum(heads(l_scr, h)[...], axis=1, keepdims=True)).astype(BF)
-            src = o_buf.at[rows]
+            src = o_buf.at[slot]
             dst = oreg(i, c)
             for e in SIDES:
-                send(src, dst, o_s.at[e], o_r.at[e, i], dest[e])
-            send(src, dst, o_sx.at[0], o_rs.at[i], sib)
-            put(src, dst, o_sx.at[1])
+                send(src, dst, o_s.at[slot], o_r.at[e, i], dest[e])
+            send(src, dst, o_s.at[slot], o_rs.at[i], sib)
+            put(src, dst, o_loc)
             for when, stage in ((w2, wo_stage2), (w3, wo_stage3), (w4, wo_stage4)):
                 pl.when(i == when)(stage)
             o_stage2(i - l1)
             o_stage3(i - l2)
 
         lax.fori_loop(0, nb, phase1, 0)
+        put(wg_ref, wg_v, ld_mlp.at[3])
         for e, (src, _) in enumerate(caches):
             wait(_first(src, b), kv_s.at[e])
 
     loc = pltpu.VMEM
     pl.run_scoped(
-        attention, loc((d, qw + 2 * HEAD), BF), loc((b, d), BF), loc((hl * b, HEAD), BF), loc((t, HEAD), BF),
+        attention, loc((hl * b, HEAD), BF), loc((t, HEAD), BF),
         loc((t, HEAD), BF), *[loc((hl * b, HEAD), F32)] * 3)
-    wait(o_buf, o_sx.at[1])
-    for e, dst in enumerate((wg_v, wu_v, wd_v, wd_late)):
-        wait(dst, ld_mlp.at[e])
+    wait(o_buf.at[0], o_loc)
     wait(shard(r + 1 - 2 * s), wo_d.at[1])
     wait(shard(r), wo_d.at[2])
     wo_end(wo_pr)
 
-    def rest(o_blk, xh, u_buf, r_buf, cp, sums, ych, hst):
+    def rest(u_buf, r_buf, cp, sums, ych, hst):
         def load_o(j):
             wait(oall_ref.at[orow(j), pl.ds(0, 4 * qw)], o_rs.at[j], "os")
             put(oall_ref.at[orow(j)], o_blk, ld_o.at[0])
@@ -422,6 +439,12 @@
                 two = j % 2
                 wait(hbuf.at[two, :, pl.ds(other, dh)], h_r.at[two], "h")
                 wait(hbuf.at[two, :, pl.ds(mine, dh)], h_s.at[two], "hs")
+
+                @pl.when(j == 0)
+                def _():
+                    for e, dst in enumerate((wu_v, wd_v, wd_late, wg_v)):
+                        wait(dst, ld_mlp.at[e], "mlp")
+
                 norm_rows(hbuf.at[two], 1)
                 hst[j % SLOTS] = hbuf[two, pl.ds(_al(s * hb + c * ow, SUB), ow), :]
 
@@ -570,13 +593,13 @@
             wait(sums.at[e], sum_s.at[e])
         for e in SIDES:
             wait(_first(y_vm, nb * hw), y_rel.at[e])
-            wait(o_buf, o_s.at[e])
             wait(oall_ref.at[pl.ds(0, t // 2), pl.ds(0, qw)], o_rel.at[e])
             wait(_first(wo_v, wr), wo_fs.at[e])
             for k in SIDES:
                 wait(_first(wo_v, wr), wo_s.at[e, k])
         wait(_first(y_vm, nb * ow * 3), y_fwd)
-        wait(o_buf, o_sx.at[0])
+        for e in range(O_SLOTS):
+            wait(oall_ref.at[pl.ds(0, 3 * b), pl.ds(0, qw)], o_s.at[e])
         wait(oall_ref.at[:, pl.ds(0, 3 * qw)], o_fwd)
         wait(_first(wo_v, qw), wo_d.at[0])
         for e in range(len(peers)):
@@ -584,7 +607,7 @@
         wo_end(wo_ps)
 
     pl.run_scoped(
-        rest, loc((b, tp * qw), BF), loc((b, dh), BF), loc((b, f), BF), loc((b, d), BF), loc((CHIP, hb, d), BF),
+        rest, loc((b, f), BF), loc((b, d), BF), loc((CHIP, hb, d), BF),
         loc((2, 2, hw, d), BF), loc((2, ow, d), BF), loc((SLOTS, ow, d), BF))
 
 
@@ -608,12 +631,12 @@
     ow = hb // nc
     hw = ow // 2
     dh = d // 2
-    assert nc == SLOTS and f <= 4 * b and t % b == 0 and wk.shape[1] == tp * HEAD
+    assert nc == SLOTS and f <= 4 * b and nb > SLOTS and tp * qw == d and t % b == 0 and wk.shape[1] == tp * HEAD
     l1 = max(nb // 4, 1)
     l2 = min(nb * 3 // 4, nb - 2)
     hbm = pl.BlockSpec(memory_space=pl.ANY)
     bufs = [
-        (tp * qw, dh), (d, f), (d, f), (f // 2, d), None, (b, d), (t, qw),
+        (tp * qw, dh), (d, f), (d, f), (f // 2, d), None, (b, d), (O_SLOTS, b, qw),
         (2, b, d), (2, hb, d), *[(SLOTS, 2, hw, d)] * 3,
     ]
     scratch = [pltpu.VMEM(a.shape, a.dtype) for a in (pos, inv, g1, g2)]
@@ -621,7 +644,7 @@
     two, four, ring, per = (2,), (SLOTS, 2), (2, nb), (nb,)
     sems = [(4,), (3,), (4,), (), two,
             (3,), (2, 2), (2, 2), two, two, (2, 2), (2, 2),
-            two, two, ring, ring, per, two, (),
+            (O_SLOTS,), (), ring, ring, per, two, (),
             two, two, two, (), two, (SLOTS,), four, four, two, four,
             (SLOTS,), (2, SLOTS), (2, SLOTS), (LATE,), two, ()]
     scratch += [pltpu.SemaphoreType.DMA(shape) for shape in sems]

time: 346 us -> 348 us (level)
    pallas_call x1, Pallas kernels: 333 us -> 337 us  [_layer(): pl.pallas_call(functools.partial(_kernel, tp, dp, zn, split, l1, l2, nb /...]
where the time goes in v6:
time: 348 us
  Pallas kernels  347 us (100%)
    pallas_call x1, Pallas kernels, _layer(): pl.pallas_call(functools.partial(_kernel, tp, dp, zn, split, l1, l2, nb /...  337 us
    pallas_call x1, Pallas kernels, _copy(): pl.pallas_call(_copy_kernel, name='copy_out', out_shape=tuple((jax.ShapeD...  9.86 us

profile of v6, /device:TPU:81, one launch (start us, length us, event | category | flops | bytes accessed | tf_op | source)
XLA Modules:
  0.0 347.9 jit_solution(6575438307178262403)
XLA Ops:
  0.6 337.4 %layer.1 = (bf16[256,3072]{1,0:T(8,128)(2,1)}, bf16[3840,3072]{1,0:T(8,128)(2,1)S(1)}, bf16[4096,128]{1,0:T(8,128)(2,1)}, bf16[4096,128]{1,0:T(8,128)(2,1)}, bf16[4096,3072]{1,0:T(8,128)(2,1)}) custom-call(bf16[4096,3072]{1,0:T(8,128)(2,1)} %x_ref.1, s32[32,128]{1,0:T(8,128)} %bitcast.5, f32[1,128]{1,0:T(1,128)} %constant.2.clone.inv_ref, ...), custom_call_target="tpu_custom_call" | custom-call | flops 144955146240 | bytes 100663296 | tf_op jit(solution)/shard_map/layer/pallas_call | solution.py:655
  338.0 9.9 %copy_out.1 = (bf16[4096,3072]{1,0:T(8,128)(2,1)}, bf16[4096,128]{1,0:T(8,128)(2,1)}, bf16[4096,128]{1,0:T(8,128)(2,1)}) custom-call(bf16[256,3072]{1,0:T(8,128)(2,1)} %get-tuple-element.10.src, bf16[3840,3072]{1,0:T(8,128)(2,1)S(1)} %get-tuple-element.11.held, bf16[4096,128]{1,0:T(8,128)(2,1)} %get-tuple-element.12.k_src, ...), custom_call_target="tpu_custom_call" | custom-call | bytes 50331648 | tf_op jit(solution)/shard_map/copy_out/pallas_call | solution.py:702

commit v7 on v6

--- a/solution.py
+++ b/solution.py
@@ -125,8 +125,42 @@
         pl.semaphore_signal(barrier, inc=1, device_id=dev, device_id_type=MESH)
 
     small = ((pos_ref, pos_v), (inv_ref, inv_v), (g1_ref, g1_v), (g2_ref, g2_v))
+    rk = _al(r * HEAD, HEAD)
+    wq_dst = wqkv.at[:, pl.ds(0, qw)]
+    kv_dst = [wqkv.at[:, pl.ds(qw + e * HEAD, HEAD)] for e in SIDES]
+    put(_first(x_ref, b), x_buf, ld_x)
     for e, (src, dst) in enumerate(small):
         put(src, dst, ld_s.at[e])
+    put(wq_ref, wq_dst, ld_w.at[2])
+    for e, ref in enumerate((wk_ref, wv_ref)):
+        put(ref.at[:, pl.ds(rk, HEAD)], kv_dst[e], ld_w.at[e])
+
+    def norm_rows(src, which):
+        def step(e, carry):
+            for q in range(NR // SUB):
+                rows = pl.ds(_al(e * NR + q * SUB, SUB), SUB)
+                v32 = src[rows, :].astype(F32)
+                inv = lax.rsqrt(jnp.mean(v32 * v32, axis=1, keepdims=True) + EPS)
+                a_buf[rows, :] = (v32 * inv * g_scr[which:which + 1, :]).astype(BF)
+            return carry
+
+        with jax.named_scope("norm"):
+            lax.fori_loop(0, b // NR, step, 0)
+
+    for e, (src, dst) in enumerate(small):
+        wait(dst, ld_s.at[e], "small")
+    for e, ref in enumerate((g1_v, g2_v)):
+        g_scr[e:e + 1, :] = ref[...].astype(F32).reshape(1, d)
+
+    def x_norm(i):
+        wait(x_buf, ld_x, "x")
+        norm_rows(x_buf, 0)
+
+        @pl.when(i + 1 < nb)
+        def _():
+            put(x_ref.at[pl.ds(_al((i + 1) * b, b), b)], x_buf, ld_x)
+
+    x_norm(0)
     with jax.named_scope("barrier"):
         pl.semaphore_wait(barrier, len(others))
 
@@ -215,31 +249,7 @@
         for e in range(n):
             body(e)
 
-    def norm_rows(src, which):
-        def step(e, carry):
-            for q in range(NR // SUB):
-                rows = pl.ds(_al(e * NR + q * SUB, SUB), SUB)
-                v32 = src[rows, :].astype(F32)
-                inv = lax.rsqrt(jnp.mean(v32 * v32, axis=1, keepdims=True) + EPS)
-                a_buf[rows, :] = (v32 * inv * g_scr[which:which + 1, :]).astype(BF)
-            return carry
-
-        with jax.named_scope("norm"):
-            lax.fori_loop(0, b // NR, step, 0)
-
-    for e, (src, dst) in enumerate(small):
-        wait(dst, ld_s.at[e], "small")
-    for e, ref in enumerate((g1_v, g2_v)):
-        g_scr[e:e + 1, :] = ref[...].astype(F32).reshape(1, d)
-
     def attention(q_scr, k_scr, v_scr, m_scr, l_scr, acc_scr):
-        rk = _al(r * HEAD, HEAD)
-        wq_dst = wqkv.at[:, pl.ds(0, qw)]
-        kv_dst = [wqkv.at[:, pl.ds(qw + e * HEAD, HEAD)] for e in SIDES]
-        put(_first(x_ref, b), x_buf, ld_x)
-        put(wq_ref, wq_dst, ld_w.at[2])
-        for e, ref in enumerate((wk_ref, wv_ref)):
-            put(ref.at[:, pl.ds(rk, HEAD)], kv_dst[e], ld_w.at[e])
         caches = ((k_scr, k_ref), (v_scr, v_ref))
         mlp = ((wu_ref, wu_v), (_first(wd_ref, fh), wd_v), (wd_ref.at[pl.ds(fh, fh)], wd_late))
         scale = HEAD ** -0.5 * LOG2E
@@ -274,12 +284,15 @@
             return carry
 
         def phase1_slot(i):
-            wait(x_buf, ld_x, "x")
-            norm_rows(x_buf, 0)
-
-            @pl.when(i + 1 < nb)
-            def _():
-                put(x_ref.at[pl.ds(_al((i + 1) * b, b), b)], x_buf, ld_x)
+            slot = i % O_SLOTS
+
+            @pl.when(i >= O_SLOTS)
+            def _():
+                o_sent(slot)
+
+            @pl.when(i > 0)
+            def _():
+                wait(o_buf.at[0], o_loc, "oloc")
 
             @pl.when(i == 0)
             def _():
@@ -337,16 +350,6 @@
                 tile((i - 1) * b, b)
 
             tile(i * b, b, masked=True)
-            slot = i % O_SLOTS
-
-            @pl.when(i >= O_SLOTS)
-            def _():
-                o_sent(slot)
-
-            @pl.when(i > 0)
-            def _():
-                wait(o_buf.at[0], o_loc, "oloc")
-
             for h in range(hl):
                 o_buf[slot, :, h * HEAD:(h + 1) * HEAD] = (
                     heads(acc_scr, h)[...] / jnp.sum(heads(l_scr, h)[...], axis=1, keepdims=True)).astype(BF)
@@ -361,8 +364,11 @@
             o_stage2(i - l1)
             o_stage3(i - l2)
 
+            @pl.when(i + 1 < nb)
+            def _():
+                x_norm(i + 1)
+
         lax.fori_loop(0, nb, phase1, 0)
-        put(wg_ref, wg_v, ld_mlp.at[3])
         for e, (src, _) in enumerate(caches):
             wait(_first(src, b), kv_s.at[e])
 
@@ -565,6 +571,7 @@
             when_block(j, lambda: wait(cp.at[0], y_rs.at[j % LATE], "ys"))
 
         load_o(0)
+        put(wg_ref, wg_v, ld_mlp.at[3])
 
         def phase2(i, carry):
             with jax.named_scope("slot2"):

time: 348 us -> 345 us (level)
    pallas_call x1, Pallas kernels: 337 us -> 334 us  [_layer(): pl.pallas_call(functools.partial(_kernel, tp, dp, zn, split, l1, l2, nb /...]
where the time goes in v7:
time: 345 us; the launch traced here: 344 us
  Pallas kernels  344 us (100%)
    pallas_call x1, Pallas kernels, _layer(): pl.pallas_call(functools.partial(_kernel, tp, dp, zn, split, l1, l2, nb /...  334 us
    pallas_call x1, Pallas kernels, _copy(): pl.pallas_call(_copy_kernel, name='copy_out', out_shape=tuple((jax.ShapeD...  9.86 us

profile of v7, /device:TPU:81, one launch (start us, length us, event | category | flops | bytes accessed | tf_op | source)
XLA Modules:
  0.0 344.4 jit_solution(11648846791814823965)
XLA Ops:
  0.6 333.9 %layer.1 = (bf16[256,3072]{1,0:T(8,128)(2,1)}, bf16[3840,3072]{1,0:T(8,128)(2,1)S(1)}, bf16[4096,128]{1,0:T(8,128)(2,1)}, bf16[4096,128]{1,0:T(8,128)(2,1)}, bf16[4096,3072]{1,0:T(8,128)(2,1)}) custom-call(bf16[4096,3072]{1,0:T(8,128)(2,1)} %x_ref.1, s32[32,128]{1,0:T(8,128)} %bitcast.5, f32[1,128]{1,0:T(1,128)} %constant.2.clone.inv_ref, ...), custom_call_target="tpu_custom_call" | custom-call | flops 144955146240 | bytes 100663296 | tf_op jit(solution)/shard_map/layer/pallas_call | solution.py:662
  334.5 9.9 %copy_out.1 = (bf16[4096,3072]{1,0:T(8,128)(2,1)}, bf16[4096,128]{1,0:T(8,128)(2,1)}, bf16[4096,128]{1,0:T(8,128)(2,1)}) custom-call(bf16[256,3072]{1,0:T(8,128)(2,1)} %get-tuple-element.10.src, bf16[3840,3072]{1,0:T(8,128)(2,1)S(1)} %get-tuple-element.11.held, bf16[4096,128]{1,0:T(8,128)(2,1)} %get-tuple-element.12.k_src, ...), custom_call_target="tpu_custom_call" | custom-call | bytes 50331648 | tf_op jit(solution)/shard_map/copy_out/pallas_call | solution.py:709

commit v8 on v7

--- a/solution.py
+++ b/solution.py
@@ -249,6 +249,11 @@
         for e in range(n):
             body(e)
 
+    def load_o(j):
+        wait(oall_ref.at[orow(j), pl.ds(0, 4 * qw)], o_rs.at[j], "os")
+        put(oall_ref.at[orow(j)], o_blk, ld_o.at[0])
+        put(x_ref.at[orow(j), pl.ds(mine, dh)], xh, ld_o.at[1])
+
     def attention(q_scr, k_scr, v_scr, m_scr, l_scr, acc_scr):
         caches = ((k_scr, k_ref), (v_scr, v_ref))
         mlp = ((wu_ref, wu_v), (_first(wd_ref, fh), wd_v), (wd_ref.at[pl.ds(fh, fh)], wd_late))
@@ -293,6 +298,10 @@
             @pl.when(i > 0)
             def _():
                 wait(o_buf.at[0], o_loc, "oloc")
+
+            @pl.when(i == nb - 1)
+            def _():
+                load_o(0)
 
             @pl.when(i == 0)
             def _():
@@ -382,11 +391,6 @@
     wo_end(wo_pr)
 
     def rest(u_buf, r_buf, cp, sums, ych, hst):
-        def load_o(j):
-            wait(oall_ref.at[orow(j), pl.ds(0, 4 * qw)], o_rs.at[j], "os")
-            put(oall_ref.at[orow(j)], o_blk, ld_o.at[0])
-            put(x_ref.at[orow(j), pl.ds(mine, dh)], xh, ld_o.at[1])
-
         nt_h = min(512, dh)
         nt_f = min(512, f)
         nt_d = min(512, d)
@@ -570,7 +574,6 @@
         def y_seen(j):
             when_block(j, lambda: wait(cp.at[0], y_rs.at[j % LATE], "ys"))
 
-        load_o(0)
         put(wg_ref, wg_v, ld_mlp.at[3])
 
         def phase2(i, carry):

time: 345 us -> 345 us (level)
  no operation moved by 1% of the time
where the time goes in v8:
time: 345 us; the launch traced here: 344 us
  Pallas kernels  344 us (100%)
    pallas_call x1, Pallas kernels, _layer(): pl.pallas_call(functools.partial(_kernel, tp, dp, zn, split, l1, l2, nb /...  334 us
    pallas_call x1, Pallas kernels, _copy(): pl.pallas_call(_copy_kernel, name='copy_out', out_shape=tuple((jax.ShapeD...  9.86 us

profile of v8, /device:TPU:81, one launch (start us, length us, event | category | flops | bytes accessed | tf_op | source)
XLA Modules:
  0.0 344.4 jit_solution(14065747103945766011)
XLA Ops:
  0.6 333.9 %layer.1 = (bf16[256,3072]{1,0:T(8,128)(2,1)}, bf16[3840,3072]{1,0:T(8,128)(2,1)S(1)}, bf16[4096,128]{1,0:T(8,128)(2,1)}, bf16[4096,128]{1,0:T(8,128)(2,1)}, bf16[4096,3072]{1,0:T(8,128)(2,1)}) custom-call(bf16[4096,3072]{1,0:T(8,128)(2,1)} %x_ref.1, s32[32,128]{1,0:T(8,128)} %bitcast.5, f32[1,128]{1,0:T(1,128)} %constant.2.clone.inv_ref, ...), custom_call_target="tpu_custom_call" | custom-call | flops 144955146240 | bytes 100663296 | tf_op jit(solution)/shard_map/layer/pallas_call | solution.py:665
  334.5 9.9 %copy_out.1 = (bf16[4096,3072]{1,0:T(8,128)(2,1)}, bf16[4096,128]{1,0:T(8,128)(2,1)}, bf16[4096,128]{1,0:T(8,128)(2,1)}) custom-call(bf16[256,3072]{1,0:T(8,128)(2,1)} %get-tuple-element.10.src, bf16[3840,3072]{1,0:T(8,128)(2,1)S(1)} %get-tuple-element.11.held, bf16[4096,128]{1,0:T(8,128)(2,1)} %get-tuple-element.12.k_src, ...), custom_call_target="tpu_custom_call" | custom-call | bytes 50331648 | tf_op jit(solution)/shard_map/copy_out/pallas_call | solution.py:712

commit v9 on v8

--- a/solution.py
+++ b/solution.py
@@ -160,7 +160,6 @@
         def _():
             put(x_ref.at[pl.ds(_al((i + 1) * b, b), b)], x_buf, ld_x)
 
-    x_norm(0)
     with jax.named_scope("barrier"):
         pl.semaphore_wait(barrier, len(others))
 
@@ -182,6 +181,7 @@
             send(wo_ref.at[rows, pl.ds(cols, dh)], piece(c, s), wo_s.at[e, k], wo_r.at[e, s], dev)
     send(wo_ref.at[:, pl.ds(other, dh)], shard(r), wo_d.at[0], wo_d.at[1], sib)
     put(wo_ref.at[:, pl.ds(mine, dh)], shard(r), wo_d.at[2])
+    x_norm(0)
 
     def wo_swap(chip):
         for e, dev in enumerate(peers):

time: 345 us -> 344 us (level)
  no operation moved by 1% of the time
where the time goes in v9:
time: 344 us
  Pallas kernels  343 us (100%)
    pallas_call x1, Pallas kernels, _layer(): pl.pallas_call(functools.partial(_kernel, tp, dp, zn, split, l1, l2, nb /...  333 us
    pallas_call x1, Pallas kernels, _copy(): pl.pallas_call(_copy_kernel, name='copy_out', out_shape=tuple((jax.ShapeD...  9.86 us

profile of v9, /device:TPU:81, one launch (start us, length us, event | category | flops | bytes accessed | tf_op | source)
XLA Modules:
  0.0 343.7 jit_solution(12982598697972358466)
XLA Ops:
  0.6 333.2 %layer.1 = (bf16[256,3072]{1,0:T(8,128)(2,1)}, bf16[3840,3072]{1,0:T(8,128)(2,1)S(1)}, bf16[4096,128]{1,0:T(8,128)(2,1)}, bf16[4096,128]{1,0:T(8,128)(2,1)}, bf16[4096,3072]{1,0:T(8,128)(2,1)}) custom-call(bf16[4096,3072]{1,0:T(8,128)(2,1)} %x_ref.1, s32[32,128]{1,0:T(8,128)} %bitcast.5, f32[1,128]{1,0:T(1,128)} %constant.2.clone.inv_ref, ...), custom_call_target="tpu_custom_call" | custom-call | flops 144955146240 | bytes 100663296 | tf_op jit(solution)/shard_map/layer/pallas_call | solution.py:665
  333.9 9.9 %copy_out.1 = (bf16[4096,3072]{1,0:T(8,128)(2,1)}, bf16[4096,128]{1,0:T(8,128)(2,1)}, bf16[4096,128]{1,0:T(8,128)(2,1)}) custom-call(bf16[256,3072]{1,0:T(8,128)(2,1)} %get-tuple-element.10.src, bf16[3840,3072]{1,0:T(8,128)(2,1)S(1)} %get-tuple-element.11.held, bf16[4096,128]{1,0:T(8,128)(2,1)} %get-tuple-element.12.k_src, ...), custom_call_target="tpu_custom_call" | custom-call | bytes 50331648 | tf_op jit(solution)/shard_map/copy_out/pallas_call | solution.py:712
